TPU v7x, 32 devices: a whole 2x2x4 slice. The times are simulated.
32 devices in a mesh: seq: 8 (over z, x), batch: 4 (over y, core).
Axes of the slice: x: 2, y: 2, z: 4, core: 2. Of those that a mesh axis runs over, the one named last changes fastest.
Arguments:
- inputs: bfloat16 [4, 2048, 6144], P('batch', 'seq'), may hold values from -6 to 6
- out_grad: bfloat16 [4, 2048, 6144], P('batch', 'seq'), may hold values from -6 to 6
- step_size: float32 [4, 96, 2048], P('batch', None, 'seq'), may hold values from 0.5 to 2
- log_decay: float32 [4, 96, 2048], P('batch', None, 'seq'), may hold values from -1 to 0
- b_matrix: bfloat16 [4, 16, 2048], P('batch', None, 'seq'), may hold values from -1.5 to 1.5
- c_matrix: bfloat16 [4, 16, 2048], P('batch', None, 'seq'), may hold values from -0.125 to 0.125
- skip_gain: float32 [96], replicated, may hold values from 0.5 to 1.5
- lengths: int32 [4], P('batch'), may hold values from 256 to 2048
Outputs:
- grad_x: bfloat16 [4, 2048, 6144], P('batch', 'seq')
- grad_b: float32 [4, 16, 2048], P('batch', None, 'seq')
- grad_c: float32 [4, 16, 2048], P('batch', None, 'seq')
All inputs are finite; a program needn't handle non-finite values.
Results may differ from a plain program's by a relative error of at most 0.0047.
Values may be sent and summed in bfloat16 or wider, within the bound.
No kernel may reach another device: no remote copies, remote signals or barrier semaphores. Data moves between devices by JAX's collectives and lax.ppermute only.
A program may use at most 128 MiB of HBM per device.

v0:
```python
import math

import jax
import jax.numpy as jnp
from jax import lax
from jax.sharding import PartitionSpec as P

SPAN = 256


HIGHEST = lax.Precision.HIGHEST


def carried_in(value, axis, join, neutral, backward):
    count, mine = (lax.axis_size(axis), lax.axis_index(axis))
    pieces = jax.tree.map(lambda part: lax.all_gather(part, axis), value)
    if backward:
        pieces = jax.tree.map(lambda part: part[::-1], pieces)
        mine = count - 1 - mine
    so_far = jax.tree.map(
        lambda part, zero: jnp.full_like(part, 0) + jnp.asarray(zero, part.dtype), value, neutral
    )

    def step(position, so_far):
        longer = join(so_far, jax.tree.map(lambda part: part[position], pieces))
        return jax.tree.map(lambda new, old: jnp.where(position < mine, new, old), longer, so_far)

    return lax.fori_loop(0, count - 1, step, so_far)


def pair_combine(preceding, later):
    return (preceding[0] * later[0], later[0][:, None, None] * preceding[1] + later[1])


def block_summary(inputs, masked, step_size, cumulative, b_matrix, c_matrix):
    row_count, columns = inputs.shape
    head_count = step_size.shape[0]
    x_heads = inputs.reshape(row_count, head_count, columns // head_count)
    dy_heads = masked.reshape(row_count, head_count, columns // head_count)
    to_end = jnp.exp(cumulative[:, -1:] - cumulative)
    into_state = (b_matrix.astype(jnp.float32)[None] * (to_end * step_size)[:, None, :]).astype(
        jnp.bfloat16
    )
    into_grad = (c_matrix.astype(jnp.float32)[None] * jnp.exp(cumulative)[:, None, :]).astype(
        jnp.bfloat16
    )
    state_part = jnp.einsum("hnu,uhp->hnp", into_state, x_heads, preferred_element_type=jnp.float32)
    grad_part = jnp.einsum("hnu,uhp->hnp", into_grad, dy_heads, preferred_element_type=jnp.float32)
    return (jnp.exp(cumulative[:, -1]), state_part, grad_part)


def block_grads(
    inputs,
    masked,
    step_size,
    cumulative,
    b_matrix,
    c_matrix,
    incoming_state,
    grad_in,
    skip_gain,
    scale_b,
    scale_c,
):
    row_count, columns = inputs.shape
    head_count = step_size.shape[0]
    head_dim = columns // head_count
    state_size = b_matrix.shape[0]
    group_size = math.gcd(head_count, 32)
    rounds = head_count // group_size
    to_end = jnp.exp(cumulative[:, -1:] - cumulative)
    from_start = jnp.exp(cumulative)
    causal = lax.broadcasted_iota(jnp.int32, (row_count, row_count), 0) >= lax.broadcasted_iota(
        jnp.int32, (row_count, row_count), 1
    )
    c_dot_b = jnp.dot(c_matrix.T, b_matrix, preferred_element_type=jnp.float32)
    grad16 = grad_in.astype(jnp.bfloat16)
    state16 = incoming_state.astype(jnp.bfloat16)

    def one_group(group_index, running):
        grad_x, mixing, cross_b, across_c_terms = running
        offset = group_index * group_size
        x_heads = lax.dynamic_slice_in_dim(
            inputs, offset * head_dim, group_size * head_dim, 1
        ).reshape(row_count, group_size, head_dim)
        dy_heads = lax.dynamic_slice_in_dim(
            masked, offset * head_dim, group_size * head_dim, 1
        ).reshape(row_count, group_size, head_dim)
        cums_group = lax.dynamic_slice_in_dim(cumulative, offset, group_size, 0)
        dt_group = lax.dynamic_slice_in_dim(step_size, offset, group_size, 0)
        end_group = lax.dynamic_slice_in_dim(to_end, offset, group_size, 0)
        start_group = lax.dynamic_slice_in_dim(from_start, offset, group_size, 0)
        gradient_group = lax.dynamic_slice_in_dim(grad16, offset, group_size, 0)
        state_group = lax.dynamic_slice_in_dim(state16, offset, group_size, 0)
        skip_group = lax.dynamic_slice_in_dim(skip_gain, offset, group_size, 0)
        differences = cums_group[:, :, None] - cums_group[:, None, :]
        forward_decay = jnp.exp(jnp.where(causal[None], differences, -jnp.inf))
        kernel = (forward_decay * c_dot_b[None]).astype(jnp.bfloat16)
        within = jnp.einsum("hut,uhp->thp", kernel, dy_heads, preferred_element_type=jnp.float32)
        across = (
            jnp.einsum("nt,hnp->thp", b_matrix, gradient_group, preferred_element_type=jnp.float32)
            * end_group.T[:, :, None]
        )
        pieces = dt_group.T[:, :, None] * (within + across) + skip_group[
            None, :, None
        ] * dy_heads.astype(jnp.float32)
        grad_x = lax.dynamic_update_slice_in_dim(
            grad_x,
            pieces.astype(jnp.bfloat16).reshape(row_count, group_size * head_dim),
            offset * head_dim,
            1,
        )
        scores = jnp.einsum("thp,uhp->htu", x_heads, dy_heads, preferred_element_type=jnp.float32)
        mixing = mixing + jnp.sum(
            dt_group[:, :, None] * jnp.swapaxes(forward_decay, 1, 2) * scores, axis=0
        )
        b_terms = jnp.einsum(
            "thp,hnp->htn", x_heads, gradient_group, preferred_element_type=jnp.float32
        )
        cross_b = cross_b + jnp.einsum(
            "htn,ht->nt", b_terms, dt_group * end_group, precision=HIGHEST
        )
        c_terms = jnp.einsum(
            "thp,hnp->htn", dy_heads, state_group, preferred_element_type=jnp.float32
        )
        across_c_terms = across_c_terms + jnp.einsum(
            "htn,ht->nt", c_terms, start_group, precision=HIGHEST
        )
        return (grad_x, mixing, cross_b, across_c_terms)

    initial = (
        jnp.zeros((row_count, columns), jnp.bfloat16),
        jnp.zeros((row_count, row_count), jnp.float32),
        jnp.zeros((state_size, row_count), jnp.float32),
        jnp.zeros((state_size, row_count), jnp.float32),
    )
    grad_x, mixing, cross_b, across_c_terms = lax.fori_loop(0, rounds, one_group, initial)
    grad_b = (
        jnp.dot(c_matrix.astype(jnp.float32), mixing.T, precision=HIGHEST) + cross_b
    ) * scale_b
    grad_c = (
        jnp.dot(b_matrix.astype(jnp.float32), mixing, precision=HIGHEST) + across_c_terms
    ) * scale_c
    return (grad_x, grad_b, grad_c)


def slab_grads(
    input_lines,
    dy_rows,
    dt_rows,
    cum_rows,
    b_rows,
    c_rows,
    state_blocks,
    grad_blocks,
    skip_part,
    scale_b,
    scale_c,
):
    tokens, columns = input_lines.shape
    head_count = dt_rows.shape[0]
    state_size = b_rows.shape[0]
    blocks = tokens // SPAN
    x_blocks = input_lines.reshape(blocks, SPAN, columns)
    dy_blocks = dy_rows.reshape(blocks, SPAN, columns)
    dt_blocks = dt_rows.reshape(head_count, blocks, SPAN).transpose(1, 0, 2)
    cum_blocks = cum_rows.reshape(head_count, blocks, SPAN).transpose(1, 0, 2)
    b_blocks = b_rows.reshape(state_size, blocks, SPAN).transpose(1, 0, 2)
    c_blocks = c_rows.reshape(state_size, blocks, SPAN).transpose(1, 0, 2)
    grad_x, grad_b, grad_c = lax.map(
        lambda element: block_grads(*element, skip_part, scale_b, scale_c),
        (x_blocks, dy_blocks, dt_blocks, cum_blocks, b_blocks, c_blocks, state_blocks, grad_blocks),
    )
    grad_x = grad_x.reshape(tokens, columns)
    grad_b = grad_b.transpose(1, 0, 2).reshape(state_size, tokens)
    grad_c = grad_c.transpose(1, 0, 2).reshape(state_size, tokens)
    return (grad_x, grad_b, grad_c)


def local(inputs, out_grad, step_size, log_decay, b_matrix, c_matrix, skip_gain, lengths):
    tokens = inputs.shape[1]
    columns = inputs.shape[2]
    head_count = step_size.shape[1]
    head_dim = columns // head_count
    state_size = b_matrix.shape[1]
    shard_count = lax.axis_size("seq")
    blocks = tokens // SPAN
    first_row = lax.axis_index("seq") * tokens
    interior = first_row + lax.iota(jnp.int32, tokens) < lengths[0]
    masked = jnp.where(interior[:, None], out_grad[0], jnp.zeros((), jnp.bfloat16))
    x_blocks = inputs[0].reshape(blocks, SPAN, columns)
    dy_blocks = masked.reshape(blocks, SPAN, columns)
    dt_blocks = step_size[0].reshape(head_count, blocks, SPAN).transpose(1, 0, 2)
    cum_rows = jnp.cumsum(log_decay[0].reshape(head_count, blocks, SPAN), axis=2).reshape(
        head_count, tokens
    )
    cumulative = cum_rows.reshape(head_count, blocks, SPAN).transpose(1, 0, 2)
    b_blocks = b_matrix[0].reshape(state_size, blocks, SPAN).transpose(1, 0, 2)
    c_blocks = c_matrix[0].reshape(state_size, blocks, SPAN).transpose(1, 0, 2)
    decays, state_parts, grad_parts = lax.map(
        lambda element: block_summary(*element),
        (x_blocks, dy_blocks, dt_blocks, cumulative, b_blocks, c_blocks),
    )

    def fold_blocks(running, element):
        totals, portion_sum = running
        factor, portion = element
        return ((totals * factor, factor[:, None, None] * portion_sum + portion), None)

    identity = (
        jnp.ones((head_count,), jnp.float32),
        jnp.zeros((head_count, state_size, head_dim), jnp.float32),
    )
    (whole_decay, state_total), _ = lax.scan(fold_blocks, identity, (decays, state_parts))
    (_, grad_total), _ = lax.scan(fold_blocks, identity, (decays, grad_parts), reverse=True)
    _, incoming_state = carried_in((whole_decay, state_total), "seq", pair_combine, identity, False)
    _, grad_in = carried_in((whole_decay, grad_total), "seq", pair_combine, identity, True)

    def pass_on(running, element):
        factor, portion = element
        return (factor[:, None, None] * running + portion, running)

    _, state_blocks = lax.scan(pass_on, incoming_state, (decays, state_parts))
    _, grad_blocks = lax.scan(pass_on, grad_in, (decays, grad_parts), reverse=True)
    scale_b = 1.0 / math.sqrt(columns)
    scale_c = math.sqrt(state_size / (columns * shard_count * tokens))
    grad_x, grad_b, grad_c = slab_grads(
        inputs[0],
        masked,
        step_size[0],
        cum_rows,
        b_matrix[0],
        c_matrix[0],
        state_blocks,
        grad_blocks,
        skip_gain,
        scale_b,
        scale_c,
    )
    return (grad_x[None], grad_b[None], grad_c[None])


def solution(mesh):
    placed = (
        P("batch", "seq", None),
        P("batch", "seq", None),
        P("batch", None, "seq"),
        P("batch", None, "seq"),
        P("batch", None, "seq"),
        P("batch", None, "seq"),
        P(),
        P("batch"),
    )
    return jax.shard_map(
        local,
        mesh=mesh,
        in_specs=placed,
        out_specs=(P("batch", "seq", None), P("batch", None, "seq"), P("batch", None, "seq")),
        check_vma=False,
    )
```

profile of v0, /device:TPU:0, one launch (start us, length us, event | category | flops | bytes accessed | tf_op | source)
XLA Modules:
  0.0 312.8 jit_solution(6232807471840022084)
XLA Ops:
  7.2 0.9 reshape.159
  10.1 1.0 slice_reduce_fusion.1
  11.1 1.7 bitcast_multiply_fusion.1
  12.8 4.7 %copy.34 = bf16[1,256,6144]{1,2,0:T(8,128)(2,1)} copy(bf16[1,256,6144]{2,1,0:T(8,128)(2,1)} %param.14) | data formatting | bytes 6291456 | tf_op args[0]
  17.5 3.7 %convolution_add_fusion = f32[96,16,64]{2,1,0:T(8,128)} fusion(bf16[256,96,64]{0,2,1:T(8,128)(2,1)} %bitcast.14, f32[96,256]{1,0:T(8,128)S(1)} %get-tuple-element.927, f32[16,256]{1,0:T(8,128)S(1)} %bitcast_convert_fusion.1, f32[96]{0:T(128)S(1)} %exponential_multiply_fusion), kind=kOutput, calls=%fused_computation.55 | convolution fusion | flops 51216384 | bytes 3654016 | tf_op jit(solution)/shard_map/while/body/eval_jaxpr/hnu,uhp->hnp/dot_general | solution.py:47
  21.9 3.2 %copy.29 = bf16[1,256,6144]{1,2,0:T(8,128)(2,1)S(1)} copy(bf16[1,256,6144]{2,1,0:T(8,128)(2,1)} %param.15) | data formatting | bytes 6291456 | tf_op args[1]
  25.2 2.9 fusion.32
  29.6 24.1 %all-reduce = f32[768]{0:T(1024)S(1)} all-reduce(f32[768]{0:T(1024)S(1)} %dynamic-update-slice), channel_id=2, replica_groups=mesh['seq'=8,'batch'=4] {'seq'}, use_global_device_ids=true, to_apply=%add | all-reduce | flops 768 | bytes 6144
  53.7 0.9 fusion.46
  54.6 3.8 %bitcast_select_fusion = bf16[256,6144]{0,1:T(8,128)(2,1)} fusion(bf16[1,256,6144]{1,2,0:T(8,128)(2,1)} %copy-done.1, pred[256]{0:T(512)(128)(4,1)S(1)} %add_compare_fusion), kind=kLoop, calls=%fused_computation.48 | loop fusion | flops 1572864 | bytes 6291712 | tf_op jit(solution)/shard_map/jit(_where)/select_n | solution.py:190
  58.4 64.7 %all-gather.8.cloned.1.call-done = f32[768,16,64]{2,1,0:T(8,128)} async-done(((f32[96,16,64]{2,1,0:T(8,128)}), f32[768,16,64]{2,1,0:T(8,128)}) %all-gather.8.cloned.1.call-update) | async-done | bytes 3145744 | tf_op jit(solution)/shard_map/all_gather | solution.py:16
  123.1 10.3 %while.40 = (s32[]{:T(128)}, f32[96,16,64]{2,1,0:T(8,128)S(1)}, s32[]{:T(128)}, f32[8,96]{1,0:T(8,128)S(1)}, f32[8,96,16,64]{3,2,1,0:T(8,128)}, /*index=5*/s32[]{:T(128)}, s32[]{:T(128)}) while((s32[]{:T(128)}, f32[96,16,64]{2,1,0:T(8,128)S(1)}, s32[]{:T(128)}, f32[8,96]{1,0:T(8,128)S(1)}, f32[8,96,16,64]{3,2,1,0:T(8,128)}, ...), condition=%wide.region_5.6_spmd.clone, body=%wide.region_4.5_spmd.clone.sunk | while | flops 393220 | bytes 1180905 | solution.py:28
  123.1 1.4 fusion.77
  124.6 1.4 fusion.77
  126.0 1.4 fusion.77
  127.5 1.4 fusion.77
  129.0 1.4 fusion.77
  130.4 1.5 fusion.77
  132.0 1.4 fusion.77
  133.4 0.8 convert_element_type.59
  134.2 88.0 %all-gather.6.cloned.1.call-done = f32[768,16,64]{2,1,0:T(8,128)} async-done(((f32[96,16,64]{2,1,0:T(8,128)}), f32[768,16,64]{2,1,0:T(8,128)}) %all-gather.6.cloned.1.call-update) | async-done | bytes 3145744 | tf_op jit(solution)/shard_map/all_gather | solution.py:16
  222.2 5.8 %rev.7 = f32[8,96,16,64]{3,2,1,0:T(8,128)} reverse(f32[8,96,16,64]{3,2,1,0:T(8,128)} %bitcast.172), dimensions={0} | reverse | bytes 6291456 | tf_op jit(solution)/shard_map/rev | solution.py:18
  228.0 10.2 %while.39 = (s32[]{:T(128)}, f32[96,16,64]{2,1,0:T(8,128)S(1)}, s32[]{:T(128)}, f32[8,96]{1,0:T(8,128)S(1)}, f32[8,96,16,64]{3,2,1,0:T(8,128)}, /*index=5*/s32[]{:T(128)}, s32[]{:T(128)}) while((s32[]{:T(128)}, f32[96,16,64]{2,1,0:T(8,128)S(1)}, s32[]{:T(128)}, f32[8,96]{1,0:T(8,128)S(1)}, f32[8,96,16,64]{3,2,1,0:T(8,128)}, ...), condition=%wide.region_3.4_spmd.clone, body=%wide.region_2.3_spmd.clone.sunk | while | flops 393220 | bytes 1180905 | solution.py:28
  228.1 1.4 fusion.76
  229.5 1.4 fusion.76
  231.0 1.4 fusion.76
  232.4 1.4 fusion.76
  233.9 1.4 fusion.76
  235.4 1.4 fusion.76
  236.8 1.4 fusion.76
  238.3 0.8 convert_element_type.57
  239.1 2.0 broadcast.85.clone
  241.1 61.8 %while.41 = (s32[]{:T(128)}, bf16[256,6144]{1,0:T(8,128)(2,1)}, f32[256,256]{1,0:T(8,128)S(1)}, f32[16,256]{1,0:T(8,128)S(1)}, f32[16,256]{1,0:T(8,128)}, /*inde...) while((s32[]{:T(128)}, bf16[256,6144]{1,0:T(8,128)(2,1)}, ...), condition=%wide.region_8.9_spmd.clone.clone, body=%wide.region_6.8_spmd.clone.clone.sunk | while | flops 610484224 | bytes 30188352 | solution.py:137
  241.1 0.8 multiply_bitcast_fusion.2
  241.9 2.7 fusion.87
  244.6 0.8 constant_dynamic-slice_fusion.8
  245.4 1.8 constant_dynamic-slice_fusion.7
  248.0 4.3 %fusion.88 = bf16[256,32,64]{0,2,1:T(8,128)(2,1)} fusion(f32[32,64,256]{2,1,0:T(8,128)S(1)} %copy-done, bf16[256,32,64]{0,2,1:T(8,128)(2,1)S(1)} %bitcast.165, f32[256,256]{1,0:T(8,128)} %get-tuple-element.1200, f32[32,256]{1,0:T(8,128)S(1)} %constant_dynamic-slice_fusion.8, pred[256,256]{1,0:T(8,128)(4,1)S(1)} %iota_compare_fusion.2, ...), kind=kOutput, calls=%fused_computation.19.clone.1 | convolution fusion | flops 280494080 | bytes 4620416 | tf_op jit(solution)/shard_map/while/body/eval_jaxpr/while/body/eval_jaxpr/hut,uhp->thp/dot_general | solution.py:99
  252.3 1.5 copy.61
  253.8 1.0 constant_dynamic-update-slice_fusion.2
  255.1 3.5 %multiply_reduce_fusion.2 = f32[256,256]{1,0:T(8,128)S(1)} fusion(f32[32,256]{1,0:T(8,128)S(1)} %get-tuple-element.1102, f32[32,256]{1,0:T(8,128)S(1)} %constant_dynamic-slice_fusion.8, pred[256,256]{1,0:T(8,128)(4,1)S(1)} %copy.62, bf16[256,32,64]{0,2,1:T(8,128)(2,1)S(1)} %bitcast.168, bf16[256,32,64]{0,2,1:T(8,128)(2,1)S(1)} %bitcast.166), kind=kOutput, calls=%fused_computation.7.clone.1 | convolution fusion | flops 278855680 | bytes 2490368 | tf_op jit(solution)/shard_map/while/body/eval_jaxpr/while/body/eval_jaxpr/thp,uhp->htu/dot_general | solution.py:113
  258.7 1.2 fusion.90
  259.9 1.2 fusion.91
  261.7 0.8 multiply_bitcast_fusion.2
  262.5 2.7 fusion.87
  265.2 0.8 constant_dynamic-slice_fusion.8
  266.0 1.8 constant_dynamic-slice_fusion.7
  268.6 4.3 %fusion.88 = bf16[256,32,64]{0,2,1:T(8,128)(2,1)} fusion(f32[32,64,256]{2,1,0:T(8,128)S(1)} %copy-done, bf16[256,32,64]{0,2,1:T(8,128)(2,1)S(1)} %bitcast.165, f32[256,256]{1,0:T(8,128)} %get-tuple-element.1200, f32[32,256]{1,0:T(8,128)S(1)} %constant_dynamic-slice_fusion.8, pred[256,256]{1,0:T(8,128)(4,1)S(1)} %iota_compare_fusion.2, ...), kind=kOutput, calls=%fused_computation.19.clone.1 | convolution fusion | flops 280494080 | bytes 4620416 | tf_op jit(solution)/shard_map/while/body/eval_jaxpr/while/body/eval_jaxpr/hut,uhp->thp/dot_general | solution.py:99
  272.9 1.5 copy.61
  274.4 1.0 constant_dynamic-update-slice_fusion.2
  275.7 3.5 %multiply_reduce_fusion.2 = f32[256,256]{1,0:T(8,128)S(1)} fusion(f32[32,256]{1,0:T(8,128)S(1)} %get-tuple-element.1102, f32[32,256]{1,0:T(8,128)S(1)} %constant_dynamic-slice_fusion.8, pred[256,256]{1,0:T(8,128)(4,1)S(1)} %copy.62, bf16[256,32,64]{0,2,1:T(8,128)(2,1)S(1)} %bitcast.168, bf16[256,32,64]{0,2,1:T(8,128)(2,1)S(1)} %bitcast.166), kind=kOutput, calls=%fused_computation.7.clone.1 | convolution fusion | flops 278855680 | bytes 2490368 | tf_op jit(solution)/shard_map/while/body/eval_jaxpr/while/body/eval_jaxpr/thp,uhp->htu/dot_general | solution.py:113
  279.3 1.2 fusion.90
  280.5 1.2 fusion.91
  282.3 0.8 multiply_bitcast_fusion.2
  283.1 2.7 fusion.87
  286.6 1.8 constant_dynamic-slice_fusion.7
  289.2 4.3 %fusion.88 = bf16[256,32,64]{0,2,1:T(8,128)(2,1)} fusion(f32[32,64,256]{2,1,0:T(8,128)S(1)} %copy-done, bf16[256,32,64]{0,2,1:T(8,128)(2,1)S(1)} %bitcast.165, f32[256,256]{1,0:T(8,128)} %get-tuple-element.1200, f32[32,256]{1,0:T(8,128)S(1)} %constant_dynamic-slice_fusion.8, pred[256,256]{1,0:T(8,128)(4,1)S(1)} %iota_compare_fusion.2, ...), kind=kOutput, calls=%fused_computation.19.clone.1 | convolution fusion | flops 280494080 | bytes 4620416 | tf_op jit(solution)/shard_map/while/body/eval_jaxpr/while/body/eval_jaxpr/hut,uhp->thp/dot_general | solution.py:99
  293.5 1.5 copy.61
  295.0 1.0 constant_dynamic-update-slice_fusion.2
  296.3 3.5 %multiply_reduce_fusion.2 = f32[256,256]{1,0:T(8,128)S(1)} fusion(f32[32,256]{1,0:T(8,128)S(1)} %get-tuple-element.1102, f32[32,256]{1,0:T(8,128)S(1)} %constant_dynamic-slice_fusion.8, pred[256,256]{1,0:T(8,128)(4,1)S(1)} %copy.62, bf16[256,32,64]{0,2,1:T(8,128)(2,1)S(1)} %bitcast.168, bf16[256,32,64]{0,2,1:T(8,128)(2,1)S(1)} %bitcast.166), kind=kOutput, calls=%fused_computation.7.clone.1 | convolution fusion | flops 278855680 | bytes 2490368 | tf_op jit(solution)/shard_map/while/body/eval_jaxpr/while/body/eval_jaxpr/thp,uhp->htu/dot_general | solution.py:113
  299.9 1.2 fusion.90
  301.1 1.2 fusion.91
  302.9 1.5 fusion.37
  304.4 1.6 fusion.40
  (95 shorter events, 8.8 us)
Async XLA Ops:
  7.2 116.0 %all-gather.8.cloned.1.call-start = ((), (), s32[]{:S(2)}) async-start(), calls=%async_computation.1 | async-start | bytes 7077888 | tf_op jit(solution)/shard_map/all_gather | solution.py:16
  12.8 4.7 %copy-start.4 = (bf16[1,16,256]{2,1,0:T(8,128)(2,1)S(1)}, bf16[1,16,256]{2,1,0:T(8,128)(2,1)}, u32[]{:S(2)}) copy-start(bf16[1,16,256]{2,1,0:T(8,128)(2,1)} %param.18) | copy-start | bytes 24580
  21.2 201.0 %all-gather.6.cloned.1.call-start = ((), (), s32[]{:S(2)}) async-start(), calls=%async_computation | async-start | bytes 7077888 | tf_op jit(solution)/shard_map/all_gather | solution.py:16
  21.9 3.2 %copy-start.6 = (bf16[1,16,256]{2,1,0:T(8,128)(2,1)S(1)}, bf16[1,16,256]{2,1,0:T(8,128)(2,1)}, u32[]{:S(2)}) copy-start(bf16[1,16,256]{2,1,0:T(8,128)(2,1)} %param.19) | copy-start | bytes 24580
  25.1 3.0 copy-start.1
  25.1 3.0 copy-start.7
  245.4 2.6 copy-start
  258.6 2.5 copy-start.2
  258.6 3.1 copy-start.5
  261.1 0.6 copy-start.3
  266.0 2.6 copy-start
  279.2 2.5 copy-start.2
  279.2 3.1 copy-start.5
  281.7 0.6 copy-start.3
  286.6 2.6 copy-start
  299.8 2.5 copy-start.2
  299.8 3.1 copy-start.5
  302.3 0.6 copy-start.3
Sparse Core Ops, SparseCore 0:
  21.3 101.7 all-gather.7
  125.3 96.8 all-gather.5
where the time goes:
time: 315 us; the launch traced here: 313 us
  waiting for transfers between devices  153 us (49%)
  matrix products  49.4 us (16%)
  local copies, waits for them, and re-layouts  39.1 us (12%)
  other arithmetic  31.2 us (10%)
  blocking collectives  24.1 us (8%)
  between operations  15.5 us (5%)
    all_gather x2, waiting for transfers between devices, carried_in(): pieces = jax.tree.map(lambda part: lax.all_gather(part, axis), value)  153 us
    unnamed x1, blocking collectives  24.1 us
    select_n x14, other arithmetic, step(): jnp.where(position < mine, new, old)  20 us
    dot_general x3, matrix products, one_group(): jnp.einsum('hut,uhp->thp', kernel, dy_heads, preferred_element_type=jnp.f...  13 us
    dot_general x3, matrix products, one_group(): jnp.einsum('thp,uhp->htu', x_heads, dy_heads, preferred_element_type=jnp....  10.5 us
    unnamed x13, local copies, waits for them, and re-layouts  8.72 us
    dot_general x3, matrix products, one_group(): jnp.einsum('nt,hnp->thp', b_matrix, gradient_group, preferred_element_typ...  8.23 us
    dynamic_update_slice x6, local copies, waits for them, and re-layouts, one_group(): lax.dynamic_update_slice_in_dim(grad_x, pieces.astype(jnp.bfloat16).resha...  7.58 us
  transfers between devices with their start and end apart: 2, of which 2 were waited for; matrix products, arithmetic and copies ran while one was open for 7% of the time, Pallas kernels for 0%

commit v1 on v0

v1 whole, which is shorter than its diff:
```python
import functools
import math

import jax
import jax.numpy as jnp
from jax import lax
from jax.experimental import pallas as pl
from jax.experimental.pallas import tpu as pltpu
from jax.sharding import PartitionSpec as P

SPAN = 256
LANES = 128
LOG2E = math.log2(math.e)
F32 = jnp.float32
BF16 = jnp.bfloat16
VM = pltpu.VMEM
ANY = pl.ANY


def place():
    idx = lax.axis_index("seq")
    count = lax.axis_size("seq")
    return idx, lax.rem(idx, 2), idx < count // 2


def valid_rows(len_ref, tokens):
    return len_ref[0] - lax.axis_index("seq") * tokens


def lane_low(shape, head_dim):
    return lax.broadcasted_iota(jnp.int32, shape, 1) < head_dim


def running_sum(values):
    rows, span = values.shape
    high = values.astype(BF16)
    rest = values - high.astype(F32)
    middle = rest.astype(BF16)
    low = (rest - middle.astype(F32)).astype(BF16)
    upper = lax.broadcasted_iota(jnp.int32, (span, span), 0) <= lax.broadcasted_iota(
        jnp.int32, (span, span), 1
    )
    pieces = jnp.concatenate([high, middle, low], axis=0)
    sums = jnp.dot(pieces, upper.astype(BF16), preferred_element_type=F32)
    return sums[:rows] + sums[rows : 2 * rows] + sums[2 * rows :]


def weights(ld, dt, valid):
    cum = running_sum(ld)
    end = cum[:, -1:]
    inside = lax.broadcasted_iota(jnp.int32, cum.shape, 1) < valid
    into_state = dt * jnp.exp(end - cum)
    into_grad = jnp.where(inside, jnp.exp(cum), 0.0)
    return end, into_state, into_grad


def summary_kernel(tasks, head_dim, len_ref, ld_ref, dt_ref, b_ref, c_ref, x_ref, dy_ref, *refs):
    outs = refs[: len(tasks)]
    decay_ref, buf_ref, w_ref, spread_ref, sems = refs[len(tasks) :]
    idx, mine, lower = place()
    heads, span = ld_ref.shape
    half_heads = heads // 2
    width = half_heads * head_dim
    chunks = sems.shape[1]
    chunk = width // chunks
    kinds = [lower if first else jnp.logical_not(lower) for first, own in tasks]
    halves = [mine if own else 1 - mine for first, own in tasks]

    def copy(t, i, src):
        start = pl.multiple_of(halves[t] * width + i * chunk, LANES)
        return pltpu.make_async_copy(
            src.at[:, pl.ds(start, chunk)],
            buf_ref.at[t, :, pl.ds(i * chunk, chunk)],
            sems.at[t, i],
        )

    for t in range(len(tasks)):
        for i in range(chunks):

            @pl.when(kinds[t])
            def _():
                copy(t, i, x_ref).start()

            @pl.when(jnp.logical_not(kinds[t]))
            def _():
                copy(t, i, dy_ref).start()

    valid = valid_rows(len_ref, span)
    low = lane_low((STATE_ROWS(b_ref), LANES), head_dim)
    done = {}
    for own in sorted({own for first, own in tasks}):
        half = mine if own else 1 - mine
        rows = pl.ds(pl.multiple_of(half * half_heads, 8), half_heads)
        done[own] = weights(ld_ref[rows, :], dt_ref[rows, :], valid)
    decay_half = tasks[0][1]
    spread_ref[...] = jnp.broadcast_to(jnp.exp(done[decay_half][0]), (half_heads, LANES))
    pairs = half_heads // 2
    even = spread_ref[pl.ds(0, pairs, stride=2), :]
    odd = spread_ref[pl.ds(1, pairs, stride=2), :]
    spread = jnp.where(lane_low((pairs, LANES), head_dim), even, odd)
    if decay_half:
        decay_ref[...] = spread
    else:
        high = spread.astype(BF16).astype(F32)
        both = jnp.concatenate([high, spread - high], axis=0).astype(BF16)
        decay_ref[...] = both.reshape(decay_ref.shape)
    for t, (first, own) in enumerate(tasks):
        end, into_state, into_grad = done[own]
        w_ref[t] = jnp.where(kinds[t], into_state, into_grad)
        mat = jnp.where(kinds[t], b_ref[...].astype(F32), c_ref[...].astype(F32))
        states = mat.shape[0]
        per = 2 * LANES // head_dim
        for i in range(chunks):
            copy(t, i, x_ref).wait()
            for g in range(i * chunk // (2 * LANES), (i + 1) * chunk // (2 * LANES)):
                lhs = jnp.concatenate(
                    [
                        (mat * w_ref[t, pl.ds(per * g + j, 1), :]).astype(BF16)
                        for j in range(per)
                    ],
                    axis=0,
                )
                rhs = buf_ref[t, :, pl.ds(2 * LANES * g, 2 * LANES)]
                res = jnp.dot(lhs, rhs, preferred_element_type=F32)
                for q in range(2):
                    top = res[2 * q * states : (2 * q + 1) * states, q * LANES : (q + 1) * LANES]
                    bottom = res[
                        (2 * q + 1) * states : (2 * q + 2) * states, q * LANES : (q + 1) * LANES
                    ]
                    outs[t][2 * g + q] = jnp.where(low, top, bottom).astype(outs[t].dtype)


def STATE_ROWS(ref):
    return ref.shape[0]


def summary(tasks, types, length, ld, dt, b, c, x, dy):
    heads, span = ld.shape
    columns = x.shape[1]
    head_dim = columns // heads
    states = b.shape[0]
    tiles = columns // 2 // LANES
    pairs = heads // 4
    if tasks[0][1]:
        decay = jax.ShapeDtypeStruct((pairs, LANES), F32)
    else:
        decay = jax.ShapeDtypeStruct((2 * pairs // states, states, LANES), BF16)
    whole = lambda: pl.BlockSpec(memory_space=VM)
    count = len(tasks)
    return pl.pallas_call(
        functools.partial(summary_kernel, tasks, head_dim),
        out_shape=[jax.ShapeDtypeStruct((tiles, states, LANES), t) for t in types] + [decay],
        in_specs=[pl.BlockSpec(memory_space=pltpu.SMEM)]
        + [whole() for _ in range(4)]
        + [pl.BlockSpec(memory_space=ANY)] * 2,
        out_specs=[whole() for _ in range(count + 1)],
        scratch_shapes=[
            pltpu.VMEM((count, span, columns // 2), BF16),
            pltpu.VMEM((count, heads // 2, span), F32),
            pltpu.VMEM((heads // 2, LANES), F32),
            pltpu.SemaphoreType.DMA((count, 4)),
        ],
        compiler_params=pltpu.CompilerParams(vmem_limit_bytes=(4 + 4 * count) << 20),
        name="summary",
    )(length, ld, dt, b, c, x, dy)


def pair_flags(second):
    idx, mine, lower = place()
    ahead = jnp.where(lower, mine == 0, mine == 1)
    return jnp.logical_not(ahead) if second else ahead


def partner_rows(decay_ref):
    count = decay_ref.shape[0] * decay_ref.shape[1]
    both = decay_ref[...].reshape(count, LANES).astype(F32)
    return both[: count // 2] + both[count // 2 :]


def chain_kernel(second, carries, finish, msg, *refs):
    refs = list(refs)
    decay_ref, mine_ref, x_ref, y_ref = refs[:4]
    carry_refs = refs[4 : 4 + carries]
    rest = refs[4 + carries :]
    ahead = pair_flags(second)
    tiles = x_ref.shape[0]
    dp_ref = rest[-1]
    dp_ref[...] = partner_rows(decay_ref)
    for j in range(tiles):
        dp = dp_ref[pl.ds(j, 1), :]
        d = mine_ref[pl.ds(j, 1), :]
        x = x_ref[j]
        y = y_ref[j].astype(F32)
        carry = None
        for ref in carry_refs:
            carry = ref[j].astype(F32) if carry is None else carry + ref[j].astype(F32)
        at = 0
        if msg:
            total = jnp.where(ahead, dp, d) * jnp.where(ahead, x, y) + jnp.where(ahead, y, x)
            if carry is not None:
                total = total + d * dp * carry
            rest[at][j] = total.astype(BF16)
            at += 1
        if finish:
            if carry is None:
                carry = jnp.zeros_like(x)
            passed = jnp.where(ahead, d, dp) * carry + jnp.where(ahead, x, y)
            own = jnp.where(ahead, carry, passed)
            send = jnp.where(ahead, passed, carry)
            rest[at][j] = own.astype(BF16)
            rest[at + 1][j] = send.astype(BF16)


def chain(second, decay, mine, x, y, carries, msg, finish):
    shape = jax.ShapeDtypeStruct(x.shape, BF16)
    outs = int(msg) + 2 * int(finish)
    whole = lambda: pl.BlockSpec(memory_space=VM)
    return pl.pallas_call(
        functools.partial(chain_kernel, second, len(carries), finish, msg),
        out_shape=[shape] * outs,
        in_specs=[whole() for _ in range(4 + len(carries))],
        out_specs=[whole() for _ in range(outs)],
        scratch_shapes=[pltpu.VMEM(mine.shape, F32)],
        compiler_params=pltpu.CompilerParams(vmem_limit_bytes=4 << 20),
        name="chain",
    )(decay, mine, x, y, *carries)


def intra_kernel(head0, per_step, head_dim, first, len_ref, skip_ref, *refs):
    if first:
        ld_ref, dt_ref, b_ref, c_ref, x_ref, dy_ref = refs[:6]
        rest = refs[6:]
    else:
        ld_ref, dt_ref, b_ref, c_ref, x_ref, dy_ref, mix_in, part_in = refs[:8]
        rest = refs[8:]
    part_ref, mix_ref, cb_ref, row_ref, col_ref = rest
    span = x_ref.shape[0]
    half = span // 2
    valid = valid_rows(len_ref, span)
    step = pl.program_id(0)
    call_heads = row_ref.shape[0]

    @pl.when(step == 0)
    def _():
        if first:
            mix_ref[...] = jnp.zeros_like(mix_ref)
        else:
            mix_ref[...] = mix_in[...]
        t = lax.broadcasted_iota(jnp.int32, (span, span), 0)
        u = lax.broadcasted_iota(jnp.int32, (span, span), 1)
        dots = lax.dot_general(
            b_ref[...], c_ref[...], (((0,), (0,)), ((), ())), preferred_element_type=F32
        )
        cb_ref[...] = jnp.where(jnp.logical_and(u >= t, u < valid), dots, 0.0)
        cum = running_sum(ld_ref[pl.ds(head0, call_heads), :]) * LOG2E
        row_ref[...] = cum
        shifted = cum - jnp.log(dt_ref[pl.ds(head0, call_heads), :]) * LOG2E
        col_ref[...] = shifted.T

    lane = lax.broadcasted_iota(jnp.int32, (1, LANES), 1)
    keep0 = (lane < head_dim).astype(BF16)
    keep1 = (lane >= head_dim).astype(BF16)
    low = lane < head_dim
    inside = lax.broadcasted_iota(jnp.int32, (span, LANES), 0) < valid
    nt = (((1,), (1,)), ((), ()))

    def one_pair(p, cols):
        h = 2 * p
        xp = x_ref[:, pl.ds(p * LANES, LANES)]
        yp = dy_ref[:, pl.ds(p * LANES, LANES)]
        outs = []
        sums = None
        for j in range(2):
            scores = lax.dot_general(
                xp * (keep1 if j else keep0), yp, nt, preferred_element_type=F32
            )
            row = row_ref[pl.ds(step * per_step + h + j, 1), :]
            col = cols[:, h + j : h + j + 1]
            f00 = jnp.exp2(jnp.minimum(row[:, :half] - col[:half], 100.0))
            f01 = jnp.exp2(row[:, half:] - col[:half])
            f11 = jnp.exp2(jnp.minimum(row[:, half:] - col[half:], 100.0))
            k00 = (f00 * cb_ref[:half, :half]).astype(BF16)
            k01 = (f01 * cb_ref[:half, half:]).astype(BF16)
            k11 = (f11 * cb_ref[half:, half:]).astype(BF16)
            top = jnp.dot(
                jnp.concatenate([k00, k01], axis=1), yp, preferred_element_type=F32
            )
            bottom = jnp.dot(k11, yp[half:], preferred_element_type=F32)
            outs.append(jnp.concatenate([top, bottom], axis=0))
            terms = [
                f00 * scores[:half, :half],
                f01 * scores[:half, half:],
                f11 * scores[half:, half:],
            ]
            sums = terms if sums is None else [a + b for a, b in zip(sums, terms)]
        mix_ref[:half, :half] += sums[0]
        mix_ref[:half, half:] += sums[1]
        mix_ref[half:, half:] += sums[2]
        at = head0 + step * per_step + h
        skip = jnp.where(low, skip_ref[at], skip_ref[at + 1])
        direct = jnp.where(inside, skip * yp.astype(F32), 0.0)
        part_ref[:, pl.ds(p * LANES, LANES)] = (
            jnp.where(low, outs[0], outs[1]) + direct
        ).astype(part_ref.dtype)

    if call_heads == per_step:
        cols = col_ref[...]
    else:
        cols = jnp.where(step == 0, col_ref[:, :per_step], col_ref[:, per_step:])
    for p in range(per_step // 2):
        one_pair(p, cols)


def intra(head0, call_heads, per_step, length, skip, ld, dt, b, c, x, dy, mix, part):
    heads, span = ld.shape
    columns = x.shape[1]
    head_dim = columns // heads
    first = mix is None
    width = per_step * head_dim
    base = head0 // per_step
    whole = lambda: pl.BlockSpec(memory_space=VM)
    slab = lambda: pl.BlockSpec((span, width), lambda i: (0, base + i))
    smem = lambda: pl.BlockSpec(memory_space=pltpu.SMEM)
    in_specs = [smem(), smem()] + [whole() for _ in range(4)] + [slab(), slab()]
    args = [length, skip, ld, dt, b, c, x, dy]
    aliases = {}
    if not first:
        in_specs += [whole(), pl.BlockSpec(memory_space=ANY)]
        args += [mix, part]
        aliases = {9: 0}
    return pl.pallas_call(
        functools.partial(intra_kernel, head0, per_step, head_dim, first),
        grid=(call_heads // per_step,),
        out_shape=[
            jax.ShapeDtypeStruct((span, columns), BF16),
            jax.ShapeDtypeStruct((span, span), F32),
        ],
        in_specs=in_specs,
        out_specs=[slab(), pl.BlockSpec((span, span), lambda i: (0, 0))],
        scratch_shapes=[
            pltpu.VMEM((span, span), F32),
            pltpu.VMEM((call_heads, span), F32),
            pltpu.VMEM((span, call_heads), F32),
        ],
        input_output_aliases=aliases,
        compiler_params=pltpu.CompilerParams(vmem_limit_bytes=24 << 20),
        cost_estimate=pl.CostEstimate(
            flops=call_heads * 2 * 2 * span * span * 256,
            transcendentals=call_heads * span * span,
            bytes_accessed=call_heads * head_dim * span * 2 * 3,
        ),
        name="intra",
    )(*args)


def inter_kernel(
    own, last, head_dim, scale_b, scale_c, len_ref, ld_ref, dt_ref, b_ref, c_ref,
    x_ref, dy_ref, one_ref, two_ref, gb_in, gc_in, part_ref, out_ref, gb_ref, gc_ref, ws_ref, wg_ref
):
    idx, mine, lower = place()
    half = mine if own else 1 - mine
    span, width = x_ref.shape
    heads = ld_ref.shape[0]
    half_heads = heads // 2
    states = b_ref.shape[0]
    valid = valid_rows(len_ref, span)
    step = pl.program_id(0)
    nt = (((1,), (1,)), ((), ()))

    @pl.when(step == 0)
    def _():
        rows = pl.ds(pl.multiple_of(half * half_heads, 8), half_heads)
        end, into_state, into_grad = weights(ld_ref[rows, :], dt_ref[rows, :], valid)
        ws_ref[...] = into_state
        wg_ref[...] = into_grad
        if last:
            gb_ref[...] = gb_in[...]
            gc_ref[...] = gc_in[...]
        else:
            t = lax.broadcasted_iota(jnp.int32, (span, span), 0)
            u = lax.broadcasted_iota(jnp.int32, (span, span), 1)
            mix = jnp.where(jnp.logical_and(u >= t, u < valid), gb_in[...], 0.0)
            high = mix.astype(BF16)
            rest = (mix - high.astype(F32)).astype(BF16)
            c = c_ref[...]
            b = b_ref[...]
            gb_ref[...] = lax.dot_general(
                c, high, nt, preferred_element_type=F32
            ) + lax.dot_general(c, rest, nt, preferred_element_type=F32)
            gc_ref[...] = jnp.dot(b, high, preferred_element_type=F32) + jnp.dot(
                b, rest, preferred_element_type=F32
            )

    per = 2 * LANES // head_dim
    slab = 2 * LANES
    rowhead = lax.broadcasted_iota(jnp.int32, (per * states, slab), 0) // states
    lanehead = lax.broadcasted_iota(jnp.int32, (per * states, slab), 1) // head_dim
    diag = (rowhead == lanehead).astype(F32).astype(BF16)
    b = b_ref[...].astype(F32)
    groups = width // slab
    gb = None
    gc = None
    for g in range(groups):
        tile = step * (2 * groups) + 2 * g
        a0, a1 = one_ref[tile], one_ref[tile + 1]
        z0, z1 = two_ref[tile], two_ref[tile + 1]
        one = jnp.concatenate([a0, a1], axis=1)
        two = jnp.concatenate([z0, z1], axis=1)
        grad = jnp.where(lower, two, one)
        state = jnp.where(lower, one, two)
        grad_diag = jnp.concatenate([grad] * per, axis=0) * diag
        state_diag = jnp.concatenate([state] * per, axis=0) * diag
        h = step * (groups * per) + g * per
        rows_s = [ws_ref[pl.ds(h + j, 1), :] for j in range(per)]
        rows_g = [wg_ref[pl.ds(h + j, 1), :] for j in range(per)]
        left = jnp.concatenate([(b * r).astype(BF16) for r in rows_s], axis=0)
        cols = pl.ds(g * slab, slab)
        across = lax.dot_general(
            left, grad_diag, (((0,), (0,)), ((), ())), preferred_element_type=F32
        )
        out_ref[:, cols] = (part_ref[:, cols].astype(F32) + across).astype(out_ref.dtype)
        rb = lax.dot_general(grad_diag, x_ref[:, cols], nt, preferred_element_type=F32)
        rc = lax.dot_general(state_diag, dy_ref[:, cols], nt, preferred_element_type=F32)
        for j in range(per):
            tb = rows_s[j] * rb[j * states : (j + 1) * states]
            tc = rows_g[j] * rc[j * states : (j + 1) * states]
            gb = tb if gb is None else gb + tb
            gc = tc if gc is None else gc + tc
    gb_ref[...] += gb
    gc_ref[...] += gc
    if last:

        @pl.when(step == pl.num_programs(0) - 1)
        def _():
            gb_ref[...] = gb_ref[...] * scale_b
            gc_ref[...] = gc_ref[...] * scale_c


def inter(own, last, scale_b, scale_c, length, ld, dt, b, c, x, dy, one, two, gb, gc, part):
    heads, span = ld.shape
    columns = x.shape[1]
    head_dim = columns // heads
    states = b.shape[0]
    steps = 3
    width = columns // 2 // steps
    whole = lambda: pl.BlockSpec(memory_space=VM)

    def at(i):
        mine = lax.rem(lax.axis_index("seq"), 2)
        return (0, (mine if own else 1 - mine) * steps + i)

    slab = lambda: pl.BlockSpec((span, width), at)
    small = jax.ShapeDtypeStruct((states, span), F32)
    return pl.pallas_call(
        functools.partial(inter_kernel, own, last, head_dim, scale_b, scale_c),
        grid=(steps,),
        out_shape=[jax.ShapeDtypeStruct((span, columns), BF16), small, small],
        in_specs=[pl.BlockSpec(memory_space=pltpu.SMEM)]
        + [whole() for _ in range(4)]
        + [slab(), slab()]
        + [whole() for _ in range(4)]
        + [slab()],
        out_specs=[slab(), pl.BlockSpec((states, span), lambda i: (0, 0))]
        + [pl.BlockSpec((states, span), lambda i: (0, 0))],
        scratch_shapes=[pltpu.VMEM((heads // 2, span), F32)] * 2,
        input_output_aliases={11: 0},
        compiler_params=pltpu.CompilerParams(vmem_limit_bytes=24 << 20),
        cost_estimate=pl.CostEstimate(
            flops=heads // 2 * 2 * span * span * 256,
            transcendentals=0,
            bytes_accessed=columns // 2 * span * 2 * 4,
        ),
        name="inter",
    )(length, ld, dt, b, c, x, dy, one, two, gb, gc, part)


def local(inputs, out_grad, step_size, log_decay, b_matrix, c_matrix, skip_gain, lengths):
    x, dy, dt, ld = inputs[0], out_grad[0], step_size[0], log_decay[0]
    b, c = b_matrix[0], c_matrix[0]
    tokens, columns = x.shape
    heads = ld.shape[0]
    states = b.shape[0]
    count = lax.axis_size("seq")
    units = count // 2
    if tokens != SPAN or count % 4:
        raise ValueError("unsupported sizes")
    scale_b = 1.0 / math.sqrt(columns)
    scale_c = math.sqrt(states / (columns * count * tokens))
    swap = lambda v: lax.ppermute(v, "seq", [(i, i ^ 1) for i in range(count)])

    def hop(v, s):
        back = units - 1 - s
        pairs = [(2 * s + q, 2 * (s + 1) + q) for q in range(2)]
        pairs += [(2 * back + q, 2 * (back - 1) + q) for q in range(2)]
        return lax.ppermute(v, "seq", pairs)

    small = (ld, dt, b, c, x, dy)
    x1_send, d_send = summary(((True, False),), (BF16,), lengths, *small)
    y1, d_other = swap((x1_send, d_send))
    x2_own, x1_own, x2_send, d_own = summary(
        ((False, True), (True, True), (False, False)), (F32, F32, BF16), lengths, *small
    )
    y2 = swap(x2_send)

    received = []
    for s in range(units - 1):
        near = s < units // 2
        args = (d_other, d_own, x1_own, y1) if near else (d_other, d_own, x2_own, y2)
        (msg,) = chain(not near, *args, received[-1:], True, False)
        received.append(hop(msg, s))
    early = received[: units // 2 - 1]
    late = received[units // 2 - 1 :]
    own1, send1 = chain(False, d_other, d_own, x1_own, y1, early, False, True)
    got1 = swap(send1)
    own2, send2 = chain(True, d_other, d_own, x2_own, y2, late, False, True)
    got2 = swap(send2)

    mix = part = None
    call_heads = 16
    for head0 in range(0, heads, call_heads):
        part, mix = intra(
            head0, call_heads, 8, lengths, skip_gain, ld, dt, b, c, x, dy, mix, part
        )
    part, gb, gc = inter(
        True, False, scale_b, scale_c, lengths, *small, own1, own2, mix, mix, part
    )
    part, gb, gc = inter(
        False, True, scale_b, scale_c, lengths, *small, got1, got2, gb, gc, part
    )
    return (part[None], gb[None], gc[None])


def solution(mesh):
    placed = (
        P("batch", "seq", None),
        P("batch", "seq", None),
        P("batch", None, "seq"),
        P("batch", None, "seq"),
        P("batch", None, "seq"),
        P("batch", None, "seq"),
        P(),
        P("batch"),
    )
    return jax.shard_map(
        local,
        mesh=mesh,
        in_specs=placed,
        out_specs=(P("batch", "seq", None), P("batch", None, "seq"), P("batch", None, "seq")),
        check_vma=False,
    )
```

time: 315 us -> 58.3 us (0.19)
  waiting for transfers between devices: 153 us -> 2.02 us
  matrix products: 49.4 us -> 0 us
  Pallas kernels: 0 us -> 35.5 us
  local copies, waits for them, and re-layouts: 39.1 us -> 6.98 us
  other arithmetic: 31.2 us -> 0 us
  blocking collectives: 24.1 us -> 0 us
  between operations: 15.5 us -> 1.4 us
  starting transfers between devices: 0.08 us -> 11.9 us
    all_gather x2 -> x0, waiting for transfers between devices: 153 us -> none  [carried_in(): pieces = jax.tree.map(lambda part: lax.all_gather(part, axis), value)]
    dot_general x20 -> x0, matrix products: 49.4 us -> none  [the longest x3 13 us: one_group(): jnp.einsum('hut,uhp->thp', kernel, dy_heads, preferred_element_type=jnp.f...]
    pallas_call x0 -> x15, Pallas kernels: none -> 35.5 us  [the longest x6 21.3 us: intra(): pl.pallas_call(functools.partial(intra_kernel, head0, per_step, head_dim,...]
    unnamed x1 -> x0, blocking collectives: 24.1 us -> none
    select_n x15 -> x0, other arithmetic: 23.8 us -> none  [the longest x14 20 us: step(): jnp.where(position < mine, new, old)]
    ppermute x0 -> x8, starting transfers between devices: none -> 11.9 us  [the longest x5 6.31 us: local(): swap = lambda v: lax.ppermute(v, 'seq', [(i, i ^ 1) for i in range(count)])]
    dynamic_slice x9 -> x0, local copies, waits for them, and re-layouts: 9.96 us -> none  [the longest x3 5.48 us: one_group(): lax.dynamic_slice_in_dim(inputs, offset * head_dim, group_size * head_dim...]
    dynamic_update_slice x6 -> x0, local copies, waits for them, and re-layouts: 7.58 us -> none  [one_group(): lax.dynamic_update_slice_in_dim(grad_x, pieces.astype(jnp.bfloat16).resha...]
  transfers between devices with their start and end apart: 2 -> 8, of which waited for: 2 -> 1; matrix products, arithmetic and copies ran while one was open for 7% -> 0% of each run, Pallas kernels for 0% -> 51%
where the time goes in v1:
time: 58.3 us; the launch traced here: 57.8 us
  Pallas kernels  35.5 us (61%)
  starting transfers between devices  11.9 us (20%)
  local copies, waits for them, and re-layouts  6.98 us (12%)
  waiting for transfers between devices  2.02 us (3%)
  between operations  1.4 us (2%)
    pallas_call x6, Pallas kernels, intra(): pl.pallas_call(functools.partial(intra_kernel, head0, per_step, head_dim,...  21.3 us
    pallas_call x2, Pallas kernels, inter(): pl.pallas_call(functools.partial(inter_kernel, own, last, head_dim, scale...  8.95 us
    unnamed x26, local copies, waits for them, and re-layouts  6.98 us
    ppermute x5, starting transfers between devices, local(): swap = lambda v: lax.ppermute(v, 'seq', [(i, i ^ 1) for i in range(count)])  6.31 us
    ppermute x3, starting transfers between devices, hop(): return lax.ppermute(v, 'seq', pairs)  5.63 us
    pallas_call x2, Pallas kernels, summary(): pl.pallas_call(functools.partial(summary_kernel, tasks, head_dim), out_sh...  4.88 us
    ppermute x3, waiting for transfers between devices, hop(): return lax.ppermute(v, 'seq', pairs)  2 us
  transfers between devices with their start and end apart: 8, of which 1 were waited for; matrix products, arithmetic and copies ran while one was open for 0% of the time, Pallas kernels for 51%

profile of v1, /device:TPU:0, one launch (start us, length us, event | category | flops | bytes accessed | tf_op | source)
XLA Modules:
  0.0 57.8 jit_solution(2008520992819409538)
XLA Ops:
  1.3 0.0 copy-start
  1.3 1.9 %copy-done = bf16[1,256,6144]{2,1,0:T(8,128)(2,1)S(1)} copy-done((bf16[1,256,6144]{2,1,0:T(8,128)(2,1)S(1)}, bf16[1,256,6144]{2,1,0:T(8,128)(2,1)}, u32[]{:S(2)}) %copy-start) | copy-done | bytes 3145752
  3.2 0.0 copy-start.2
  3.2 1.9 %copy-done.2 = bf16[1,256,6144]{2,1,0:T(8,128)(2,1)S(1)} copy-done((bf16[1,256,6144]{2,1,0:T(8,128)(2,1)S(1)}, bf16[1,256,6144]{2,1,0:T(8,128)(2,1)}, u32[]{:S(2)}) %copy-start.2) | copy-done | bytes 3145752
  5.1 0.0 copy-start.4
  5.1 0.9 %copy-done.4 = f32[1,96,256]{2,1,0:T(8,128)S(1)} copy-done((f32[1,96,256]{2,1,0:T(8,128)S(1)}, f32[1,96,256]{2,1,0:T(8,128)}, u32[]{:S(2)}) %copy-start.4) | copy-done | bytes 98328
  6.0 0.0 copy-start.6
  6.0 0.9 %copy-done.6 = f32[1,96,256]{2,1,0:T(8,128)S(1)} copy-done((f32[1,96,256]{2,1,0:T(8,128)S(1)}, f32[1,96,256]{2,1,0:T(8,128)}, u32[]{:S(2)}) %copy-start.6) | copy-done | bytes 98328
  6.8 0.0 copy-start.8
  6.8 0.7 %copy-done.8 = bf16[1,16,256]{2,1,0:T(8,128)(2,1)S(1)} copy-done((bf16[1,16,256]{2,1,0:T(8,128)(2,1)S(1)}, bf16[1,16,256]{2,1,0:T(8,128)(2,1)}, u32[]{:S(2)}) %copy-start.8) | copy-done | bytes 8216
  7.5 0.0 copy-start.10
  7.5 0.7 %copy-done.10 = bf16[1,16,256]{2,1,0:T(8,128)(2,1)S(1)} copy-done((bf16[1,16,256]{2,1,0:T(8,128)(2,1)S(1)}, bf16[1,16,256]{2,1,0:T(8,128)(2,1)}, u32[]{:S(2)}) %copy-start.10) | copy-done | bytes 8216
  8.2 0.0 copy-start.1
  8.2 0.0 copy-start.3
  8.2 0.0 copy-start.5
  8.2 0.0 copy-start.7
  8.3 0.0 copy-start.9
  8.3 0.0 copy-start.11
  8.3 1.4 %summary.2 = (bf16[24,16,128]{2,1,0:T(8,128)(2,1)S(1)}, bf16[3,16,128]{2,1,0:T(8,128)(2,1)S(1)}) custom-call(s32[1]{0:T(128)S(6)} %copy.25.len_ref, f32[96,256]{1,0:T(8,128)S(1)} %bitcast.29, f32[96,256]{1,0:T(8,128)S(1)} %bitcast.39, bf16[16,256]{1,0:T(8,128)(2,1)S(1)} %bitcast.49, bf16[16,256]{1,0:T(8,128)(2,1)S(1)} %bitcast.59, ...), custom_call_target="tpu_custom_call" | custom-call | tf_op jit(solution)/shard_map/summary/pallas_call | solution.py:150
  9.6 3.0 %collective-permute-start = (bf16[3,16,128]{2,1,0:T(8,128)(2,1)S(1)}, bf16[3,16,128]{2,1,0:T(8,128)(2,1)S(1)}, u32[]{:S(2)}, u32[]{:S(2)}) collective-permute-start(bf16[3,16,128]{2,1,0:T(8,128)(2,1)S(1)} %get-tuple-element.31), channel_id=1, source_target_pairs={{0,4},{4,0},{8,12},{12,8},{16,20},{20,16},{24,28},{28,24},{1,5},{5... | collective-permute-start | bytes 36872 | tf_op jit(solution)/shard_map/ppermute | solution.py:489
  12.7 0.0 copy-start.12
  12.7 0.1 collective-permute-start.1
  12.8 0.0 copy-done.1
  12.8 0.0 copy-done.3
  12.8 0.0 copy-done.5
  12.8 0.0 copy-done.7
  12.8 0.0 copy-done.9
  12.8 0.0 copy-done.11
  12.8 3.5 %summary.3 = (f32[24,16,128]{2,1,0:T(8,128)S(1)}, f32[24,16,128]{2,1,0:T(8,128)S(1)}, bf16[24,16,128]{2,1,0:T(8,128)(2,1)S(1)}, f32[24,128]{1,0:T(8,128)S(1)}) custom-call(s32[1]{0:T(128)S(6)} %copy.25.len_ref, f32[96,256]{1,0:T(8,128)S(1)} %bitcast.30, f32[96,256]{1,0:T(8,128)S(1)} %bitcast.40, bf16[16,256]{1,0:T(8,128)(2,1)S(1)} %bitcast.50, ...), custom_call_target="tpu_custom_call" | custom-call | tf_op jit(solution)/shard_map/summary/pallas_call | solution.py:150
  16.3 2.0 %collective-permute-start.4 = (bf16[24,16,128]{2,1,0:T(8,128)(2,1)S(1)}, bf16[24,16,128]{2,1,0:T(8,128)(2,1)S(1)}, u32[]{:S(2)}, u32[]{:S(2)}) collective-permute-start(bf16[24,16,128]{2,1,0:T(8,128)(2,1)S(1)} %get-tuple-element.37), channel_id=1, source_target_pairs={{0,4},{4,0},{8,12},{12,8},{16,20},{20,16},{24,28},{28,24},{1,5},{5... | collective-permute-start | bytes 294920 | tf_op jit(solution)/shard_map/ppermute | solution.py:489
  18.3 0.0 copy-done.12
  18.3 3.5 %intra.6 = (bf16[256,6144]{1,0:T(8,128)(2,1)}, f32[256,256]{1,0:T(8,128)S(1)}) custom-call(s32[1]{0:T(128)S(6)} %copy.25.len_ref, f32[96]{0:T(128)S(1)} %copy-done.12, f32[96,256]{1,0:T(8,128)S(1)} %bitcast.31, f32[96,256]{1,0:T(8,128)S(1)} %bitcast.41, bf16[16,256]{1,0:T(8,128)(2,1)S(1)} %bitcast.51, bf16[16,256]{1,0:T(8,128)(2,1)S(1)} %bitcast.61, ...), custom_call_target="tpu_custom_call" | custom-call | flops 1073741824 | bytes 1572864 | tf_op jit(solution)/shard_map/intra/pallas_call | solution.py:331
  21.8 3.6 %intra.7 = (bf16[256,6144]{1,0:T(8,128)(2,1)}, f32[256,256]{1,0:T(8,128)S(1)}) custom-call(s32[1]{0:T(128)S(6)} %copy.25.len_ref, f32[96]{0:T(128)S(1)} %copy-done.12, f32[96,256]{1,0:T(8,128)S(1)} %bitcast.32, f32[96,256]{1,0:T(8,128)S(1)} %bitcast.42, bf16[16,256]{1,0:T(8,128)(2,1)S(1)} %bitcast.52, ...), custom_call_target="tpu_custom_call", output_to_operand_aliasing={{0}: (9, {})} | custom-call | flops 1073741824 | bytes 1572864 | tf_op jit(solution)/shard_map/intra/pallas_call | solution.py:331
  25.4 3.5 %intra.8 = (bf16[256,6144]{1,0:T(8,128)(2,1)}, f32[256,256]{1,0:T(8,128)S(1)}) custom-call(s32[1]{0:T(128)S(6)} %copy.25.len_ref, f32[96]{0:T(128)S(1)} %copy-done.12, f32[96,256]{1,0:T(8,128)S(1)} %bitcast.33, f32[96,256]{1,0:T(8,128)S(1)} %bitcast.43, bf16[16,256]{1,0:T(8,128)(2,1)S(1)} %bitcast.53, ...), custom_call_target="tpu_custom_call", output_to_operand_aliasing={{0}: (9, {})} | custom-call | flops 1073741824 | bytes 1572864 | tf_op jit(solution)/shard_map/intra/pallas_call | solution.py:331
  28.9 0.0 collective-permute-done.refs_0_
  28.9 0.0 collective-permute-done.1.refs_3_
  28.9 0.1 chain.5
  29.0 3.5 %collective-permute-start.2 = (bf16[24,16,128]{2,1,0:T(8,128)(2,1)S(1)}, bf16[24,16,128]{2,1,0:T(8,128)(2,1)S(1)}, u32[]{:S(2)}, u32[]{:S(2)}) collective-permute-start(bf16[24,16,128]{2,1,0:T(8,128)(2,1)S(1)} %chain.5), channel_id=1, source_target_pairs={{0,8},{4,12},{24,16},{28,20},{1,9},{5,13},{25,17},{29,21},{2,10},{... | collective-permute-start | bytes 294920 | tf_op jit(solution)/shard_map/ppermute | solution.py:495
  32.5 3.6 %intra.9 = (bf16[256,6144]{1,0:T(8,128)(2,1)}, f32[256,256]{1,0:T(8,128)S(1)}) custom-call(s32[1]{0:T(128)S(6)} %copy.25.len_ref, f32[96]{0:T(128)S(1)} %copy-done.12, f32[96,256]{1,0:T(8,128)S(1)} %bitcast.34, f32[96,256]{1,0:T(8,128)S(1)} %bitcast.44, bf16[16,256]{1,0:T(8,128)(2,1)S(1)} %bitcast.54, ...), custom_call_target="tpu_custom_call", output_to_operand_aliasing={{0}: (9, {})} | custom-call | flops 1073741824 | bytes 1572864 | tf_op jit(solution)/shard_map/intra/pallas_call | solution.py:331
  36.1 0.0 collective-permute-done.2.refs_4_
  36.1 0.1 chain.7
  36.2 0.7 %collective-permute-start.5 = (bf16[24,16,128]{2,1,0:T(8,128)(2,1)S(1)}, bf16[24,16,128]{2,1,0:T(8,128)(2,1)S(1)}, u32[]{:S(2)}, u32[]{:S(2)}) collective-permute-start(bf16[24,16,128]{2,1,0:T(8,128)(2,1)S(1)} %chain.7), channel_id=1, source_target_pairs={{8,16},{12,20},{16,8},{20,12},{9,17},{13,21},{17,9},{21,13},{10,18... | collective-permute-start | bytes 294920 | tf_op jit(solution)/shard_map/ppermute | solution.py:495
  36.8 3.6 %intra.10 = (bf16[256,6144]{1,0:T(8,128)(2,1)}, f32[256,256]{1,0:T(8,128)S(1)}) custom-call(s32[1]{0:T(128)S(6)} %copy.25.len_ref, f32[96]{0:T(128)S(1)} %copy-done.12, f32[96,256]{1,0:T(8,128)S(1)} %bitcast.35, f32[96,256]{1,0:T(8,128)S(1)} %bitcast.45, bf16[16,256]{1,0:T(8,128)(2,1)S(1)} %bitcast.55, ...), custom_call_target="tpu_custom_call", output_to_operand_aliasing={{0}: (9, {})} | custom-call | flops 1073741824 | bytes 1572864 | tf_op jit(solution)/shard_map/intra/pallas_call | solution.py:331
  40.4 0.0 collective-permute-done.4.refs_3_
  40.4 0.0 collective-permute-done.5.refs_4_
  40.4 0.1 chain.8
  40.5 1.5 %collective-permute-start.6 = (bf16[24,16,128]{2,1,0:T(8,128)(2,1)S(1)}, bf16[24,16,128]{2,1,0:T(8,128)(2,1)S(1)}, u32[]{:S(2)}, u32[]{:S(2)}) collective-permute-start(bf16[24,16,128]{2,1,0:T(8,128)(2,1)S(1)} %chain.8), channel_id=1, source_target_pairs={{16,24},{20,28},{8,0},{12,4},{17,25},{21,29},{9,1},{13,5},{18,26},... | collective-permute-start | bytes 294920 | tf_op jit(solution)/shard_map/ppermute | solution.py:495
  42.0 3.5 %intra.11 = (bf16[256,6144]{1,0:T(8,128)(2,1)}, f32[256,256]{1,0:T(8,128)S(1)}) custom-call(s32[1]{0:T(128)S(6)} %copy.25.len_ref, f32[96]{0:T(128)S(1)} %copy-done.12, f32[96,256]{1,0:T(8,128)S(1)} %bitcast.36, f32[96,256]{1,0:T(8,128)S(1)} %bitcast.46, bf16[16,256]{1,0:T(8,128)(2,1)S(1)} %bitcast.56, ...), custom_call_target="tpu_custom_call", output_to_operand_aliasing={{0}: (9, {})} | custom-call | flops 1073741824 | bytes 1572864 | tf_op jit(solution)/shard_map/intra/pallas_call | solution.py:331
  45.5 0.1 chain.6
  45.6 0.6 %collective-permute-start.3 = (bf16[24,16,128]{2,1,0:T(8,128)(2,1)S(1)}, bf16[24,16,128]{2,1,0:T(8,128)(2,1)S(1)}, u32[]{:S(2)}, u32[]{:S(2)}) collective-permute-start(bf16[24,16,128]{2,1,0:T(8,128)(2,1)S(1)} %get-tuple-element.35), channel_id=1, source_target_pairs={{0,4},{4,0},{8,12},{12,8},{16,20},{20,16},{24,28},{28,24},{1,5},{5... | collective-permute-start | bytes 294920 | tf_op jit(solution)/shard_map/ppermute | solution.py:489
  46.2 2.0 %collective-permute-done.6.refs_5_ = bf16[24,16,128]{2,1,0:T(8,128)(2,1)S(1)} collective-permute-done((bf16[24,16,128]{2,1,0:T(8,128)(2,1)S(1)}, bf16[24,16,128]{2,1,0:T(8,128)(2,1)S(1)}, u32[]{:S(2)}, u32[]{:S(2)}) %collective-permute-start.6) | collective-permute-done | bytes 98336 | tf_op jit(solution)/shard_map/ppermute | solution.py:495
  48.2 0.1 chain.9
  48.3 0.6 %collective-permute-start.7 = (bf16[24,16,128]{2,1,0:T(8,128)(2,1)S(1)}, bf16[24,16,128]{2,1,0:T(8,128)(2,1)S(1)}, u32[]{:S(2)}, u32[]{:S(2)}) collective-permute-start(bf16[24,16,128]{2,1,0:T(8,128)(2,1)S(1)} %get-tuple-element.38), channel_id=1, source_target_pairs={{0,4},{4,0},{8,12},{12,8},{16,20},{20,16},{24,28},{28,24},{1,5},{5... | collective-permute-start | bytes 294920 | tf_op jit(solution)/shard_map/ppermute | solution.py:489
  48.9 4.4 %inter.2 = (bf16[256,6144]{1,0:T(8,128)(2,1)}, f32[16,256]{1,0:T(8,128)S(1)}, f32[16,256]{1,0:T(8,128)S(1)}) custom-call(s32[1]{0:T(128)S(6)} %copy.25.len_ref, f32[96,256]{1,0:T(8,128)S(1)} %bitcast.37, f32[96,256]{1,0:T(8,128)S(1)} %bitcast.47, bf16[16,256]{1,0:T(8,128)(2,1)S(1)} %bitcast.57, ...), custom_call_target="tpu_custom_call", output_to_operand_aliasing={{0}: (11, {})} | custom-call | flops 1610612736 | bytes 6291456 | tf_op jit(solution)/shard_map/inter/pallas_call | solution.py:454
  53.3 0.0 collective-permute-done.3.one_ref
  53.3 0.0 collective-permute-done.7.two_ref
  53.3 4.6 %inter.3 = (bf16[256,6144]{1,0:T(8,128)(2,1)}, f32[16,256]{1,0:T(8,128)}, f32[16,256]{1,0:T(8,128)}) custom-call(s32[1]{0:T(128)S(6)} %copy.25.len_ref, f32[96,256]{1,0:T(8,128)S(1)} %bitcast.38, f32[96,256]{1,0:T(8,128)S(1)} %bitcast.48, bf16[16,256]{1,0:T(8,128)(2,1)S(1)} %bitcast.58, ...), custom_call_target="tpu_custom_call", output_to_operand_aliasing={{0}: (11, {})} | custom-call | flops 1610612736 | bytes 6291456 | tf_op jit(solution)/shard_map/inter/pallas_call | solution.py:454
Async XLA Ops:
  1.3 1.9 %copy-start = (bf16[1,256,6144]{2,1,0:T(8,128)(2,1)S(1)}, bf16[1,256,6144]{2,1,0:T(8,128)(2,1)}, u32[]{:S(2)}) copy-start(bf16[1,256,6144]{2,1,0:T(8,128)(2,1)} %param.8) | copy-start | bytes 9437188
  3.2 1.9 %copy-start.2 = (bf16[1,256,6144]{2,1,0:T(8,128)(2,1)S(1)}, bf16[1,256,6144]{2,1,0:T(8,128)(2,1)}, u32[]{:S(2)}) copy-start(bf16[1,256,6144]{2,1,0:T(8,128)(2,1)} %param.9) | copy-start | bytes 9437188
  5.1 0.9 %copy-start.4 = (f32[1,96,256]{2,1,0:T(8,128)S(1)}, f32[1,96,256]{2,1,0:T(8,128)}, u32[]{:S(2)}) copy-start(f32[1,96,256]{2,1,0:T(8,128)} %param.11) | copy-start | bytes 294916
  6.0 0.9 %copy-start.6 = (f32[1,96,256]{2,1,0:T(8,128)S(1)}, f32[1,96,256]{2,1,0:T(8,128)}, u32[]{:S(2)}) copy-start(f32[1,96,256]{2,1,0:T(8,128)} %param.10) | copy-start | bytes 294916
  6.8 0.7 %copy-start.8 = (bf16[1,16,256]{2,1,0:T(8,128)(2,1)S(1)}, bf16[1,16,256]{2,1,0:T(8,128)(2,1)}, u32[]{:S(2)}) copy-start(bf16[1,16,256]{2,1,0:T(8,128)(2,1)} %param.12) | copy-start | bytes 24580
  7.5 0.7 %copy-start.10 = (bf16[1,16,256]{2,1,0:T(8,128)(2,1)S(1)}, bf16[1,16,256]{2,1,0:T(8,128)(2,1)}, u32[]{:S(2)}) copy-start(bf16[1,16,256]{2,1,0:T(8,128)(2,1)} %param.13) | copy-start | bytes 24580
  8.2 4.5 %copy-start.1 = (bf16[1,256,6144]{2,1,0:T(8,128)(2,1)S(1)}, bf16[1,256,6144]{2,1,0:T(8,128)(2,1)}, u32[]{:S(2)}) copy-start(bf16[1,256,6144]{2,1,0:T(8,128)(2,1)} %param.8) | copy-start | bytes 9437188
  8.2 4.5 %copy-start.3 = (bf16[1,256,6144]{2,1,0:T(8,128)(2,1)S(1)}, bf16[1,256,6144]{2,1,0:T(8,128)(2,1)}, u32[]{:S(2)}) copy-start(bf16[1,256,6144]{2,1,0:T(8,128)(2,1)} %param.9) | copy-start | bytes 9437188
  8.2 4.5 %copy-start.5 = (f32[1,96,256]{2,1,0:T(8,128)S(1)}, f32[1,96,256]{2,1,0:T(8,128)}, u32[]{:S(2)}) copy-start(f32[1,96,256]{2,1,0:T(8,128)} %param.11) | copy-start | bytes 294916
  8.2 4.5 %copy-start.7 = (f32[1,96,256]{2,1,0:T(8,128)S(1)}, f32[1,96,256]{2,1,0:T(8,128)}, u32[]{:S(2)}) copy-start(f32[1,96,256]{2,1,0:T(8,128)} %param.10) | copy-start | bytes 294916
  8.3 4.5 %copy-start.9 = (bf16[1,16,256]{2,1,0:T(8,128)(2,1)S(1)}, bf16[1,16,256]{2,1,0:T(8,128)(2,1)}, u32[]{:S(2)}) copy-start(bf16[1,16,256]{2,1,0:T(8,128)(2,1)} %param.12) | copy-start | bytes 24580
  8.3 4.5 %copy-start.11 = (bf16[1,16,256]{2,1,0:T(8,128)(2,1)S(1)}, bf16[1,16,256]{2,1,0:T(8,128)(2,1)}, u32[]{:S(2)}) copy-start(bf16[1,16,256]{2,1,0:T(8,128)(2,1)} %param.13) | copy-start | bytes 24580
  9.6 19.3 %collective-permute-start = (bf16[3,16,128]{2,1,0:T(8,128)(2,1)S(1)}, bf16[3,16,128]{2,1,0:T(8,128)(2,1)S(1)}, u32[]{:S(2)}, u32[]{:S(2)}) collective-permute-start(bf16[3,16,128]{2,1,0:T(8,128)(2,1)S(1)} %get-tuple-element.31), channel_id=1, source_target_pairs={{0,4},{4,0},{8,12},{12,8},{16,20},{20,16},{24,28},{28,24},{1,5},{5... | collective-permute-start | bytes 36872 | tf_op jit(solution)/shard_map/ppermute | solution.py:489
  12.7 5.7 %copy-start.12 = (f32[96]{0:T(128)S(1)}, f32[96]{0:T(128)}, u32[]{:S(2)}) copy-start(f32[96]{0:T(128)} %skip_ref.11) | copy-start | bytes 1156
  12.7 16.2 %collective-permute-start.1 = (bf16[24,16,128]{2,1,0:T(8,128)(2,1)S(1)}, bf16[24,16,128]{2,1,0:T(8,128)(2,1)S(1)}, u32[]{:S(2)}, u32[]{:S(2)}) collective-permute-start(bf16[24,16,128]{2,1,0:T(8,128)(2,1)S(1)} %get-tuple-element.34), channel_id=1, source_target_pairs={{0,4},{4,0},{8,12},{12,8},{16,20},{20,16},{24,28},{28,24},{1,5},{5... | collective-permute-start | bytes 294920 | tf_op jit(solution)/shard_map/ppermute | solution.py:489
  16.3 24.1 %collective-permute-start.4 = (bf16[24,16,128]{2,1,0:T(8,128)(2,1)S(1)}, bf16[24,16,128]{2,1,0:T(8,128)(2,1)S(1)}, u32[]{:S(2)}, u32[]{:S(2)}) collective-permute-start(bf16[24,16,128]{2,1,0:T(8,128)(2,1)S(1)} %get-tuple-element.37), channel_id=1, source_target_pairs={{0,4},{4,0},{8,12},{12,8},{16,20},{20,16},{24,28},{28,24},{1,5},{5... | collective-permute-start | bytes 294920 | tf_op jit(solution)/shard_map/ppermute | solution.py:489
  29.0 7.1 %collective-permute-start.2 = (bf16[24,16,128]{2,1,0:T(8,128)(2,1)S(1)}, bf16[24,16,128]{2,1,0:T(8,128)(2,1)S(1)}, u32[]{:S(2)}, u32[]{:S(2)}) collective-permute-start(bf16[24,16,128]{2,1,0:T(8,128)(2,1)S(1)} %chain.5), channel_id=1, source_target_pairs={{0,8},{4,12},{24,16},{28,20},{1,9},{5,13},{25,17},{29,21},{2,10},{... | collective-permute-start | bytes 294920 | tf_op jit(solution)/shard_map/ppermute | solution.py:495
  36.2 4.3 %collective-permute-start.5 = (bf16[24,16,128]{2,1,0:T(8,128)(2,1)S(1)}, bf16[24,16,128]{2,1,0:T(8,128)(2,1)S(1)}, u32[]{:S(2)}, u32[]{:S(2)}) collective-permute-start(bf16[24,16,128]{2,1,0:T(8,128)(2,1)S(1)} %chain.7), channel_id=1, source_target_pairs={{8,16},{12,20},{16,8},{20,12},{9,17},{13,21},{17,9},{21,13},{10,18... | collective-permute-start | bytes 294920 | tf_op jit(solution)/shard_map/ppermute | solution.py:495
  40.5 7.7 %collective-permute-start.6 = (bf16[24,16,128]{2,1,0:T(8,128)(2,1)S(1)}, bf16[24,16,128]{2,1,0:T(8,128)(2,1)S(1)}, u32[]{:S(2)}, u32[]{:S(2)}) collective-permute-start(bf16[24,16,128]{2,1,0:T(8,128)(2,1)S(1)} %chain.8), channel_id=1, source_target_pairs={{16,24},{20,28},{8,0},{12,4},{17,25},{21,29},{9,1},{13,5},{18,26},... | collective-permute-start | bytes 294920 | tf_op jit(solution)/shard_map/ppermute | solution.py:495
  45.6 7.7 %collective-permute-start.3 = (bf16[24,16,128]{2,1,0:T(8,128)(2,1)S(1)}, bf16[24,16,128]{2,1,0:T(8,128)(2,1)S(1)}, u32[]{:S(2)}, u32[]{:S(2)}) collective-permute-start(bf16[24,16,128]{2,1,0:T(8,128)(2,1)S(1)} %get-tuple-element.35), channel_id=1, source_target_pairs={{0,4},{4,0},{8,12},{12,8},{16,20},{20,16},{24,28},{28,24},{1,5},{5... | collective-permute-start | bytes 294920 | tf_op jit(solution)/shard_map/ppermute | solution.py:489
  48.3 5.0 %collective-permute-start.7 = (bf16[24,16,128]{2,1,0:T(8,128)(2,1)S(1)}, bf16[24,16,128]{2,1,0:T(8,128)(2,1)S(1)}, u32[]{:S(2)}, u32[]{:S(2)}) collective-permute-start(bf16[24,16,128]{2,1,0:T(8,128)(2,1)S(1)} %get-tuple-element.38), channel_id=1, source_target_pairs={{0,4},{4,0},{8,12},{12,8},{16,20},{20,16},{24,28},{28,24},{1,5},{5... | collective-permute-start | bytes 294920 | tf_op jit(solution)/shard_map/ppermute | solution.py:489

commit v2 on v0

v2 whole, which is shorter than its diff:
```python
import functools
import math

import jax
import jax.numpy as jnp
from jax import lax
from jax.experimental import pallas as pl
from jax.experimental.pallas import tpu as pltpu
from jax.sharding import PartitionSpec as P

SPAN = 256
LANES = 128
SLAB = 2 * LANES
LOG2E = math.log2(math.e)
F32 = jnp.float32
BF16 = jnp.bfloat16
NT = (((1,), (1,)), ((), ()))
TN = (((0,), (0,)), ((), ()))
OTHER, OWN = 0, 1


def place():
    idx = lax.axis_index("seq")
    count = lax.axis_size("seq")
    return idx, lax.rem(idx, 2), idx < count // 2


def mm(a, b, dims=None):
    if dims is None:
        return jnp.dot(a, b, preferred_element_type=F32)
    return lax.dot_general(a, b, dims, preferred_element_type=F32)


def whole():
    return pl.BlockSpec(memory_space=pltpu.VMEM)


def smem():
    return pl.BlockSpec(memory_space=pltpu.SMEM)


def hbm():
    return pl.BlockSpec(memory_space=pltpu.HBM)


def iota(shape, axis):
    return lax.broadcasted_iota(jnp.int32, shape, axis)


def running_sum(values):
    rows, span = values.shape
    sub = span // 2
    high = values.astype(BF16)
    rest = values - high.astype(F32)
    middle = rest.astype(BF16)
    low = (rest - middle.astype(F32)).astype(BF16)
    upper = (iota((sub, sub), 0) <= iota((sub, sub), 1)).astype(F32).astype(BF16)
    pieces = jnp.concatenate([high, middle, low], axis=0)
    halves = []
    for s in range(2):
        sums = mm(pieces[:, s * sub : (s + 1) * sub], upper)
        halves.append(sums[:rows] + sums[rows : 2 * rows] + sums[2 * rows :])
    return jnp.concatenate(halves, axis=1)


def weights(ld, dt):
    cum = running_sum(ld)
    rows, span = cum.shape
    sub = span // 2
    end_a, end_b = cum[:, sub - 1 : sub], cum[:, span - 1 : span]
    ends = jnp.where(iota(cum.shape, 1) < sub, end_a, end_b)
    return cum, dt * jnp.exp(ends - cum), jnp.exp(cum), jnp.exp(end_a), jnp.exp(end_b)


def spread(column, scratch_ref, head_dim):
    rows = scratch_ref.shape[0]
    scratch_ref[...] = jnp.broadcast_to(column, scratch_ref.shape)
    even = scratch_ref[pl.ds(0, rows // 2, stride=2), :]
    odd = scratch_ref[pl.ds(1, rows // 2, stride=2), :]
    return jnp.where(iota(even.shape, 1) < head_dim, even, odd)


def load_tasks(tasks, kinds, mine, x_ref, dy_ref, data_ref, sems):
    width = data_ref.shape[3]
    chunks = sems.shape[1]
    chunk = width // chunks

    def copy(t, i, kind, src):
        rel = OWN if tasks[t][1] else OTHER
        half = mine if tasks[t][1] else 1 - mine
        start = pl.multiple_of(half * width + i * chunk, LANES)
        return pltpu.make_async_copy(
            src.at[:, pl.ds(start, chunk)],
            data_ref.at[rel, kind, :, pl.ds(i * chunk, chunk)],
            sems.at[t, i],
        )

    for t in range(len(tasks)):
        for i in range(chunks):

            @pl.when(kinds[t] == 0)
            def _():
                copy(t, i, 0, x_ref).start()

            @pl.when(kinds[t] == 1)
            def _():
                copy(t, i, 1, dy_ref).start()

    return lambda t, i: copy(t, i, kinds[t], x_ref).wait()


def run_task(t, kind, rel, valid, wait, chunks, head_dim, b, c, w_ref, rows_ref, data_ref, x_ref, sub_ref):
    span, width = data_ref.shape[2:]
    half_span = span // 2
    chunk = width // chunks
    is_state = kind == 0
    mat = jnp.where(is_state, b, c)
    states = mat.shape[0]
    per = SLAB // head_dim
    low = iota((states, LANES), 1) < head_dim
    for i in range(chunks):
        wait(t, i)

        @pl.when(jnp.logical_and(kind == 1, valid < span))
        def _():
            cols = pl.ds(i * chunk, chunk)
            inside = iota((span, chunk), 0) < valid
            data = data_ref[rel, 1, :, cols].astype(F32)
            data_ref[rel, 1, :, cols] = jnp.where(inside, data, 0.0).astype(BF16)

        for g in range(i * chunk // SLAB, (i + 1) * chunk // SLAB):
            lhs = jnp.concatenate(
                [(mat * w_ref[pl.ds(per * g + j, 1), :]).astype(BF16) for j in range(per)],
                axis=0,
            )
            cols = pl.ds(SLAB * g, SLAB)
            parts = [
                mm(
                    lhs[:, s * half_span : (s + 1) * half_span],
                    data_ref[rel, kind, pl.ds(s * half_span, half_span), cols],
                )
                for s in range(2)
            ]
            for q in range(2):
                lanes = slice(q * LANES, (q + 1) * LANES)
                top = slice(2 * q * states, (2 * q + 1) * states)
                bottom = slice((2 * q + 1) * states, (2 * q + 2) * states)
                e0, e1 = [jnp.where(low, p[top, lanes], p[bottom, lanes]) for p in parts]
                j = 2 * g + q
                d_a, d_b = rows_ref[0, pl.ds(j, 1), :], rows_ref[1, pl.ds(j, 1), :]
                total = jnp.where(is_state, d_b, 1.0) * e0 + jnp.where(is_state, 1.0, d_a) * e1
                x_ref[j] = total.astype(x_ref.dtype)
                sub_ref[j] = jnp.where(is_state, e0, e1)


def first_kernel(
    head_dim, len_ref, ld_hbm, dt_hbm, b_hbm, c_hbm, x_ref, dy_ref,
    msg_ref, sub_ref, data_ref, ld_ref, dt_ref, b_ref, c_ref, w_ref, rows_ref, spread_ref, sems, small_sems
):
    idx, mine, lower = place()
    kind = jnp.where(lower, 0, 1)
    span = ld_ref.shape[1]
    half_heads = ld_ref.shape[0] // 2
    small = [
        pltpu.make_async_copy(src, dst, small_sems.at[i])
        for i, (src, dst) in enumerate(
            ((ld_hbm, ld_ref), (dt_hbm, dt_ref), (b_hbm, b_ref), (c_hbm, c_ref))
        )
    ]
    for copy in small:
        copy.start()
    wait = load_tasks(((True, False),), (kind,), mine, x_ref, dy_ref, data_ref, sems)
    for copy in small:
        copy.wait()
    rows = pl.ds(pl.multiple_of((1 - mine) * half_heads, 8), half_heads)
    cum, ws, wg, d_a, d_b = weights(ld_ref[rows, :], dt_ref[rows, :])
    w_ref[...] = jnp.where(kind == 0, ws, wg)
    rows_a = spread(d_a, spread_ref, head_dim)
    rows_b = spread(d_b, spread_ref, head_dim)
    rows_ref[0] = rows_a
    rows_ref[1] = rows_b
    both = rows_a * rows_b
    high = both.astype(BF16).astype(F32)
    tiles = sub_ref.shape[0]
    extra = jnp.concatenate([high, both - high], axis=0).astype(BF16)
    msg_ref[tiles:] = extra.reshape((msg_ref.shape[0] - tiles,) + msg_ref.shape[1:])
    valid = len_ref[0] - idx * span
    run_task(
        0, kind, OTHER, valid, wait, sems.shape[1], head_dim,
        b_ref[...].astype(F32), c_ref[...].astype(F32), w_ref, rows_ref, data_ref, msg_ref, sub_ref,
    )


def first_part(length, ld, dt, b, c, x, dy):
    heads, span = ld.shape
    columns = x.shape[1]
    states = b.shape[0]
    tiles = columns // 2 // LANES
    pairs = heads // 4
    tile = lambda n, t: jax.ShapeDtypeStruct((n, states, LANES), t)
    same = lambda a: jax.ShapeDtypeStruct(a.shape, a.dtype)
    return pl.pallas_call(
        functools.partial(first_kernel, columns // heads),
        out_shape=[
            tile(tiles + 2 * pairs // states, BF16),
            tile(tiles, F32),
            jax.ShapeDtypeStruct((2, 2, span, columns // 2), BF16),
            same(ld), same(dt), same(b), same(c),
        ],
        in_specs=[smem()] + [hbm() for _ in range(6)],
        out_specs=[whole() for _ in range(7)],
        scratch_shapes=[
            pltpu.VMEM((heads // 2, span), F32),
            pltpu.VMEM((2, pairs, LANES), F32),
            pltpu.VMEM((heads // 2, LANES), F32),
            pltpu.SemaphoreType.DMA((1, 4)),
            pltpu.SemaphoreType.DMA((4,)),
        ],
        compiler_params=pltpu.CompilerParams(vmem_limit_bytes=12 << 20),
        name="first",
    )(length, ld, dt, b, c, x, dy)


def rest_kernel(
    head_dim, len_ref, skip_ref, ld_ref, dt_ref, b_ref, c_ref, data_in, x_ref, dy_ref,
    data_ref, send_ref, x1_ref, x2_ref, sub_other_ref, sub1_ref, sub2_ref, d_ref, rows_ref,
    w_ref, row_ref, col_ref, cb_ref, skip_rows_ref, task_w_ref, spread_ref, sems
):
    idx, mine, lower = place()
    kind1 = jnp.where(lower, 0, 1)
    kind2 = 1 - kind1
    heads, span = ld_ref.shape
    half_heads = heads // 2
    pairs = half_heads // 2
    sub = span // 2
    tasks = ((True, True), (False, True), (False, False))
    kinds = (kind1, kind2, kind2)
    wait = load_tasks(tasks, kinds, mine, x_ref, dy_ref, data_ref, sems)
    low = iota((1, LANES), 1) < head_dim
    for rel in (OTHER, OWN):
        half = mine if rel == OWN else 1 - mine
        rows = pl.ds(pl.multiple_of(half * half_heads, 8), half_heads)
        dt = dt_ref[rows, :]
        cum, ws, wg, d_a, d_b = weights(ld_ref[rows, :], dt)
        w_ref[rel, 0] = ws
        w_ref[rel, 1] = wg
        rows_ref[rel, 0] = spread(d_a, spread_ref, head_dim)
        rows_ref[rel, 1] = spread(d_b, spread_ref, head_dim)
        row = cum * LOG2E
        row_ref[rel] = row
        col_ref[rel] = (row - jnp.log(dt) * LOG2E).T
        for j in range(pairs):
            at = half * half_heads + 2 * j
            skip_rows_ref[rel, pl.ds(j, 1), :] = jnp.where(low, skip_ref[at], skip_ref[at + 1])
    d_ref[...] = rows_ref[OWN, 0] * rows_ref[OWN, 1]
    for s in range(2):
        cols = slice(s * sub, (s + 1) * sub)
        dots = mm(b_ref[:, cols], c_ref[:, cols], TN)
        cb_ref[s] = jnp.where(iota(dots.shape, 1) >= iota(dots.shape, 0), dots, 0.0)
    b, c = b_ref[...].astype(F32), c_ref[...].astype(F32)
    valid = len_ref[0] - idx * span
    outs = ((x1_ref, sub1_ref), (x2_ref, sub2_ref), (send_ref, sub_other_ref))
    for t, (first, own) in enumerate(tasks):
        rel = OWN if own else OTHER
        task_w_ref[t] = jnp.where(kinds[t] == 0, w_ref[rel, 0], w_ref[rel, 1])
        run_task(
            t, kinds[t], rel, valid, wait, sems.shape[1], head_dim, b, c,
            task_w_ref.at[t], rows_ref.at[rel], data_ref, outs[t][0], outs[t][1],
        )


def rest_part(length, skip, ld, dt, b, c, data, x, dy):
    heads, span = ld.shape
    columns = x.shape[1]
    states = b.shape[0]
    tiles = columns // 2 // LANES
    pairs = heads // 4
    sub = span // 2
    shape = jax.ShapeDtypeStruct
    tile = lambda t: shape((tiles, states, LANES), t)
    outs = [
        shape(data.shape, BF16),
        tile(BF16), tile(F32), tile(F32), tile(F32), tile(F32), tile(F32),
        shape((pairs, LANES), F32),
        shape((2, 2, pairs, LANES), F32),
        shape((2, 2, heads // 2, span), F32),
        shape((2, heads // 2, span), F32),
        shape((2, span, heads // 2), F32),
        shape((2, sub, sub), F32),
        shape((2, pairs, LANES), F32),
    ]
    return pl.pallas_call(
        functools.partial(rest_kernel, columns // heads),
        out_shape=outs,
        in_specs=[smem(), smem()] + [whole() for _ in range(5)] + [hbm(), hbm()],
        out_specs=[whole() for _ in outs],
        scratch_shapes=[
            pltpu.VMEM((3, heads // 2, span), F32),
            pltpu.VMEM((heads // 2, LANES), F32),
            pltpu.SemaphoreType.DMA((3, 4)),
        ],
        input_output_aliases={6: 0},
        compiler_params=pltpu.CompilerParams(vmem_limit_bytes=16 << 20),
        name="rest",
    )(length, skip, ld, dt, b, c, data, x, dy)


def pair_flags(second):
    idx, mine, lower = place()
    ahead = jnp.where(lower, mine == 0, mine == 1)
    return jnp.logical_not(ahead) if second else ahead


def chain_kernel(second, carries, finish, msg, *refs):
    decay_ref, mine_ref, x_ref, y_ref = refs[:4]
    carry_refs = refs[4 : 4 + carries]
    rest = refs[4 + carries :]
    dp_ref = rest[-1]
    ahead = pair_flags(second)
    tiles = x_ref.shape[0]
    count = dp_ref.shape[0]
    both = decay_ref[tiles:].reshape(2 * count, LANES).astype(F32)
    dp_ref[...] = both[:count] + both[count:]
    for j in range(tiles):
        dp = dp_ref[pl.ds(j, 1), :]
        d = mine_ref[pl.ds(j, 1), :]
        x = x_ref[j]
        y = y_ref[j].astype(F32)
        carry = None
        for ref in carry_refs:
            carry = ref[j].astype(F32) if carry is None else carry + ref[j].astype(F32)
        at = 0
        if msg:
            total = jnp.where(ahead, dp, d) * jnp.where(ahead, x, y) + jnp.where(ahead, y, x)
            if carry is not None:
                total = total + d * dp * carry
            rest[at][j] = total.astype(BF16)
            at += 1
        if finish:
            if carry is None:
                carry = jnp.zeros_like(x)
            passed = jnp.where(ahead, d, dp) * carry + jnp.where(ahead, x, y)
            rest[at][j] = jnp.where(ahead, carry, passed).astype(BF16)
            rest[at + 1][j] = jnp.where(ahead, passed, carry).astype(BF16)


def chain(second, decay, mine, x, y, carries, msg, finish):
    shape = jax.ShapeDtypeStruct(x.shape, BF16)
    outs = int(msg) + 2 * int(finish)
    return pl.pallas_call(
        functools.partial(chain_kernel, second, len(carries), finish, msg),
        out_shape=[shape] * outs,
        in_specs=[whole() for _ in range(4 + len(carries))],
        out_specs=[whole() for _ in range(outs)],
        scratch_shapes=[pltpu.VMEM(mine.shape, F32)],
        compiler_params=pltpu.CompilerParams(vmem_limit_bytes=4 << 20),
        name="chain",
    )(decay, mine, x, y, *carries)


def intra_kernel(rel, pair0, pairs, head_dim, first, row_ref, col_ref, cb_ref, skip_ref, data_ref, *refs):
    mix_in = None if first else refs[0]
    part_ref, mix_ref = refs[-2:]
    sub = cb_ref.shape[1]
    lane = iota((1, LANES), 1)
    keep = [
        (lane < head_dim).astype(F32).astype(BF16),
        (lane >= head_dim).astype(F32).astype(BF16),
    ]
    for s in range(2):
        here = pl.ds(s * sub, sub)
        acc = None if first else mix_in[s]
        for p in range(pairs):
            cols = pl.ds((pair0 + p) * LANES, LANES)
            xs = data_ref[rel, 0, here, cols]
            ys = data_ref[rel, 1, here, cols]
            split = jnp.concatenate([ys * keep[0], ys * keep[1]], axis=0)
            scores = mm(xs, split, NT)
            kernels = []
            for j in range(2):
                h = 2 * (pair0 + p) + j
                row = row_ref[rel, pl.ds(h, 1), here]
                col = col_ref[rel, here, pl.ds(h, 1)]
                decay = jnp.exp2(jnp.minimum(row - col, 100.0))
                kernels.append((decay * cb_ref[s]).astype(BF16))
                term = decay * scores[:, j * sub : (j + 1) * sub]
                acc = term if acc is None else acc + term
            within = mm(jnp.concatenate(kernels, axis=1), split)
            skip = skip_ref[rel, pl.ds(pair0 + p, 1), :]
            part_ref[here, pl.ds(p * LANES, LANES)] = (
                within + skip * ys.astype(F32)
            ).astype(part_ref.dtype)
        mix_ref[s] = acc


def intra(rel, pair0, pairs, head_dim, row, col, cb, skip, data, mix):
    span = data.shape[2]
    args = [row, col, cb, skip, data] + ([] if mix is None else [mix])
    heads = 2 * pairs
    return pl.pallas_call(
        functools.partial(intra_kernel, rel, pair0, pairs, head_dim, mix is None),
        out_shape=[
            jax.ShapeDtypeStruct((span, pairs * LANES), BF16),
            jax.ShapeDtypeStruct(cb.shape, F32),
        ],
        in_specs=[whole() for _ in args],
        out_specs=[whole(), whole()],
        compiler_params=pltpu.CompilerParams(vmem_limit_bytes=16 << 20),
        cost_estimate=pl.CostEstimate(
            flops=heads * 2 * span * span * 128,
            transcendentals=heads * span * span // 2,
            bytes_accessed=heads * head_dim * span * 2 * 3,
        ),
        name="intra",
    )(*args)


def inter_kernel(last, head_dim, slabs, scale_b, scale_c, b_ref, c_ref, w_ref, rows_ref, data_ref,
                 one_ref, two_ref, sub1_ref, sub2_ref, *refs):
    idx, mine, lower = place()
    rel = OTHER if last else OWN
    parts = refs[:slabs]
    refs = refs[slabs:]
    if last:
        gb_in, gc_in, slab_in, out_ref, gb_ref, gc_ref, buf_ref, sems = refs
    else:
        mix_ref, buf_ref, gb_ref, gc_ref = refs
    span, width = data_ref.shape[2:]
    sub = span // 2
    states = b_ref.shape[0]
    per = SLAB // head_dim
    if last:
        own_copy = pltpu.make_async_copy(
            slab_in, out_ref.at[:, pl.ds(pl.multiple_of(mine * width, LANES), width)], sems.at[0]
        )
        own_copy.start()
    rowhead = iota((per * states, SLAB), 0) // states
    lanehead = iota((per * states, SLAB), 1) // head_dim
    diag = (rowhead == lanehead).astype(F32).astype(BF16)
    b = b_ref[...].astype(F32)
    groups = width // SLAB
    slab_width = width // slabs
    gb = [None, None]
    gc = [None, None]
    copies = []
    sends = 1 if not last else sems.shape[0] - 1
    for g in range(groups):
        j = 2 * g
        pair = lambda ref: jnp.concatenate([ref[j], ref[j + 1]], axis=1)
        one, two, sub1, sub2 = pair(one_ref), pair(two_ref), pair(sub1_ref), pair(sub2_ref)
        grad = jnp.where(lower, two, one)
        state = jnp.where(lower, one, two)
        grad_sub = jnp.where(lower, sub2, sub1)
        state_sub = jnp.where(lower, sub1, sub2)
        row = lambda k: jnp.concatenate(
            [rows_ref[rel, k, pl.ds(j, 1), :], rows_ref[rel, k, pl.ds(j + 1, 1), :]], axis=1
        )
        grads = [(grad_sub + row(1) * grad.astype(F32)).astype(BF16), grad]
        states_in = [state, (state_sub + row(0) * state.astype(F32)).astype(BF16)]
        cols = pl.ds(g * SLAB, SLAB)
        part = parts[g * SLAB // slab_width]
        part_cols = pl.ds(g * SLAB % slab_width, SLAB)
        for s in range(2):
            here = pl.ds(s * sub, sub)
            rows_s = [w_ref[rel, 0, pl.ds(per * g + i, 1), here] for i in range(per)]
            rows_g = [w_ref[rel, 1, pl.ds(per * g + i, 1), here] for i in range(per)]
            grad_diag = jnp.concatenate([grads[s]] * per, axis=0) * diag
            state_diag = jnp.concatenate([states_in[s]] * per, axis=0) * diag
            bs = b[:, s * sub : (s + 1) * sub]
            left = jnp.concatenate([(bs * r).astype(BF16) for r in rows_s], axis=0)
            across = mm(left, grad_diag, TN)
            buf_ref[here, cols] = (part[here, part_cols].astype(F32) + across).astype(BF16)
            rb = mm(grad_diag, data_ref[rel, 0, here, cols], NT)
            rc = mm(state_diag, data_ref[rel, 1, here, cols], NT)
            for i in range(per):
                rows = slice(i * states, (i + 1) * states)
                tb, tc = rows_s[i] * rb[rows], rows_g[i] * rc[rows]
                gb[s] = tb if gb[s] is None else gb[s] + tb
                gc[s] = tc if gc[s] is None else gc[s] + tc
        if last and (g + 1) % (groups // sends) == 0:
            k = (g + 1) // (groups // sends) - 1
            wide = width // sends
            start = pl.multiple_of((1 - mine) * width + k * wide, LANES)
            send = pltpu.make_async_copy(
                buf_ref.at[:, pl.ds(k * wide, wide)],
                out_ref.at[:, pl.ds(start, wide)],
                sems.at[k + 1],
            )
            send.start()
            copies.append(send)
    gb = jnp.concatenate(gb, axis=1)
    gc = jnp.concatenate(gc, axis=1)
    if last:
        gb_ref[...] = (gb_in[...] + gb) * scale_b
        gc_ref[...] = (gc_in[...] + gc) * scale_c
        own_copy.wait()
        for send in copies:
            send.wait()
    else:
        mixed_b, mixed_c = [], []
        for s in range(2):
            here = slice(s * sub, (s + 1) * sub)
            keep = iota((sub, sub), 1) >= iota((sub, sub), 0)
            mix = jnp.where(keep, mix_ref[s], 0.0)
            high = mix.astype(BF16)
            rest = (mix - high.astype(F32)).astype(BF16)
            bs, cs = b_ref[:, here], c_ref[:, here]
            mixed_b.append(mm(cs, high, NT) + mm(cs, rest, NT))
            mixed_c.append(mm(bs, high) + mm(bs, rest))
        gb_ref[...] = gb + jnp.concatenate(mixed_b, axis=1)
        gc_ref[...] = gc + jnp.concatenate(mixed_c, axis=1)


def inter(last, head_dim, scale_b, scale_c, b, c, w, rows, data, one, two, sub1, sub2, parts, extra):
    states = b.shape[0]
    span, width = data.shape[2:]
    small = jax.ShapeDtypeStruct((states, span), F32)
    args = [b, c, w, rows, data, one, two, sub1, sub2, *parts, *extra]
    sends = 4
    if last:
        out0, spec0 = jax.ShapeDtypeStruct((span, 2 * width), BF16), hbm()
        scratch = [pltpu.VMEM((span, width), BF16), pltpu.SemaphoreType.DMA((sends + 1,))]
    else:
        out0, spec0 = jax.ShapeDtypeStruct((span, width), BF16), whole()
        scratch = []
    return pl.pallas_call(
        functools.partial(inter_kernel, last, head_dim, len(parts), scale_b, scale_c),
        out_shape=[out0, small, small],
        in_specs=[whole() for _ in args],
        out_specs=[spec0, whole(), whole()],
        scratch_shapes=scratch,
        compiler_params=pltpu.CompilerParams(vmem_limit_bytes=16 << 20),
        cost_estimate=pl.CostEstimate(
            flops=width * 2 * span * 256 * 3,
            transcendentals=0,
            bytes_accessed=width * span * 2 * 4,
        ),
        name="inter",
    )(*args)


def local(inputs, out_grad, step_size, log_decay, b_matrix, c_matrix, skip_gain, lengths):
    x, dy = inputs[0], out_grad[0]
    tokens, columns = x.shape
    heads = step_size.shape[1]
    states = b_matrix.shape[1]
    head_dim = columns // heads
    count = lax.axis_size("seq")
    units = count // 2
    if tokens != SPAN or count % 4:
        raise ValueError("unsupported sizes")
    scale_b = 1.0 / math.sqrt(columns)
    scale_c = math.sqrt(states / (columns * count * tokens))
    swap = lambda v: lax.ppermute(v, "seq", [(i, i ^ 1) for i in range(count)])

    def hop(v, s):
        back = units - 1 - s
        pairs = [(2 * s + q, 2 * (s + 1) + q) for q in range(2)]
        pairs += [(2 * back + q, 2 * (back - 1) + q) for q in range(2)]
        return lax.ppermute(v, "seq", pairs)

    fixed = lambda v: pltpu.with_memory_space_constraint(v, pltpu.HBM)
    x, dy = fixed(x), fixed(dy)
    small = [fixed(v) for v in (log_decay[0], step_size[0], b_matrix[0], c_matrix[0])]
    msg1, sub1_other, data, ld, dt, b, c = first_part(lengths, *small, x, dy)
    y1 = swap(msg1)
    data, x2_send, x1, x2, sub2_other, sub1, sub2, d, rows, w, row, col, cb, skip = rest_part(
        lengths, skip_gain, ld, dt, b, c, data, x, dy
    )
    y2 = swap(x2_send)

    received = []
    for s in range(units - 1):
        near = s < units // 2
        args = (y1, d, x1, y1) if near else (y1, d, x2, y2)
        (msg,) = chain(not near, *args, received[-1:], True, False)
        received.append(hop(msg, s))
    early = received[: units // 2 - 1]
    late = received[units // 2 - 1 :]
    own1, send1 = chain(False, y1, d, x1, y1, early, False, True)
    got1 = swap(send1)
    own2, send2 = chain(True, y1, d, x2, y2, late, False, True)
    got2 = swap(send2)

    calls = 3
    pairs = heads // 4 // calls
    mix = None
    parts = {OTHER: [], OWN: []}
    for rel in (OWN, OTHER):
        for k in range(calls):
            part, mix = intra(rel, k * pairs, pairs, head_dim, row, col, cb, skip, data, mix)
            parts[rel].append(part)
    slab, gb, gc = inter(
        False, head_dim, scale_b, scale_c, b, c, w, rows, data, own1, own2, sub1, sub2,
        parts[OWN], [mix],
    )
    out, gb, gc = inter(
        True, head_dim, scale_b, scale_c, b, c, w, rows, data, got1, got2, sub1_other, sub2_other,
        parts[OTHER], [gb, gc, slab],
    )
    return (out[None], gb[None], gc[None])


def solution(mesh):
    placed = (
        P("batch", "seq", None),
        P("batch", "seq", None),
        P("batch", None, "seq"),
        P("batch", None, "seq"),
        P("batch", None, "seq"),
        P("batch", None, "seq"),
        P(),
        P("batch"),
    )
    return jax.shard_map(
        local,
        mesh=mesh,
        in_specs=placed,
        out_specs=(P("batch", "seq", None), P("batch", None, "seq"), P("batch", None, "seq")),
        check_vma=False,
    )
```

time: 315 us -> 38.4 us (0.12)
  waiting for transfers between devices: 153 us -> 8.2 us
  matrix products: 49.4 us -> 0 us
  local copies, waits for them, and re-layouts: 39.1 us -> 0.01 us
  other arithmetic: 31.2 us -> 0 us
  blocking collectives: 24.1 us -> 0 us
  Pallas kernels: 0 us -> 17.5 us
  between operations: 15.5 us -> 1.57 us
  starting transfers between devices: 0.08 us -> 11 us
    all_gather x2 -> x0, waiting for transfers between devices: 153 us -> none  [carried_in(): pieces = jax.tree.map(lambda part: lax.all_gather(part, axis), value)]
    dot_general x20 -> x0, matrix products: 49.4 us -> none  [the longest x3 13 us: one_group(): jnp.einsum('hut,uhp->thp', kernel, dy_heads, preferred_element_type=jnp.f...]
    unnamed x1 -> x0, blocking collectives: 24.1 us -> none
    select_n x15 -> x0, other arithmetic: 23.8 us -> none  [the longest x14 20 us: step(): jnp.where(position < mine, new, old)]
    pallas_call x0 -> x15, Pallas kernels: none -> 17.5 us  [the longest x6 5.88 us: intra(): pl.pallas_call(functools.partial(intra_kernel, rel, pair0, pairs, head_di...]
    ppermute x0 -> x7, starting transfers between devices: none -> 11 us  [the longest x3 6.21 us: hop(): return lax.ppermute(v, 'seq', pairs)]
    dynamic_slice x9 -> x0, local copies, waits for them, and re-layouts: 9.96 us -> none  [the longest x3 5.48 us: one_group(): lax.dynamic_slice_in_dim(inputs, offset * head_dim, group_size * head_dim...]
    unnamed x13 -> x2, local copies, waits for them, and re-layouts: 8.72 us -> 0.01 us
  transfers between devices with their start and end apart: 2 -> 7, of which waited for: 2 -> 3; matrix products, arithmetic and copies ran while one was open for 7% -> 0% of each run, Pallas kernels for 0% -> 32%
where the time goes in v2:
time: 38.4 us; the launch traced here: 38.3 us
  Pallas kernels  17.5 us (46%)
  starting transfers between devices  11 us (29%)
  waiting for transfers between devices  8.2 us (21%)
  between operations  1.57 us (4%)
    ppermute x3, starting transfers between devices, hop(): return lax.ppermute(v, 'seq', pairs)  6.21 us
    pallas_call x6, Pallas kernels, intra(): pl.pallas_call(functools.partial(intra_kernel, rel, pair0, pairs, head_di...  5.88 us
    ppermute x3, waiting for transfers between devices, hop(): return lax.ppermute(v, 'seq', pairs)  5.61 us
    ppermute x4, starting transfers between devices, local(): swap = lambda v: lax.ppermute(v, 'seq', [(i, i ^ 1) for i in range(count)])  4.83 us
    pallas_call x1, Pallas kernels, rest_part(): pl.pallas_call(functools.partial(rest_kernel, columns // heads), out_shap...  4.48 us
    pallas_call x2, Pallas kernels, inter(): pl.pallas_call(functools.partial(inter_kernel, last, head_dim, len(parts)...  4.29 us
    ppermute x4, waiting for transfers between devices, local(): swap = lambda v: lax.ppermute(v, 'seq', [(i, i ^ 1) for i in range(count)])  2.58 us
    pallas_call x1, Pallas kernels, first_part(): pl.pallas_call(functools.partial(first_kernel, columns // heads), out_sha...  2.48 us
  transfers between devices with their start and end apart: 7, of which 3 were waited for; matrix products, arithmetic and copies ran while one was open for 0% of the time, Pallas kernels for 32%

profile of v2, /device:TPU:0, one launch (start us, length us, event | category | flops | bytes accessed | tf_op | source)
XLA Modules:
  0.0 38.3 jit_solution(7941164325723926961)
XLA Ops:
  1.3 0.0 copy-start
  1.3 2.5 %first.1 = (bf16[27,16,128]{2,1,0:T(8,128)(2,1)S(1)}, f32[24,16,128]{2,1,0:T(8,128)S(1)}, bf16[2,2,256,3072]{3,2,1,0:T(8,128)(2,1)S(1)}, f32[96,256]{1,0:T(8,128...) custom-call(s32[1]{0:T(128)S(6)} %copy.13.len_ref, f32[96,256]{1,0:T(8,128)} %bitcast.13, ...), custom_call_target="tpu_custom_call" | custom-call | tf_op jit(solution)/shard_map/first/pallas_call | solution.py:202
  3.8 3.0 %collective-permute-start = (bf16[27,16,128]{2,1,0:T(8,128)(2,1)S(1)}, bf16[27,16,128]{2,1,0:T(8,128)(2,1)S(1)}, u32[]{:S(2)}, u32[]{:S(2)}) collective-permute-start(bf16[27,16,128]{2,1,0:T(8,128)(2,1)S(1)} %get-tuple-element.54), channel_id=1, source_target_pairs={{0,4},{4,0},{8,12},{12,8},{16,20},{20,16},{24,28},{28,24},{1,5},{5... | collective-permute-start | bytes 331784 | tf_op jit(solution)/shard_map/ppermute | solution.py:554
  6.8 0.0 copy-done
  6.8 4.5 %rest.1 = (bf16[2,2,256,3072]{3,2,1,0:T(8,128)(2,1)S(1)}, bf16[24,16,128]{2,1,0:T(8,128)(2,1)S(1)}, f32[24,16,128]{2,1,0:T(8,128)S(1)}, f32[24,16,128]{2,1,0:T(8...) custom-call(s32[1]{0:T(128)S(6)} %copy.13.len_ref, ...), custom_call_target="tpu_custom_call", output_to_operand_aliasing={{0}: (6, {})} | custom-call | tf_op jit(solution)/shard_map/rest/pallas_call | solution.py:292
  11.3 0.0 collective-permute-done.refs_0_.refs_3_
  11.3 0.1 chain.5
  11.4 4.1 %collective-permute-start.1 = (bf16[24,16,128]{2,1,0:T(8,128)(2,1)S(1)}, bf16[24,16,128]{2,1,0:T(8,128)(2,1)S(1)}, u32[]{:S(2)}, u32[]{:S(2)}) collective-permute-start(bf16[24,16,128]{2,1,0:T(8,128)(2,1)S(1)} %chain.5), channel_id=1, source_target_pairs={{0,8},{4,12},{24,16},{28,20},{1,9},{5,13},{25,17},{29,21},{2,10},{... | collective-permute-start | bytes 294920 | tf_op jit(solution)/shard_map/ppermute | solution.py:560
  15.5 0.6 %collective-permute-start.3 = (bf16[24,16,128]{2,1,0:T(8,128)(2,1)S(1)}, bf16[24,16,128]{2,1,0:T(8,128)(2,1)S(1)}, u32[]{:S(2)}, u32[]{:S(2)}) collective-permute-start(bf16[24,16,128]{2,1,0:T(8,128)(2,1)S(1)} %get-tuple-element.59), channel_id=1, source_target_pairs={{0,4},{4,0},{8,12},{12,8},{16,20},{20,16},{24,28},{28,24},{1,5},{5... | collective-permute-start | bytes 294920 | tf_op jit(solution)/shard_map/ppermute | solution.py:554
  16.1 1.6 %collective-permute-done.1.refs_4_ = bf16[24,16,128]{2,1,0:T(8,128)(2,1)S(1)} collective-permute-done((bf16[24,16,128]{2,1,0:T(8,128)(2,1)S(1)}, bf16[24,16,128]{2,1,0:T(8,128)(2,1)S(1)}, u32[]{:S(2)}, u32[]{:S(2)}) %collective-permute-start.1) | collective-permute-done | bytes 98336 | tf_op jit(solution)/shard_map/ppermute | solution.py:560
  17.7 0.1 chain.7
  17.7 0.7 %collective-permute-start.4 = (bf16[24,16,128]{2,1,0:T(8,128)(2,1)S(1)}, bf16[24,16,128]{2,1,0:T(8,128)(2,1)S(1)}, u32[]{:S(2)}, u32[]{:S(2)}) collective-permute-start(bf16[24,16,128]{2,1,0:T(8,128)(2,1)S(1)} %chain.7), channel_id=1, source_target_pairs={{8,16},{12,20},{16,8},{20,12},{9,17},{13,21},{17,9},{21,13},{10,18... | collective-permute-start | bytes 294920 | tf_op jit(solution)/shard_map/ppermute | solution.py:560
  18.4 1.0 %intra.6 = (bf16[256,1024]{1,0:T(8,128)(2,1)S(1)}, f32[2,128,128]{2,1,0:T(8,128)S(1)}) custom-call(f32[2,48,256]{2,1,0:T(8,128)S(1)} %get-tuple-element.63.row_ref, f32[2,256,48]{2,1,0:T(8,128)S(1)} %get-tuple-element.64.col_ref, f32[2,128,128]{2,1,0:T(8,128)S(1)} %get-tuple-element.65.cb_ref, f32[2,24,128]{2,1,0:T(8,128)S(1)} %get-tuple-element.66.skip_ref, ...), custom_call_target="tpu_custom_call" | custom-call | flops 268435456 | bytes 1572864 | tf_op jit(solution)/shard_map/intra/pallas_call | solution.py:400
  19.4 1.0 %intra.7 = (bf16[256,1024]{1,0:T(8,128)(2,1)S(1)}, f32[2,128,128]{2,1,0:T(8,128)S(1)}) custom-call(f32[2,48,256]{2,1,0:T(8,128)S(1)} %get-tuple-element.63.row_ref, f32[2,256,48]{2,1,0:T(8,128)S(1)} %get-tuple-element.64.col_ref, f32[2,128,128]{2,1,0:T(8,128)S(1)} %get-tuple-element.65.cb_ref, f32[2,24,128]{2,1,0:T(8,128)S(1)} %get-tuple-element.66.skip_ref, ...), custom_call_target="tpu_custom_call" | custom-call | flops 268435456 | bytes 1572864 | tf_op jit(solution)/shard_map/intra/pallas_call | solution.py:400
  20.4 0.0 collective-permute-done.3.refs_3_
  20.4 0.0 collective-permute-done.4.refs_4_
  20.4 0.1 chain.8
  20.5 1.5 %collective-permute-start.5 = (bf16[24,16,128]{2,1,0:T(8,128)(2,1)S(1)}, bf16[24,16,128]{2,1,0:T(8,128)(2,1)S(1)}, u32[]{:S(2)}, u32[]{:S(2)}) collective-permute-start(bf16[24,16,128]{2,1,0:T(8,128)(2,1)S(1)} %chain.8), channel_id=1, source_target_pairs={{16,24},{20,28},{8,0},{12,4},{17,25},{21,29},{9,1},{13,5},{18,26},... | collective-permute-start | bytes 294920 | tf_op jit(solution)/shard_map/ppermute | solution.py:560
  22.0 1.0 %intra.8 = (bf16[256,1024]{1,0:T(8,128)(2,1)S(1)}, f32[2,128,128]{2,1,0:T(8,128)S(1)}) custom-call(f32[2,48,256]{2,1,0:T(8,128)S(1)} %get-tuple-element.63.row_ref, f32[2,256,48]{2,1,0:T(8,128)S(1)} %get-tuple-element.64.col_ref, f32[2,128,128]{2,1,0:T(8,128)S(1)} %get-tuple-element.65.cb_ref, f32[2,24,128]{2,1,0:T(8,128)S(1)} %get-tuple-element.66.skip_ref, ...), custom_call_target="tpu_custom_call" | custom-call | flops 268435456 | bytes 1572864 | tf_op jit(solution)/shard_map/intra/pallas_call | solution.py:400
  23.0 1.0 %intra.9 = (bf16[256,1024]{1,0:T(8,128)(2,1)S(1)}, f32[2,128,128]{2,1,0:T(8,128)S(1)}) custom-call(f32[2,48,256]{2,1,0:T(8,128)S(1)} %get-tuple-element.63.row_ref, f32[2,256,48]{2,1,0:T(8,128)S(1)} %get-tuple-element.64.col_ref, f32[2,128,128]{2,1,0:T(8,128)S(1)} %get-tuple-element.65.cb_ref, f32[2,24,128]{2,1,0:T(8,128)S(1)} %get-tuple-element.66.skip_ref, ...), custom_call_target="tpu_custom_call" | custom-call | flops 268435456 | bytes 1572864 | tf_op jit(solution)/shard_map/intra/pallas_call | solution.py:400
  23.9 1.0 %intra.10 = (bf16[256,1024]{1,0:T(8,128)(2,1)S(1)}, f32[2,128,128]{2,1,0:T(8,128)S(1)}) custom-call(f32[2,48,256]{2,1,0:T(8,128)S(1)} %get-tuple-element.63.row_ref, f32[2,256,48]{2,1,0:T(8,128)S(1)} %get-tuple-element.64.col_ref, f32[2,128,128]{2,1,0:T(8,128)S(1)} %get-tuple-element.65.cb_ref, f32[2,24,128]{2,1,0:T(8,128)S(1)} %get-tuple-element.66.skip_ref, ...), custom_call_target="tpu_custom_call" | custom-call | flops 268435456 | bytes 1572864 | tf_op jit(solution)/shard_map/intra/pallas_call | solution.py:400
  24.9 1.0 %intra.11 = (bf16[256,1024]{1,0:T(8,128)(2,1)S(1)}, f32[2,128,128]{2,1,0:T(8,128)S(1)}) custom-call(f32[2,48,256]{2,1,0:T(8,128)S(1)} %get-tuple-element.63.row_ref, f32[2,256,48]{2,1,0:T(8,128)S(1)} %get-tuple-element.64.col_ref, f32[2,128,128]{2,1,0:T(8,128)S(1)} %get-tuple-element.65.cb_ref, f32[2,24,128]{2,1,0:T(8,128)S(1)} %get-tuple-element.66.skip_ref, ...), custom_call_target="tpu_custom_call" | custom-call | flops 268435456 | bytes 1572864 | tf_op jit(solution)/shard_map/intra/pallas_call | solution.py:400
  25.9 0.1 chain.6
  26.0 0.6 %collective-permute-start.2 = (bf16[24,16,128]{2,1,0:T(8,128)(2,1)S(1)}, bf16[24,16,128]{2,1,0:T(8,128)(2,1)S(1)}, u32[]{:S(2)}, u32[]{:S(2)}) collective-permute-start(bf16[24,16,128]{2,1,0:T(8,128)(2,1)S(1)} %get-tuple-element.57), channel_id=1, source_target_pairs={{0,4},{4,0},{8,12},{12,8},{16,20},{20,16},{24,28},{28,24},{1,5},{5... | collective-permute-start | bytes 294920 | tf_op jit(solution)/shard_map/ppermute | solution.py:554
  26.6 4.0 %collective-permute-done.5.refs_5_ = bf16[24,16,128]{2,1,0:T(8,128)(2,1)S(1)} collective-permute-done((bf16[24,16,128]{2,1,0:T(8,128)(2,1)S(1)}, bf16[24,16,128]{2,1,0:T(8,128)(2,1)S(1)}, u32[]{:S(2)}, u32[]{:S(2)}) %collective-permute-start.5) | collective-permute-done | bytes 98336 | tf_op jit(solution)/shard_map/ppermute | solution.py:560
  30.6 0.1 chain.9
  30.7 0.6 %collective-permute-start.6 = (bf16[24,16,128]{2,1,0:T(8,128)(2,1)S(1)}, bf16[24,16,128]{2,1,0:T(8,128)(2,1)S(1)}, u32[]{:S(2)}, u32[]{:S(2)}) collective-permute-start(bf16[24,16,128]{2,1,0:T(8,128)(2,1)S(1)} %get-tuple-element.60), channel_id=1, source_target_pairs={{0,4},{4,0},{8,12},{12,8},{16,20},{20,16},{24,28},{28,24},{1,5},{5... | collective-permute-start | bytes 294920 | tf_op jit(solution)/shard_map/ppermute | solution.py:554
  31.3 1.5 %inter.2 = (bf16[256,3072]{1,0:T(8,128)(2,1)S(1)}, f32[16,256]{1,0:T(8,128)S(1)}, f32[16,256]{1,0:T(8,128)S(1)}) custom-call(bf16[16,256]{1,0:T(8,128)(2,1)S(1)} %get-tuple-element.46.b_ref, bf16[16,256]{1,0:T(8,128)(2,1)S(1)} %get-tuple-element.47.c_ref, f32[2,2,48,256]{3,2,1,0:T(8,128)S(1)} %get-tuple-element.51.w_ref, ...), custom_call_target="tpu_custom_call" | custom-call | flops 1207959552 | bytes 6291456 | tf_op jit(solution)/shard_map/inter/pallas_call | solution.py:526
  32.8 0.0 collective-permute-done.2.one_ref
  32.8 2.6 %collective-permute-done.6.two_ref = bf16[24,16,128]{2,1,0:T(8,128)(2,1)S(1)} collective-permute-done((bf16[24,16,128]{2,1,0:T(8,128)(2,1)S(1)}, bf16[24,16,128]{2,1,0:T(8,128)(2,1)S(1)}, u32[]{:S(2)}, u32[]{:S(2)}) %collective-permute-start.6) | collective-permute-done | bytes 98336 | tf_op jit(solution)/shard_map/ppermute | solution.py:554
  35.4 2.8 %inter.3 = (bf16[256,6144]{1,0:T(8,128)(2,1)}, f32[16,256]{1,0:T(8,128)}, f32[16,256]{1,0:T(8,128)}) custom-call(bf16[16,256]{1,0:T(8,128)(2,1)S(1)} %get-tuple-element.46.b_ref, bf16[16,256]{1,0:T(8,128)(2,1)S(1)} %get-tuple-element.47.c_ref, f32[2,2,48,256]{3,2,1,0:T(8,128)S(1)} %get-tuple-element.51.w_ref, ...), custom_call_target="tpu_custom_call" | custom-call | flops 1207959552 | bytes 6291456 | tf_op jit(solution)/shard_map/inter/pallas_call | solution.py:526
Async XLA Ops:
  1.3 5.5 %copy-start = (f32[96]{0:T(128)S(1)}, f32[96]{0:T(128)}, u32[]{:S(2)}) copy-start(f32[96]{0:T(128)} %skip_ref.1) | copy-start | bytes 1156
  3.8 7.5 %collective-permute-start = (bf16[27,16,128]{2,1,0:T(8,128)(2,1)S(1)}, bf16[27,16,128]{2,1,0:T(8,128)(2,1)S(1)}, u32[]{:S(2)}, u32[]{:S(2)}) collective-permute-start(bf16[27,16,128]{2,1,0:T(8,128)(2,1)S(1)} %get-tuple-element.54), channel_id=1, source_target_pairs={{0,4},{4,0},{8,12},{12,8},{16,20},{20,16},{24,28},{28,24},{1,5},{5... | collective-permute-start | bytes 331784 | tf_op jit(solution)/shard_map/ppermute | solution.py:554
  11.4 6.3 %collective-permute-start.1 = (bf16[24,16,128]{2,1,0:T(8,128)(2,1)S(1)}, bf16[24,16,128]{2,1,0:T(8,128)(2,1)S(1)}, u32[]{:S(2)}, u32[]{:S(2)}) collective-permute-start(bf16[24,16,128]{2,1,0:T(8,128)(2,1)S(1)} %chain.5), channel_id=1, source_target_pairs={{0,8},{4,12},{24,16},{28,20},{1,9},{5,13},{25,17},{29,21},{2,10},{... | collective-permute-start | bytes 294920 | tf_op jit(solution)/shard_map/ppermute | solution.py:560
  15.5 4.9 %collective-permute-start.3 = (bf16[24,16,128]{2,1,0:T(8,128)(2,1)S(1)}, bf16[24,16,128]{2,1,0:T(8,128)(2,1)S(1)}, u32[]{:S(2)}, u32[]{:S(2)}) collective-permute-start(bf16[24,16,128]{2,1,0:T(8,128)(2,1)S(1)} %get-tuple-element.59), channel_id=1, source_target_pairs={{0,4},{4,0},{8,12},{12,8},{16,20},{20,16},{24,28},{28,24},{1,5},{5... | collective-permute-start | bytes 294920 | tf_op jit(solution)/shard_map/ppermute | solution.py:554
  17.7 2.6 %collective-permute-start.4 = (bf16[24,16,128]{2,1,0:T(8,128)(2,1)S(1)}, bf16[24,16,128]{2,1,0:T(8,128)(2,1)S(1)}, u32[]{:S(2)}, u32[]{:S(2)}) collective-permute-start(bf16[24,16,128]{2,1,0:T(8,128)(2,1)S(1)} %chain.7), channel_id=1, source_target_pairs={{8,16},{12,20},{16,8},{20,12},{9,17},{13,21},{17,9},{21,13},{10,18... | collective-permute-start | bytes 294920 | tf_op jit(solution)/shard_map/ppermute | solution.py:560
  20.5 10.1 %collective-permute-start.5 = (bf16[24,16,128]{2,1,0:T(8,128)(2,1)S(1)}, bf16[24,16,128]{2,1,0:T(8,128)(2,1)S(1)}, u32[]{:S(2)}, u32[]{:S(2)}) collective-permute-start(bf16[24,16,128]{2,1,0:T(8,128)(2,1)S(1)} %chain.8), channel_id=1, source_target_pairs={{16,24},{20,28},{8,0},{12,4},{17,25},{21,29},{9,1},{13,5},{18,26},... | collective-permute-start | bytes 294920 | tf_op jit(solution)/shard_map/ppermute | solution.py:560
  26.0 6.8 %collective-permute-start.2 = (bf16[24,16,128]{2,1,0:T(8,128)(2,1)S(1)}, bf16[24,16,128]{2,1,0:T(8,128)(2,1)S(1)}, u32[]{:S(2)}, u32[]{:S(2)}) collective-permute-start(bf16[24,16,128]{2,1,0:T(8,128)(2,1)S(1)} %get-tuple-element.57), channel_id=1, source_target_pairs={{0,4},{4,0},{8,12},{12,8},{16,20},{20,16},{24,28},{28,24},{1,5},{5... | collective-permute-start | bytes 294920 | tf_op jit(solution)/shard_map/ppermute | solution.py:554
  30.7 4.7 %collective-permute-start.6 = (bf16[24,16,128]{2,1,0:T(8,128)(2,1)S(1)}, bf16[24,16,128]{2,1,0:T(8,128)(2,1)S(1)}, u32[]{:S(2)}, u32[]{:S(2)}) collective-permute-start(bf16[24,16,128]{2,1,0:T(8,128)(2,1)S(1)} %get-tuple-element.60), channel_id=1, source_target_pairs={{0,4},{4,0},{8,12},{12,8},{16,20},{20,16},{24,28},{28,24},{1,5},{5... | collective-permute-start | bytes 294920 | tf_op jit(solution)/shard_map/ppermute | solution.py:554

commit v3 on v2

--- a/solution.py
+++ b/solution.py
@@ -119,15 +119,9 @@
     per = SLAB // head_dim
     low = iota((states, LANES), 1) < head_dim
     for i in range(chunks):
-        wait(t, i)
-
-        @pl.when(jnp.logical_and(kind == 1, valid < span))
-        def _():
-            cols = pl.ds(i * chunk, chunk)
-            inside = iota((span, chunk), 0) < valid
-            data = data_ref[rel, 1, :, cols].astype(F32)
-            data_ref[rel, 1, :, cols] = jnp.where(inside, data, 0.0).astype(BF16)
-
+        if wait is not None:
+            wait(t, i)
+            mask_rows(rel, kind, valid, pl.ds(i * chunk, chunk), data_ref)
         for g in range(i * chunk // SLAB, (i + 1) * chunk // SLAB):
             lhs = jnp.concatenate(
                 [(mat * w_ref[pl.ds(per * g + j, 1), :]).astype(BF16) for j in range(per)],
@@ -155,10 +149,12 @@
 
 def first_kernel(
     head_dim, len_ref, ld_hbm, dt_hbm, b_hbm, c_hbm, x_ref, dy_ref,
-    msg_ref, sub_ref, data_ref, ld_ref, dt_ref, b_ref, c_ref, w_ref, rows_ref, spread_ref, sems, small_sems
+    msg_ref, sub1_ref, sub2_ref, data_ref, ld_ref, dt_ref, b_ref, c_ref, w_ref, rows_ref, row_ref,
+    task_w_ref, spread_ref, sems, small_sems
 ):
     idx, mine, lower = place()
-    kind = jnp.where(lower, 0, 1)
+    kind1 = jnp.where(lower, 0, 1)
+    kinds = (kind1, 1 - kind1)
     span = ld_ref.shape[1]
     half_heads = ld_ref.shape[0] // 2
     small = [
@@ -169,26 +165,29 @@
     ]
     for copy in small:
         copy.start()
-    wait = load_tasks(((True, False),), (kind,), mine, x_ref, dy_ref, data_ref, sems)
+    wait = load_tasks(((True, False), (False, False)), kinds, mine, x_ref, dy_ref, data_ref, sems)
     for copy in small:
         copy.wait()
     rows = pl.ds(pl.multiple_of((1 - mine) * half_heads, 8), half_heads)
     cum, ws, wg, d_a, d_b = weights(ld_ref[rows, :], dt_ref[rows, :])
-    w_ref[...] = jnp.where(kind == 0, ws, wg)
+    w_ref[0] = ws
+    w_ref[1] = wg
+    row_ref[...] = cum * LOG2E
     rows_a = spread(d_a, spread_ref, head_dim)
     rows_b = spread(d_b, spread_ref, head_dim)
     rows_ref[0] = rows_a
     rows_ref[1] = rows_b
-    both = rows_a * rows_b
-    high = both.astype(BF16).astype(F32)
-    tiles = sub_ref.shape[0]
-    extra = jnp.concatenate([high, both - high], axis=0).astype(BF16)
-    msg_ref[tiles:] = extra.reshape((msg_ref.shape[0] - tiles,) + msg_ref.shape[1:])
+    tiles = sub1_ref.shape[0]
+    extra = narrow_rows(rows_a * rows_b)
+    msg_ref[2 * tiles :] = extra.reshape((msg_ref.shape[0] - 2 * tiles,) + msg_ref.shape[1:])
     valid = len_ref[0] - idx * span
-    run_task(
-        0, kind, OTHER, valid, wait, sems.shape[1], head_dim,
-        b_ref[...].astype(F32), c_ref[...].astype(F32), w_ref, rows_ref, data_ref, msg_ref, sub_ref,
-    )
+    b, c = b_ref[...].astype(F32), c_ref[...].astype(F32)
+    for t, sub_ref in enumerate((sub1_ref, sub2_ref)):
+        task_w_ref[t] = jnp.where(kinds[t] == 0, ws, wg)
+        run_task(
+            t, kinds[t], OTHER, valid, wait, sems.shape[1], head_dim, b, c, task_w_ref.at[t],
+            rows_ref, data_ref, msg_ref.at[pl.ds(t * tiles, tiles)], sub_ref,
+        )
 
 
 def first_part(length, ld, dt, b, c, x, dy):
@@ -197,23 +196,25 @@
     states = b.shape[0]
     tiles = columns // 2 // LANES
     pairs = heads // 4
-    tile = lambda n, t: jax.ShapeDtypeStruct((n, states, LANES), t)
-    same = lambda a: jax.ShapeDtypeStruct(a.shape, a.dtype)
+    shape = jax.ShapeDtypeStruct
+    tile = lambda n, t: shape((n, states, LANES), t)
+    same = lambda a: shape(a.shape, a.dtype)
+    outs = [
+        tile(2 * tiles + 2 * pairs // states, BF16),
+        tile(tiles, F32),
+        tile(tiles, F32),
+        shape((2, 2, span, columns // 2), BF16),
+        same(ld), same(dt), same(b), same(c),
+    ] + table_shapes(heads, span)[:3]
     return pl.pallas_call(
         functools.partial(first_kernel, columns // heads),
-        out_shape=[
-            tile(tiles + 2 * pairs // states, BF16),
-            tile(tiles, F32),
-            jax.ShapeDtypeStruct((2, 2, span, columns // 2), BF16),
-            same(ld), same(dt), same(b), same(c),
-        ],
+        out_shape=outs,
         in_specs=[smem()] + [hbm() for _ in range(6)],
-        out_specs=[whole() for _ in range(7)],
+        out_specs=[whole() for _ in outs],
         scratch_shapes=[
-            pltpu.VMEM((heads // 2, span), F32),
-            pltpu.VMEM((2, pairs, LANES), F32),
+            pltpu.VMEM((2, heads // 2, span), F32),
             pltpu.VMEM((heads // 2, LANES), F32),
-            pltpu.SemaphoreType.DMA((1, 4)),
+            pltpu.SemaphoreType.DMA((2, 4)),
             pltpu.SemaphoreType.DMA((4,)),
         ],
         compiler_params=pltpu.CompilerParams(vmem_limit_bytes=12 << 20),
@@ -221,88 +222,101 @@
     )(length, ld, dt, b, c, x, dy)
 
 
-def rest_kernel(
-    head_dim, len_ref, skip_ref, ld_ref, dt_ref, b_ref, c_ref, data_in, x_ref, dy_ref,
-    data_ref, send_ref, x1_ref, x2_ref, sub_other_ref, sub1_ref, sub2_ref, d_ref, rows_ref,
-    w_ref, row_ref, col_ref, cb_ref, skip_rows_ref, task_w_ref, spread_ref, sems
+def mask_rows(rel, kind, valid, cols, data_ref):
+    span = data_ref.shape[2]
+
+    @pl.when(jnp.logical_and(kind == 1, valid < span))
+    def _():
+        inside = iota((span, cols.size), 0) < valid
+        data = data_ref[rel, 1, :, cols].astype(F32)
+        data_ref[rel, 1, :, cols] = jnp.where(inside, data, 0.0).astype(BF16)
+
+
+def more_tables(half, head_dim, row, dt_ref, skip_ref, col_ref, skip_rows_ref):
+    half_heads = row.shape[0]
+    low = iota((1, LANES), 1) < head_dim
+    rows = pl.ds(pl.multiple_of(half * half_heads, 8), half_heads)
+    col_ref[...] = (row - jnp.log(dt_ref[rows, :]) * LOG2E).T
+    for j in range(half_heads // 2):
+        at = half * half_heads + 2 * j
+        skip_rows_ref[pl.ds(j, 1), :] = jnp.where(low, skip_ref[at], skip_ref[at + 1])
+
+
+def own_kernel(
+    head_dim, len_ref, skip_ref, ld_ref, dt_ref, b_ref, c_ref, rowo_ref, data_in, x_ref, dy_ref,
+    data_ref, x1_ref, sub1_ref, x2_ref, sub2_ref, d_ref, cb_ref,
+    w_ref, rows_ref, row_ref, col_ref, skip_rows_ref, colo_ref, skipo_ref,
+    task_w_ref, spread_ref, sems
 ):
     idx, mine, lower = place()
     kind1 = jnp.where(lower, 0, 1)
-    kind2 = 1 - kind1
-    heads, span = ld_ref.shape
-    half_heads = heads // 2
-    pairs = half_heads // 2
+    kinds = (kind1, 1 - kind1)
+    span = ld_ref.shape[1]
+    half_heads = ld_ref.shape[0] // 2
     sub = span // 2
-    tasks = ((True, True), (False, True), (False, False))
-    kinds = (kind1, kind2, kind2)
-    wait = load_tasks(tasks, kinds, mine, x_ref, dy_ref, data_ref, sems)
-    low = iota((1, LANES), 1) < head_dim
-    for rel in (OTHER, OWN):
-        half = mine if rel == OWN else 1 - mine
-        rows = pl.ds(pl.multiple_of(half * half_heads, 8), half_heads)
-        dt = dt_ref[rows, :]
-        cum, ws, wg, d_a, d_b = weights(ld_ref[rows, :], dt)
-        w_ref[rel, 0] = ws
-        w_ref[rel, 1] = wg
-        rows_ref[rel, 0] = spread(d_a, spread_ref, head_dim)
-        rows_ref[rel, 1] = spread(d_b, spread_ref, head_dim)
-        row = cum * LOG2E
-        row_ref[rel] = row
-        col_ref[rel] = (row - jnp.log(dt) * LOG2E).T
-        for j in range(pairs):
-            at = half * half_heads + 2 * j
-            skip_rows_ref[rel, pl.ds(j, 1), :] = jnp.where(low, skip_ref[at], skip_ref[at + 1])
-    d_ref[...] = rows_ref[OWN, 0] * rows_ref[OWN, 1]
+    valid = len_ref[0] - idx * span
+    wait = load_tasks(((True, True), (False, True)), kinds, mine, x_ref, dy_ref, data_ref, sems)
+    rows = pl.ds(pl.multiple_of(mine * half_heads, 8), half_heads)
+    cum, ws, wg, d_a, d_b = weights(ld_ref[rows, :], dt_ref[rows, :])
+    w_ref[0] = ws
+    w_ref[1] = wg
+    rows_ref[0] = spread(d_a, spread_ref, head_dim)
+    rows_ref[1] = spread(d_b, spread_ref, head_dim)
+    row = cum * LOG2E
+    row_ref[...] = row
+    d_ref[...] = rows_ref[0] * rows_ref[1]
+    more_tables(mine, head_dim, row, dt_ref, skip_ref, col_ref, skip_rows_ref)
+    more_tables(1 - mine, head_dim, rowo_ref[...], dt_ref, skip_ref, colo_ref, skipo_ref)
     for s in range(2):
         cols = slice(s * sub, (s + 1) * sub)
         dots = mm(b_ref[:, cols], c_ref[:, cols], TN)
         cb_ref[s] = jnp.where(iota(dots.shape, 1) >= iota(dots.shape, 0), dots, 0.0)
     b, c = b_ref[...].astype(F32), c_ref[...].astype(F32)
-    valid = len_ref[0] - idx * span
-    outs = ((x1_ref, sub1_ref), (x2_ref, sub2_ref), (send_ref, sub_other_ref))
-    for t, (first, own) in enumerate(tasks):
-        rel = OWN if own else OTHER
-        task_w_ref[t] = jnp.where(kinds[t] == 0, w_ref[rel, 0], w_ref[rel, 1])
+    for t, (total_ref, sub_ref) in enumerate(((x1_ref, sub1_ref), (x2_ref, sub2_ref))):
+        task_w_ref[t] = jnp.where(kinds[t] == 0, ws, wg)
         run_task(
-            t, kinds[t], rel, valid, wait, sems.shape[1], head_dim, b, c,
-            task_w_ref.at[t], rows_ref.at[rel], data_ref, outs[t][0], outs[t][1],
-        )
-
-
-def rest_part(length, skip, ld, dt, b, c, data, x, dy):
+            t, kinds[t], OWN, valid, wait, sems.shape[1], head_dim, b, c, task_w_ref.at[t],
+            rows_ref, data_ref, total_ref, sub_ref,
+        )
+
+
+def table_shapes(heads, span):
+    shape = jax.ShapeDtypeStruct
+    half, pairs = heads // 2, heads // 4
+    return [
+        shape((2, half, span), F32),
+        shape((2, pairs, LANES), F32),
+        shape((half, span), F32),
+        shape((span, half), F32),
+        shape((pairs, LANES), F32),
+    ]
+
+
+def own_part(length, skip, ld, dt, b, c, row_other, data, x, dy):
     heads, span = ld.shape
     columns = x.shape[1]
     states = b.shape[0]
-    tiles = columns // 2 // LANES
     pairs = heads // 4
     sub = span // 2
     shape = jax.ShapeDtypeStruct
-    tile = lambda t: shape((tiles, states, LANES), t)
-    outs = [
-        shape(data.shape, BF16),
-        tile(BF16), tile(F32), tile(F32), tile(F32), tile(F32), tile(F32),
-        shape((pairs, LANES), F32),
-        shape((2, 2, pairs, LANES), F32),
-        shape((2, 2, heads // 2, span), F32),
-        shape((2, heads // 2, span), F32),
-        shape((2, span, heads // 2), F32),
-        shape((2, sub, sub), F32),
-        shape((2, pairs, LANES), F32),
-    ]
+    tile = shape((columns // 2 // LANES, states, LANES), F32)
+    outs = [shape(data.shape, BF16), tile, tile, tile, tile, shape((pairs, LANES), F32)]
+    outs += [shape((2, sub, sub), F32)]
+    outs += table_shapes(heads, span) + table_shapes(heads, span)[3:]
     return pl.pallas_call(
-        functools.partial(rest_kernel, columns // heads),
+        functools.partial(own_kernel, columns // heads),
         out_shape=outs,
-        in_specs=[smem(), smem()] + [whole() for _ in range(5)] + [hbm(), hbm()],
+        in_specs=[smem(), smem()] + [whole() for _ in range(6)] + [hbm(), hbm()],
         out_specs=[whole() for _ in outs],
         scratch_shapes=[
-            pltpu.VMEM((3, heads // 2, span), F32),
+            pltpu.VMEM((2, heads // 2, span), F32),
             pltpu.VMEM((heads // 2, LANES), F32),
-            pltpu.SemaphoreType.DMA((3, 4)),
+            pltpu.SemaphoreType.DMA((2, 4)),
         ],
-        input_output_aliases={6: 0},
-        compiler_params=pltpu.CompilerParams(vmem_limit_bytes=16 << 20),
-        name="rest",
-    )(length, skip, ld, dt, b, c, data, x, dy)
+        input_output_aliases={7: 0},
+        compiler_params=pltpu.CompilerParams(vmem_limit_bytes=12 << 20),
+        name="own",
+    )(length, skip, ld, dt, b, c, row_other, data, x, dy)
 
 
 def pair_flags(second):
@@ -311,51 +325,94 @@
     return jnp.logical_not(ahead) if second else ahead
 
 
-def chain_kernel(second, carries, finish, msg, *refs):
-    decay_ref, mine_ref, x_ref, y_ref = refs[:4]
-    carry_refs = refs[4 : 4 + carries]
-    rest = refs[4 + carries :]
-    dp_ref = rest[-1]
+def inner_unit():
+    unit = lax.axis_index("seq") // 2
+    return jnp.logical_or(unit == 1, unit == 2)
+
+
+def wide_rows(ref, tiles):
+    both = ref[tiles:]
+    both = both.reshape(both.shape[0] * both.shape[1], LANES).astype(F32)
+    count = both.shape[0] // 2
+    return both[:count] + both[count:]
+
+
+def narrow_rows(rows):
+    high = rows.astype(BF16).astype(F32)
+    return jnp.concatenate([high, rows - high], axis=0).astype(BF16)
+
+
+def pair_total(ahead, d, dp, x, y):
+    return jnp.where(ahead, dp, d) * jnp.where(ahead, x, y) + jnp.where(ahead, y, x)
+
+
+def hand_on(ahead, d, dp, x, y, carry):
+    passed = jnp.where(ahead, d, dp) * carry + jnp.where(ahead, x, y)
+    return jnp.where(ahead, carry, passed), jnp.where(ahead, passed, carry)
+
+
+def total_kernel(second, mine_ref, x_ref, y_ref, *refs):
+    out_ref, dp_ref = refs[-2:]
     ahead = pair_flags(second)
     tiles = x_ref.shape[0]
-    count = dp_ref.shape[0]
-    both = decay_ref[tiles:].reshape(2 * count, LANES).astype(F32)
-    dp_ref[...] = both[:count] + both[count:]
+    dp_ref[...] = wide_rows(y_ref, 2 * tiles)
+    base = tiles if second else 0
+    if not second:
+        rows = narrow_rows(dp_ref[...] * mine_ref[...])
+        out_ref[tiles:] = rows.reshape((out_ref.shape[0] - tiles,) + out_ref.shape[1:])
     for j in range(tiles):
-        dp = dp_ref[pl.ds(j, 1), :]
-        d = mine_ref[pl.ds(j, 1), :]
-        x = x_ref[j]
-        y = y_ref[j].astype(F32)
-        carry = None
-        for ref in carry_refs:
-            carry = ref[j].astype(F32) if carry is None else carry + ref[j].astype(F32)
-        at = 0
-        if msg:
-            total = jnp.where(ahead, dp, d) * jnp.where(ahead, x, y) + jnp.where(ahead, y, x)
-            if carry is not None:
-                total = total + d * dp * carry
-            rest[at][j] = total.astype(BF16)
-            at += 1
-        if finish:
-            if carry is None:
-                carry = jnp.zeros_like(x)
-            passed = jnp.where(ahead, d, dp) * carry + jnp.where(ahead, x, y)
-            rest[at][j] = jnp.where(ahead, carry, passed).astype(BF16)
-            rest[at + 1][j] = jnp.where(ahead, passed, carry).astype(BF16)
-
-
-def chain(second, decay, mine, x, y, carries, msg, finish):
-    shape = jax.ShapeDtypeStruct(x.shape, BF16)
-    outs = int(msg) + 2 * int(finish)
+        dp, d = dp_ref[pl.ds(j, 1), :], mine_ref[pl.ds(j, 1), :]
+        total = pair_total(ahead, d, dp, x_ref[j], y_ref[base + j].astype(F32))
+        out_ref[j] = total.astype(BF16)
+
+
+def near_kernel(mine_ref, x_ref, y_ref, r_ref, *refs):
+    msg_ref, own_ref, send_ref, dp_ref, pd_ref = refs[-5:]
+    ahead = pair_flags(False)
+    inner = inner_unit()
+    tiles = x_ref.shape[0]
+    dp_ref[...] = wide_rows(y_ref, 2 * tiles)
+    pd_ref[...] = wide_rows(r_ref, tiles)
+    for j in range(tiles):
+        dp, d, pd = dp_ref[pl.ds(j, 1), :], mine_ref[pl.ds(j, 1), :], pd_ref[pl.ds(j, 1), :]
+        x, y, got = x_ref[j], y_ref[j].astype(F32), r_ref[j].astype(F32)
+        total = pair_total(ahead, d, dp, x, y)
+        joined = jnp.where(inner, d * dp, pd) * jnp.where(inner, got, total) + jnp.where(
+            inner, total, got
+        )
+        msg_ref[j] = joined.astype(BF16)
+        own, send = hand_on(ahead, d, dp, x, y, jnp.where(inner, got, 0.0))
+        own_ref[j] = own.astype(BF16)
+        send_ref[j] = send.astype(BF16)
+
+
+def far_kernel(mine_ref, x_ref, y_ref, r_ref, r2_ref, far_ref, *refs):
+    own_ref, send_ref, dp_ref, pd_ref = refs[-4:]
+    ahead = pair_flags(True)
+    inner = inner_unit()
+    tiles = x_ref.shape[0]
+    dp_ref[...] = wide_rows(y_ref, 2 * tiles)
+    pd_ref[...] = wide_rows(r_ref, tiles)
+    for j in range(tiles):
+        dp, d, pd = dp_ref[pl.ds(j, 1), :], mine_ref[pl.ds(j, 1), :], pd_ref[pl.ds(j, 1), :]
+        x, y = x_ref[j], y_ref[tiles + j].astype(F32)
+        far = far_ref[j].astype(F32)
+        carry = jnp.where(inner, far, r2_ref[j].astype(F32) + pd * far)
+        own, send = hand_on(ahead, d, dp, x, y, carry)
+        own_ref[j] = own.astype(BF16)
+        send_ref[j] = send.astype(BF16)
+
+
+def small_call(kernel, name, outs, rows_shape, scratch, args, after=()):
     return pl.pallas_call(
-        functools.partial(chain_kernel, second, len(carries), finish, msg),
-        out_shape=[shape] * outs,
-        in_specs=[whole() for _ in range(4 + len(carries))],
-        out_specs=[whole() for _ in range(outs)],
-        scratch_shapes=[pltpu.VMEM(mine.shape, F32)],
+        kernel,
+        out_shape=[jax.ShapeDtypeStruct(o, BF16) for o in outs],
+        in_specs=[whole() for _ in args] + [pl.BlockSpec(memory_space=pl.ANY) for _ in after],
+        out_specs=[whole() for _ in outs],
+        scratch_shapes=[pltpu.VMEM(rows_shape, F32)] * scratch,
         compiler_params=pltpu.CompilerParams(vmem_limit_bytes=4 << 20),
-        name="chain",
-    )(decay, mine, x, y, *carries)
+        name=name,
+    )(*args, *after)
 
 
 def intra_kernel(rel, pair0, pairs, head_dim, first, row_ref, col_ref, cb_ref, skip_ref, data_ref, *refs):
@@ -379,21 +436,21 @@
             kernels = []
             for j in range(2):
                 h = 2 * (pair0 + p) + j
-                row = row_ref[rel, pl.ds(h, 1), here]
-                col = col_ref[rel, here, pl.ds(h, 1)]
+                row = row_ref[pl.ds(h, 1), here]
+                col = col_ref[here, pl.ds(h, 1)]
                 decay = jnp.exp2(jnp.minimum(row - col, 100.0))
                 kernels.append((decay * cb_ref[s]).astype(BF16))
                 term = decay * scores[:, j * sub : (j + 1) * sub]
                 acc = term if acc is None else acc + term
             within = mm(jnp.concatenate(kernels, axis=1), split)
-            skip = skip_ref[rel, pl.ds(pair0 + p, 1), :]
+            skip = skip_ref[pl.ds(pair0 + p, 1), :]
             part_ref[here, pl.ds(p * LANES, LANES)] = (
                 within + skip * ys.astype(F32)
             ).astype(part_ref.dtype)
         mix_ref[s] = acc
 
 
-def intra(rel, pair0, pairs, head_dim, row, col, cb, skip, data, mix):
+def intra(rel, pair0, pairs, head_dim, row, col, cb, skip, data, mix, after=()):
     span = data.shape[2]
     args = [row, col, cb, skip, data] + ([] if mix is None else [mix])
     heads = 2 * pairs
@@ -403,7 +460,7 @@
             jax.ShapeDtypeStruct((span, pairs * LANES), BF16),
             jax.ShapeDtypeStruct(cb.shape, F32),
         ],
-        in_specs=[whole() for _ in args],
+        in_specs=[whole() for _ in args] + [pl.BlockSpec(memory_space=pl.ANY) for _ in after],
         out_specs=[whole(), whole()],
         compiler_params=pltpu.CompilerParams(vmem_limit_bytes=16 << 20),
         cost_estimate=pl.CostEstimate(
@@ -412,7 +469,7 @@
             bytes_accessed=heads * head_dim * span * 2 * 3,
         ),
         name="intra",
-    )(*args)
+    )(*args, *after)
 
 
 def inter_kernel(last, head_dim, slabs, scale_b, scale_c, b_ref, c_ref, w_ref, rows_ref, data_ref,
@@ -453,7 +510,7 @@
         grad_sub = jnp.where(lower, sub2, sub1)
         state_sub = jnp.where(lower, sub1, sub2)
         row = lambda k: jnp.concatenate(
-            [rows_ref[rel, k, pl.ds(j, 1), :], rows_ref[rel, k, pl.ds(j + 1, 1), :]], axis=1
+            [rows_ref[k, pl.ds(j, 1), :], rows_ref[k, pl.ds(j + 1, 1), :]], axis=1
         )
         grads = [(grad_sub + row(1) * grad.astype(F32)).astype(BF16), grad]
         states_in = [state, (state_sub + row(0) * state.astype(F32)).astype(BF16)]
@@ -462,8 +519,8 @@
         part_cols = pl.ds(g * SLAB % slab_width, SLAB)
         for s in range(2):
             here = pl.ds(s * sub, sub)
-            rows_s = [w_ref[rel, 0, pl.ds(per * g + i, 1), here] for i in range(per)]
-            rows_g = [w_ref[rel, 1, pl.ds(per * g + i, 1), here] for i in range(per)]
+            rows_s = [w_ref[0, pl.ds(per * g + i, 1), here] for i in range(per)]
+            rows_g = [w_ref[1, pl.ds(per * g + i, 1), here] for i in range(per)]
             grad_diag = jnp.concatenate([grads[s]] * per, axis=0) * diag
             state_diag = jnp.concatenate([states_in[s]] * per, axis=0) * diag
             bs = b[:, s * sub : (s + 1) * sub]
@@ -551,54 +608,95 @@
         raise ValueError("unsupported sizes")
     scale_b = 1.0 / math.sqrt(columns)
     scale_c = math.sqrt(states / (columns * count * tokens))
-    swap = lambda v: lax.ppermute(v, "seq", [(i, i ^ 1) for i in range(count)])
-
-    def hop(v, s):
-        back = units - 1 - s
-        pairs = [(2 * s + q, 2 * (s + 1) + q) for q in range(2)]
-        pairs += [(2 * back + q, 2 * (back - 1) + q) for q in range(2)]
-        return lax.ppermute(v, "seq", pairs)
+    def swap(v, bit):
+        return lax.ppermute(v, "seq", [(i, i ^ bit) for i in range(count)])
 
     fixed = lambda v: pltpu.with_memory_space_constraint(v, pltpu.HBM)
     x, dy = fixed(x), fixed(dy)
     small = [fixed(v) for v in (log_decay[0], step_size[0], b_matrix[0], c_matrix[0])]
-    msg1, sub1_other, data, ld, dt, b, c = first_part(lengths, *small, x, dy)
-    y1 = swap(msg1)
-    data, x2_send, x1, x2, sub2_other, sub1, sub2, d, rows, w, row, col, cb, skip = rest_part(
-        lengths, skip_gain, ld, dt, b, c, data, x, dy
+    msg, sub1_other, sub2_other, data, ld, dt, b, c, *other = first_part(lengths, *small, x, dy)
+    y = swap(msg, 1)
+    data, x1, sub1, x2, sub2, d, cb, *tables = own_part(
+        lengths, skip_gain, ld, dt, b, c, other[2], data, x, dy
     )
-    y2 = swap(x2_send)
-
-    received = []
-    for s in range(units - 1):
-        near = s < units // 2
-        args = (y1, d, x1, y1) if near else (y1, d, x2, y2)
-        (msg,) = chain(not near, *args, received[-1:], True, False)
-        received.append(hop(msg, s))
-    early = received[: units // 2 - 1]
-    late = received[units // 2 - 1 :]
-    own1, send1 = chain(False, y1, d, x1, y1, early, False, True)
-    got1 = swap(send1)
-    own2, send2 = chain(True, y1, d, x2, y2, late, False, True)
-    got2 = swap(send2)
-
+    own, other = tables[:5], other + tables[5:]
     calls = 3
     pairs = heads // 4 // calls
-    mix = None
     parts = {OTHER: [], OWN: []}
-    for rel in (OWN, OTHER):
-        for k in range(calls):
-            part, mix = intra(rel, k * pairs, pairs, head_dim, row, col, cb, skip, data, mix)
-            parts[rel].append(part)
+
+    def block(rel, k, mix, after=()):
+        table = own if rel == OWN else other
+        part, mix = intra(
+            rel, k * pairs, pairs, head_dim, table[2], table[3], cb, table[4], data, mix, after
+        )
+        parts[rel].append(part)
+        return mix
+
+    mix = block(OWN, 0, None)
+    tile = x1.shape
+    if units == 4:
+        (m1,) = small_call(
+            functools.partial(total_kernel, False), "total", [(msg.shape[0] - tile[0],) + tile[1:]], d.shape, 1,
+            [d, x1, y], [mix],
+        )
+        r1 = swap(m1, 2)
+        (m2,) = small_call(
+            functools.partial(total_kernel, True), "total", [tile], d.shape, 1, [d, x2, y], [m1]
+        )
+        r2 = swap(m2, 2)
+        mix = block(OWN, 1, mix, [m2])
+        far, own1, send1 = small_call(near_kernel, "near", [tile] * 3, d.shape, 2, [d, x1, y, r1], [mix])
+        r3 = swap(far, 4)
+        got1 = swap(send1, 1)
+        mix = block(OWN, 2, mix, [far])
+        mix = block(OTHER, 0, mix)
+        mix = block(OTHER, 1, mix)
+        own2, send2 = small_call(
+            far_kernel, "far", [tile] * 2, d.shape, 2, [d, x2, y, r1, r2, r3], [mix]
+        )
+        got2 = swap(send2, 1)
+    else:
+        mix = block(OWN, 1, mix)
+        mix = block(OWN, 2, mix)
+        mix = block(OTHER, 0, mix)
+        mix = block(OTHER, 1, mix)
+        (own1, send1), (own2, send2) = gathered(units, d, x1, x2, y)
+        got1, got2 = swap(send1, 1), swap(send2, 1)
+    mix = block(OTHER, 2, mix, [send2])
+    w, rows = own[:2]
     slab, gb, gc = inter(
         False, head_dim, scale_b, scale_c, b, c, w, rows, data, own1, own2, sub1, sub2,
         parts[OWN], [mix],
     )
     out, gb, gc = inter(
-        True, head_dim, scale_b, scale_c, b, c, w, rows, data, got1, got2, sub1_other, sub2_other,
-        parts[OTHER], [gb, gc, slab],
+        True, head_dim, scale_b, scale_c, b, c, other[0], other[1], data, got1, got2,
+        sub1_other, sub2_other, parts[OTHER], [gb, gc, slab],
     )
     return (out[None], gb[None], gc[None])
+
+
+def gathered(units, d, x1, x2, y):
+    idx = lax.axis_index("seq")
+    mine, unit = idx % 2, idx // 2
+    lower = unit < units // 2
+    tiles = x1.shape[0]
+    dp = wide_rows(y, 2 * tiles)[:, None, :]
+    d = d[:, None, :]
+    ys = (y[:tiles].astype(F32), y[tiles : 2 * tiles].astype(F32))
+    xs = (x1, x2)
+    totals = [pair_total(pair_flags(k == 1), d, dp, xs[k], ys[k]) for k in range(2)]
+    own_half = lambda v: jnp.take(lax.all_gather(v, "seq"), 2 * jnp.arange(units) + mine, axis=0)
+    forward = own_half(jnp.where(lower, totals[0], totals[1]))
+    backward = own_half(jnp.where(lower, totals[1], totals[0]))
+    decays = own_half(d * dp)
+    state = grad = jnp.zeros_like(x1)
+    for u in range(units):
+        state = jnp.where(u < unit, decays[u] * state + forward[u], state)
+        v = units - 1 - u
+        grad = jnp.where(v > unit, decays[v] * grad + backward[v], grad)
+    carries = (jnp.where(lower, state, grad), jnp.where(lower, grad, state))
+    outs = [hand_on(pair_flags(k == 1), d, dp, xs[k], ys[k], carries[k]) for k in range(2)]
+    return [[v.astype(BF16) for v in pair] for pair in outs]
 
 
 def solution(mesh):

time: 38.4 us -> 34.5 us (0.90)
  waiting for transfers between devices: 8.2 us -> 3.69 us
  Pallas kernels: 17.5 us -> 18.8 us
  starting transfers between devices: 11 us -> 10.6 us
    ppermute x7 -> x6, waiting for transfers between devices: 8.2 us -> 3.69 us  [swap(): return lax.ppermute(v, 'seq', [(i, i ^ bit) for i in range(count)])]
    pallas_call x1, Pallas kernels: 2.48 us -> 3.74 us  [first_part(): pl.pallas_call(functools.partial(first_kernel, columns // heads), out_sha...]
    pallas_call x6 -> x5, Pallas kernels: 4.89 us -> 4.14 us  [the longest x1 3.76 us: own_part(): pl.pallas_call(functools.partial(own_kernel, columns // heads), out_shape...]
    pallas_call x6, Pallas kernels: 5.88 us -> 6.57 us  [intra(): pl.pallas_call(functools.partial(intra_kernel, rel, pair0, pairs, head_di...]
    ppermute x7 -> x6, starting transfers between devices: 11 us -> 10.6 us  [swap(): return lax.ppermute(v, 'seq', [(i, i ^ bit) for i in range(count)])]
  transfers between devices with their start and end apart: 7 -> 6, of which waited for: 3 -> 2; matrix products, arithmetic and copies ran while one was open for 0% -> 0% of each run, Pallas kernels for 32% -> 35%
where the time goes in v3:
time: 34.5 us; the launch traced here: 34.6 us
  Pallas kernels  18.8 us (54%)
  starting transfers between devices  10.6 us (31%)
  waiting for transfers between devices  3.69 us (11%)
  between operations  1.54 us (4%)
    ppermute x6, starting transfers between devices, swap(): return lax.ppermute(v, 'seq', [(i, i ^ bit) for i in range(count)])  10.6 us
    pallas_call x6, Pallas kernels, intra(): pl.pallas_call(functools.partial(intra_kernel, rel, pair0, pairs, head_di...  6.57 us
    pallas_call x2, Pallas kernels, inter(): pl.pallas_call(functools.partial(inter_kernel, last, head_dim, len(parts)...  4.3 us
    pallas_call x1, Pallas kernels, own_part(): pl.pallas_call(functools.partial(own_kernel, columns // heads), out_shape...  3.76 us
    pallas_call x1, Pallas kernels, first_part(): pl.pallas_call(functools.partial(first_kernel, columns // heads), out_sha...  3.74 us
    ppermute x6, waiting for transfers between devices, swap(): return lax.ppermute(v, 'seq', [(i, i ^ bit) for i in range(count)])  3.69 us
  transfers between devices with their start and end apart: 6, of which 2 were waited for; matrix products, arithmetic and copies ran while one was open for 0% of the time, Pallas kernels for 35%

profile of v3, /device:TPU:0, one launch (start us, length us, event | category | flops | bytes accessed | tf_op | source)
XLA Modules:
  0.0 34.6 jit_solution(4553833536091965820)
XLA Ops:
  1.3 0.0 copy-start
  1.3 3.7 %first.1 = (bf16[51,16,128]{2,1,0:T(8,128)(2,1)S(1)}, f32[24,16,128]{2,1,0:T(8,128)S(1)}, f32[24,16,128]{2,1,0:T(8,128)S(1)}, bf16[2,2,256,3072]{3,2,1,0:T(8,128...) custom-call(s32[1]{0:T(128)S(6)} %copy.13.len_ref, ...), custom_call_target="tpu_custom_call" | custom-call | tf_op jit(solution)/shard_map/first/pallas_call | solution.py:209
  5.0 3.3 %collective-permute-start = (bf16[51,16,128]{2,1,0:T(8,128)(2,1)S(1)}, bf16[51,16,128]{2,1,0:T(8,128)(2,1)S(1)}, u32[]{:S(2)}, u32[]{:S(2)}) collective-permute-start(bf16[51,16,128]{2,1,0:T(8,128)(2,1)S(1)} %get-tuple-element.62), channel_id=1, source_target_pairs={{0,4},{4,0},{8,12},{12,8},{16,20},{20,16},{24,28},{28,24},{1,5},{5... | collective-permute-start | bytes 626696 | tf_op jit(solution)/shard_map/ppermute | solution.py:612
  8.3 0.0 copy-done
  8.3 3.8 %own.1 = (bf16[2,2,256,3072]{3,2,1,0:T(8,128)(2,1)S(1)}, f32[24,16,128]{2,1,0:T(8,128)S(1)}, f32[24,16,128]{2,1,0:T(8,128)S(1)}, f32[24,16,128]{2,1,0:T(8,128)S(...) custom-call(s32[1]{0:T(128)S(6)} %copy.13.len_ref, ...), custom_call_target="tpu_custom_call", output_to_operand_aliasing={{0}: (7, {})} | custom-call | tf_op jit(solution)/shard_map/own/pallas_call | solution.py:306
  12.1 1.1 %intra.6 = (bf16[256,1024]{1,0:T(8,128)(2,1)S(1)}, f32[2,128,128]{2,1,0:T(8,128)S(1)}) custom-call(f32[48,256]{1,0:T(8,128)S(1)} %get-tuple-element.63.row_ref, f32[256,48]{1,0:T(8,128)S(1)} %get-tuple-element.64.col_ref, f32[2,128,128]{2,1,0:T(8,128)S(1)} %get-tuple-element.65.cb_ref, f32[24,128]{1,0:T(8,128)S(1)} %get-tuple-element.66.skip_ref, ...), custom_call_target="tpu_custom_call" | custom-call | flops 268435456 | bytes 1572864 | tf_op jit(solution)/shard_map/intra/pallas_call | solution.py:457
  13.2 0.0 collective-permute-done.y_ref
  13.2 0.1 total.2.refs_0_
  13.3 1.9 %collective-permute-start.1 = (bf16[27,16,128]{2,1,0:T(8,128)(2,1)S(1)}, bf16[27,16,128]{2,1,0:T(8,128)(2,1)S(1)}, u32[]{:S(2)}, u32[]{:S(2)}) collective-permute-start(bf16[27,16,128]{2,1,0:T(8,128)(2,1)S(1)} %total.2.refs_0_), channel_id=1, source_target_pairs={{0,8},{4,12},{8,0},{12,4},{16,24},{20,28},{24,16},{28,20},{1,9},{5... | collective-permute-start | bytes 331784 | tf_op jit(solution)/shard_map/ppermute | solution.py:612
  15.2 0.1 total.3.refs_1_
  15.3 0.2 collective-permute-start.3
  15.5 1.1 %intra.7 = (bf16[256,1024]{1,0:T(8,128)(2,1)S(1)}, f32[2,128,128]{2,1,0:T(8,128)S(1)}) custom-call(f32[48,256]{1,0:T(8,128)S(1)} %get-tuple-element.63.row_ref, f32[256,48]{1,0:T(8,128)S(1)} %get-tuple-element.64.col_ref, f32[2,128,128]{2,1,0:T(8,128)S(1)} %get-tuple-element.65.cb_ref, f32[24,128]{1,0:T(8,128)S(1)} %get-tuple-element.66.skip_ref, ...), custom_call_target="tpu_custom_call" | custom-call | flops 268435456 | bytes 1572864 | tf_op jit(solution)/shard_map/intra/pallas_call | solution.py:457
  16.6 2.6 %collective-permute-done.1.r_ref = bf16[27,16,128]{2,1,0:T(8,128)(2,1)S(1)} collective-permute-done((bf16[27,16,128]{2,1,0:T(8,128)(2,1)S(1)}, bf16[27,16,128]{2,1,0:T(8,128)(2,1)S(1)}, u32[]{:S(2)}, u32[]{:S(2)}) %collective-permute-start.1) | collective-permute-done | bytes 110624 | tf_op jit(solution)/shard_map/ppermute | solution.py:612
  19.2 0.2 near.1
  19.3 3.1 %collective-permute-start.4 = (bf16[24,16,128]{2,1,0:T(8,128)(2,1)S(1)}, bf16[24,16,128]{2,1,0:T(8,128)(2,1)S(1)}, u32[]{:S(2)}, u32[]{:S(2)}) collective-permute-start(bf16[24,16,128]{2,1,0:T(8,128)(2,1)S(1)} %get-tuple-element.71.refs_1_), channel_id=1, source_target_pairs={{0,16},{4,20},{8,24},{12,28},{16,0},{20,4},{24,8},{28,12},{1,17},{... | collective-permute-start | bytes 294920 | tf_op jit(solution)/shard_map/ppermute | solution.py:612
  22.4 1.2 %collective-permute-start.2 = (bf16[24,16,128]{2,1,0:T(8,128)(2,1)S(1)}, bf16[24,16,128]{2,1,0:T(8,128)(2,1)S(1)}, u32[]{:S(2)}, u32[]{:S(2)}) collective-permute-start(bf16[24,16,128]{2,1,0:T(8,128)(2,1)S(1)} %get-tuple-element.70), channel_id=1, source_target_pairs={{0,4},{4,0},{8,12},{12,8},{16,20},{20,16},{24,28},{28,24},{1,5},{5... | collective-permute-start | bytes 294920 | tf_op jit(solution)/shard_map/ppermute | solution.py:612
  23.5 1.1 %intra.8 = (bf16[256,1024]{1,0:T(8,128)(2,1)S(1)}, f32[2,128,128]{2,1,0:T(8,128)S(1)}) custom-call(f32[48,256]{1,0:T(8,128)S(1)} %get-tuple-element.63.row_ref, f32[256,48]{1,0:T(8,128)S(1)} %get-tuple-element.64.col_ref, f32[2,128,128]{2,1,0:T(8,128)S(1)} %get-tuple-element.65.cb_ref, f32[24,128]{1,0:T(8,128)S(1)} %get-tuple-element.66.skip_ref, ...), custom_call_target="tpu_custom_call" | custom-call | flops 268435456 | bytes 1572864 | tf_op jit(solution)/shard_map/intra/pallas_call | solution.py:457
  24.6 1.1 %intra.9 = (bf16[256,1024]{1,0:T(8,128)(2,1)S(1)}, f32[2,128,128]{2,1,0:T(8,128)S(1)}) custom-call(f32[48,256]{1,0:T(8,128)S(1)} %get-tuple-element.57.rowo_ref.row_ref, f32[256,48]{1,0:T(8,128)S(1)} %get-tuple-element.72.col_ref, f32[2,128,128]{2,1,0:T(8,128)S(1)} %get-tuple-element.65.cb_ref, f32[24,128]{1,0:T(8,128)S(1)} %get-tuple-element.73.skip_ref, ...), custom_call_target="tpu_custom_call" | custom-call | flops 268435456 | bytes 1572864 | tf_op jit(solution)/shard_map/intra/pallas_call | solution.py:457
  25.7 1.1 %intra.10 = (bf16[256,1024]{1,0:T(8,128)(2,1)S(1)}, f32[2,128,128]{2,1,0:T(8,128)S(1)}) custom-call(f32[48,256]{1,0:T(8,128)S(1)} %get-tuple-element.57.rowo_ref.row_ref, f32[256,48]{1,0:T(8,128)S(1)} %get-tuple-element.72.col_ref, f32[2,128,128]{2,1,0:T(8,128)S(1)} %get-tuple-element.65.cb_ref, f32[24,128]{1,0:T(8,128)S(1)} %get-tuple-element.73.skip_ref, ...), custom_call_target="tpu_custom_call" | custom-call | flops 268435456 | bytes 1572864 | tf_op jit(solution)/shard_map/intra/pallas_call | solution.py:457
  26.9 0.0 collective-permute-done.3.r2_ref
  26.9 0.0 collective-permute-done.4.far_ref
  26.9 0.1 far.1
  27.0 0.9 %collective-permute-start.5 = (bf16[24,16,128]{2,1,0:T(8,128)(2,1)S(1)}, bf16[24,16,128]{2,1,0:T(8,128)(2,1)S(1)}, u32[]{:S(2)}, u32[]{:S(2)}) collective-permute-start(bf16[24,16,128]{2,1,0:T(8,128)(2,1)S(1)} %get-tuple-element.77.refs_1_), channel_id=1, source_target_pairs={{0,4},{4,0},{8,12},{12,8},{16,20},{20,16},{24,28},{28,24},{1,5},{5... | collective-permute-start | bytes 294920 | tf_op jit(solution)/shard_map/ppermute | solution.py:612
  27.9 1.1 %intra.11 = (bf16[256,1024]{1,0:T(8,128)(2,1)S(1)}, f32[2,128,128]{2,1,0:T(8,128)S(1)}) custom-call(f32[48,256]{1,0:T(8,128)S(1)} %get-tuple-element.57.rowo_ref.row_ref, f32[256,48]{1,0:T(8,128)S(1)} %get-tuple-element.72.col_ref, f32[2,128,128]{2,1,0:T(8,128)S(1)} %get-tuple-element.65.cb_ref, f32[24,128]{1,0:T(8,128)S(1)} %get-tuple-element.73.skip_ref, ...), custom_call_target="tpu_custom_call" | custom-call | flops 268435456 | bytes 1572864 | tf_op jit(solution)/shard_map/intra/pallas_call | solution.py:457
  29.0 1.5 %inter.2 = (bf16[256,3072]{1,0:T(8,128)(2,1)S(1)}, f32[16,256]{1,0:T(8,128)S(1)}, f32[16,256]{1,0:T(8,128)S(1)}) custom-call(bf16[16,256]{1,0:T(8,128)(2,1)S(1)} %get-tuple-element.51.b_ref, bf16[16,256]{1,0:T(8,128)(2,1)S(1)} %get-tuple-element.52.c_ref, f32[2,48,256]{2,1,0:T(8,128)S(1)} %get-tuple-element.83.w_ref, ...), custom_call_target="tpu_custom_call" | custom-call | flops 1207959552 | bytes 6291456 | tf_op jit(solution)/shard_map/inter/pallas_call | solution.py:583
  30.5 0.0 collective-permute-done.2.one_ref
  30.5 1.1 %collective-permute-done.5.two_ref = bf16[24,16,128]{2,1,0:T(8,128)(2,1)S(1)} collective-permute-done((bf16[24,16,128]{2,1,0:T(8,128)(2,1)S(1)}, bf16[24,16,128]{2,1,0:T(8,128)(2,1)S(1)}, u32[]{:S(2)}, u32[]{:S(2)}) %collective-permute-start.5) | collective-permute-done | bytes 98336 | tf_op jit(solution)/shard_map/ppermute | solution.py:612
  31.7 2.8 %inter.3 = (bf16[256,6144]{1,0:T(8,128)(2,1)}, f32[16,256]{1,0:T(8,128)}, f32[16,256]{1,0:T(8,128)}) custom-call(bf16[16,256]{1,0:T(8,128)(2,1)S(1)} %get-tuple-element.51.b_ref, bf16[16,256]{1,0:T(8,128)(2,1)S(1)} %get-tuple-element.52.c_ref, f32[2,48,256]{2,1,0:T(8,128)S(1)} %get-tuple-element.53.w_ref, f32[2,24,128]{2,1,0:T(8,128)S(1)} %get-tuple-element.54.rows_ref, ...), custom_call_target="tpu_custom_call" | custom-call | flops 1207959552 | bytes 6291456 | tf_op jit(solution)/shard_map/inter/pallas_call | solution.py:583
Async XLA Ops:
  1.3 7.1 %copy-start = (f32[96]{0:T(128)S(1)}, f32[96]{0:T(128)}, u32[]{:S(2)}) copy-start(f32[96]{0:T(128)} %skip_ref.1) | copy-start | bytes 1156
  5.0 8.2 %collective-permute-start = (bf16[51,16,128]{2,1,0:T(8,128)(2,1)S(1)}, bf16[51,16,128]{2,1,0:T(8,128)(2,1)S(1)}, u32[]{:S(2)}, u32[]{:S(2)}) collective-permute-start(bf16[51,16,128]{2,1,0:T(8,128)(2,1)S(1)} %get-tuple-element.62), channel_id=1, source_target_pairs={{0,4},{4,0},{8,12},{12,8},{16,20},{20,16},{24,28},{28,24},{1,5},{5... | collective-permute-start | bytes 626696 | tf_op jit(solution)/shard_map/ppermute | solution.py:612
  13.3 5.9 %collective-permute-start.1 = (bf16[27,16,128]{2,1,0:T(8,128)(2,1)S(1)}, bf16[27,16,128]{2,1,0:T(8,128)(2,1)S(1)}, u32[]{:S(2)}, u32[]{:S(2)}) collective-permute-start(bf16[27,16,128]{2,1,0:T(8,128)(2,1)S(1)} %total.2.refs_0_), channel_id=1, source_target_pairs={{0,8},{4,12},{8,0},{12,4},{16,24},{20,28},{24,16},{28,20},{1,9},{5... | collective-permute-start | bytes 331784 | tf_op jit(solution)/shard_map/ppermute | solution.py:612
  15.3 11.6 %collective-permute-start.3 = (bf16[24,16,128]{2,1,0:T(8,128)(2,1)S(1)}, bf16[24,16,128]{2,1,0:T(8,128)(2,1)S(1)}, u32[]{:S(2)}, u32[]{:S(2)}) collective-permute-start(bf16[24,16,128]{2,1,0:T(8,128)(2,1)S(1)} %total.3.refs_1_), channel_id=1, source_target_pairs={{0,8},{4,12},{8,0},{12,4},{16,24},{20,28},{24,16},{28,20},{1,9},{5... | collective-permute-start | bytes 294920 | tf_op jit(solution)/shard_map/ppermute | solution.py:612
  19.3 7.6 %collective-permute-start.4 = (bf16[24,16,128]{2,1,0:T(8,128)(2,1)S(1)}, bf16[24,16,128]{2,1,0:T(8,128)(2,1)S(1)}, u32[]{:S(2)}, u32[]{:S(2)}) collective-permute-start(bf16[24,16,128]{2,1,0:T(8,128)(2,1)S(1)} %get-tuple-element.71.refs_1_), channel_id=1, source_target_pairs={{0,16},{4,20},{8,24},{12,28},{16,0},{20,4},{24,8},{28,12},{1,17},{... | collective-permute-start | bytes 294920 | tf_op jit(solution)/shard_map/ppermute | solution.py:612
  22.4 8.2 %collective-permute-start.2 = (bf16[24,16,128]{2,1,0:T(8,128)(2,1)S(1)}, bf16[24,16,128]{2,1,0:T(8,128)(2,1)S(1)}, u32[]{:S(2)}, u32[]{:S(2)}) collective-permute-start(bf16[24,16,128]{2,1,0:T(8,128)(2,1)S(1)} %get-tuple-element.70), channel_id=1, source_target_pairs={{0,4},{4,0},{8,12},{12,8},{16,20},{20,16},{24,28},{28,24},{1,5},{5... | collective-permute-start | bytes 294920 | tf_op jit(solution)/shard_map/ppermute | solution.py:612
  27.0 4.7 %collective-permute-start.5 = (bf16[24,16,128]{2,1,0:T(8,128)(2,1)S(1)}, bf16[24,16,128]{2,1,0:T(8,128)(2,1)S(1)}, u32[]{:S(2)}, u32[]{:S(2)}) collective-permute-start(bf16[24,16,128]{2,1,0:T(8,128)(2,1)S(1)} %get-tuple-element.77.refs_1_), channel_id=1, source_target_pairs={{0,4},{4,0},{8,12},{12,8},{16,20},{20,16},{24,28},{28,24},{1,5},{5... | collective-permute-start | bytes 294920 | tf_op jit(solution)/shard_map/ppermute | solution.py:612

commit v4 on v3

v4 whole, which is shorter than its diff:
```python
import functools
import math

import jax
import jax.numpy as jnp
from jax import lax
from jax.experimental import pallas as pl
from jax.experimental.pallas import tpu as pltpu
from jax.sharding import PartitionSpec as P

SPAN = 256
LANES = 128
SLAB = 2 * LANES
LOG2E = math.log2(math.e)
F32 = jnp.float32
BF16 = jnp.bfloat16
NT = (((1,), (1,)), ((), ()))
TN = (((0,), (0,)), ((), ()))
OTHER, OWN = 0, 1


def place():
    idx = lax.axis_index("seq")
    count = lax.axis_size("seq")
    return idx, lax.rem(idx, 2), idx < count // 2


def mm(a, b, dims=None):
    if dims is None:
        return jnp.dot(a, b, preferred_element_type=F32)
    return lax.dot_general(a, b, dims, preferred_element_type=F32)


def pick(condition, a, b):
    if isinstance(condition, bool):
        return a if condition else b
    return jnp.where(condition, a, b)


def whole():
    return pl.BlockSpec(memory_space=pltpu.VMEM)


def smem():
    return pl.BlockSpec(memory_space=pltpu.SMEM)


def hbm():
    return pl.BlockSpec(memory_space=pltpu.HBM)


def iota(shape, axis):
    return lax.broadcasted_iota(jnp.int32, shape, axis)


def running_sum(values):
    rows, span = values.shape
    sub = span // 2
    high = values.astype(BF16)
    rest = values - high.astype(F32)
    middle = rest.astype(BF16)
    low = (rest - middle.astype(F32)).astype(BF16)
    upper = (iota((sub, sub), 0) <= iota((sub, sub), 1)).astype(F32).astype(BF16)
    pieces = jnp.concatenate([high, middle, low], axis=0)
    halves = []
    for s in range(2):
        sums = mm(pieces[:, s * sub : (s + 1) * sub], upper)
        halves.append(sums[:rows] + sums[rows : 2 * rows] + sums[2 * rows :])
    return jnp.concatenate(halves, axis=1)


def weights(ld, dt, valid):
    cum = running_sum(ld)
    rows, span = cum.shape
    sub = span // 2
    end_a, end_b = cum[:, sub - 1 : sub], cum[:, span - 1 : span]
    ends = jnp.where(iota(cum.shape, 1) < sub, end_a, end_b)
    into_grad = jnp.where(iota(cum.shape, 1) < valid, jnp.exp(cum), 0.0)
    return cum, dt * jnp.exp(ends - cum), into_grad, jnp.exp(end_a), jnp.exp(end_b)


def spread(column, scratch_ref, head_dim):
    rows = scratch_ref.shape[0]
    scratch_ref[...] = jnp.broadcast_to(column, scratch_ref.shape)
    even = scratch_ref[pl.ds(0, rows // 2, stride=2), :]
    odd = scratch_ref[pl.ds(1, rows // 2, stride=2), :]
    return jnp.where(iota(even.shape, 1) < head_dim, even, odd)


def run_task(is_state, weight, read, chunks, head_dim, mat, w_ref, rows_ref, put, span, width):
    sub = span // 2
    states = mat.shape[0]
    per = SLAB // head_dim
    low = iota((states, LANES), 1) < head_dim
    w_ref[...] = weight
    chunk = width // chunks
    for g in range(width // SLAB):
        if g * SLAB % chunk == 0:
            read(None, g * SLAB // chunk)
        lhs = jnp.concatenate(
            [(mat * w_ref[pl.ds(per * g + j, 1), :]).astype(BF16) for j in range(per)], axis=0
        )
        parts = [mm(lhs[:, s * sub : (s + 1) * sub], read(s, g)) for s in range(2)]
        for q in range(2):
            lanes = slice(q * LANES, (q + 1) * LANES)
            top = slice(2 * q * states, (2 * q + 1) * states)
            bottom = slice((2 * q + 1) * states, (2 * q + 2) * states)
            e0, e1 = [jnp.where(low, p[top, lanes], p[bottom, lanes]) for p in parts]
            j = 2 * g + q
            d_a, d_b = rows_ref[0, pl.ds(j, 1), :], rows_ref[1, pl.ds(j, 1), :]
            if isinstance(is_state, bool):
                total = d_b * e0 + e1 if is_state else e0 + d_a * e1
            else:
                total = jnp.where(is_state, d_b, 1.0) * e0 + jnp.where(is_state, 1.0, d_a) * e1
            put(j, total, pick(is_state, e0, e1))


def first_kernel(
    head_dim, len_ref, ld_hbm, dt_hbm, b_hbm, c_hbm, x_ref, dy_ref,
    msg_ref, sub_ref, ld_ref, dt_ref, b_ref, c_ref, w_ref, rows_ref, row_ref,
    data_ref, task_w_ref, spread_ref, sems, small_sems
):
    idx, mine, lower = place()
    span = ld_ref.shape[1]
    sub = span // 2
    half_heads = ld_ref.shape[0] // 2
    width = data_ref.shape[1]
    chunks = sems.shape[0]
    chunk = width // chunks
    small = [
        pltpu.make_async_copy(src, dst, small_sems.at[i])
        for i, (src, dst) in enumerate(
            ((ld_hbm, ld_ref), (dt_hbm, dt_ref), (b_hbm, b_ref), (c_hbm, c_ref))
        )
    ]
    for copy in small:
        copy.start()

    def fetch(i, src):
        start = pl.multiple_of((1 - mine) * width + i * chunk, LANES)
        return pltpu.make_async_copy(
            src.at[:, pl.ds(start, chunk)], data_ref.at[:, pl.ds(i * chunk, chunk)], sems.at[i]
        )

    for i in range(chunks):

        @pl.when(lower)
        def _():
            fetch(i, x_ref).start()

        @pl.when(jnp.logical_not(lower))
        def _():
            fetch(i, dy_ref).start()

    for copy in small:
        copy.wait()
    rows = pl.ds(pl.multiple_of((1 - mine) * half_heads, 8), half_heads)
    valid = len_ref[0] - idx * span
    cum, ws, wg, d_a, d_b = weights(ld_ref[rows, :], dt_ref[rows, :], valid)
    w_ref[0] = ws
    w_ref[1] = wg
    row_ref[...] = cum * LOG2E
    rows_a = spread(d_a, spread_ref, head_dim)
    rows_b = spread(d_b, spread_ref, head_dim)
    rows_ref[0] = rows_a
    rows_ref[1] = rows_b
    tiles = sub_ref.shape[0]
    extra = narrow_rows(rows_a * rows_b)
    msg_ref[tiles:] = extra.reshape((msg_ref.shape[0] - tiles,) + msg_ref.shape[1:])

    def read(s, g):
        if s is None:
            return fetch(g, x_ref).wait()
        return data_ref[pl.ds(s * sub, sub), pl.ds(g * SLAB, SLAB)]

    def put(j, total, part):
        msg_ref[j] = total.astype(BF16)
        sub_ref[j] = part

    mat = jnp.where(lower, b_ref[...].astype(F32), c_ref[...].astype(F32))
    run_task(
        lower, jnp.where(lower, ws, wg), read, chunks, head_dim, mat, task_w_ref, rows_ref, put, span, width
    )


def first_part(length, ld, dt, b, c, x, dy):
    heads, span = ld.shape
    columns = x.shape[1]
    states = b.shape[0]
    tiles = columns // 2 // LANES
    pairs = heads // 4
    shape = jax.ShapeDtypeStruct
    tile = lambda n, t: shape((n, states, LANES), t)
    same = lambda a: shape(a.shape, a.dtype)
    outs = [
        tile(tiles + 2 * pairs // states, BF16),
        tile(tiles, F32),
        same(ld), same(dt), same(b), same(c),
    ] + table_shapes(heads, span)[:3]
    return pl.pallas_call(
        functools.partial(first_kernel, columns // heads),
        out_shape=outs,
        in_specs=[smem()] + [hbm() for _ in range(6)],
        out_specs=[whole() for _ in outs],
        scratch_shapes=[
            pltpu.VMEM((span, columns // 2), BF16),
            pltpu.VMEM((heads // 2, span), F32),
            pltpu.VMEM((heads // 2, LANES), F32),
            pltpu.SemaphoreType.DMA((4,)),
            pltpu.SemaphoreType.DMA((4,)),
        ],
        compiler_params=pltpu.CompilerParams(vmem_limit_bytes=8 << 20),
        name="first",
    )(length, ld, dt, b, c, x, dy)


def more_tables(half, head_dim, row, dt_ref, skip_ref, col_ref, skip_rows_ref):
    half_heads = row.shape[0]
    low = iota((1, LANES), 1) < head_dim
    rows = pl.ds(pl.multiple_of(half * half_heads, 8), half_heads)
    col_ref[...] = (row - jnp.log(dt_ref[rows, :]) * LOG2E).T
    for j in range(half_heads // 2):
        at = half * half_heads + 2 * j
        skip_rows_ref[pl.ds(j, 1), :] = jnp.where(low, skip_ref[at], skip_ref[at + 1])


def own_kernel(
    head_dim, len_ref, skip_ref, ld_ref, dt_ref, b_ref, c_ref, wo_ref, rowso_ref, rowo_ref, x_ref, dy_ref,
    xs_ref, subs_ref, send_ref, subo_ref, d_ref, cb_ref,
    w_ref, rows_ref, row_ref, col_ref, skip_rows_ref, colo_ref, skipo_ref,
    task_w_ref, spread_ref
):
    idx, mine, lower = place()
    span = ld_ref.shape[1]
    half_heads = ld_ref.shape[0] // 2
    width = x_ref.shape[1] // 2
    sub = span // 2
    valid = len_ref[0] - idx * span
    rows = pl.ds(pl.multiple_of(mine * half_heads, 8), half_heads)
    cum, ws, wg, d_a, d_b = weights(ld_ref[rows, :], dt_ref[rows, :], valid)
    w_ref[0] = ws
    w_ref[1] = wg
    rows_ref[0] = spread(d_a, spread_ref, head_dim)
    rows_ref[1] = spread(d_b, spread_ref, head_dim)
    row = cum * LOG2E
    row_ref[...] = row
    d_ref[...] = rows_ref[0] * rows_ref[1]
    more_tables(mine, head_dim, row, dt_ref, skip_ref, col_ref, skip_rows_ref)
    more_tables(1 - mine, head_dim, rowo_ref[...], dt_ref, skip_ref, colo_ref, skipo_ref)
    for s in range(2):
        cols = slice(s * sub, (s + 1) * sub)
        dots = mm(b_ref[:, cols], c_ref[:, cols], TN)
        t, u = iota(dots.shape, 0), iota(dots.shape, 1)
        cb_ref[s] = jnp.where(jnp.logical_and(u >= t, u + s * sub < valid), dots, 0.0)
    b, c = b_ref[...].astype(F32), c_ref[...].astype(F32)
    kind_slot = jnp.where(lower, 0, 1)

    def reader(ref, half):
        def read(s, g):
            if s is None:
                return None
            start = pl.multiple_of(half * width + g * SLAB, LANES)
            return ref[pl.ds(s * sub, sub), pl.ds(start, SLAB)]

        return read

    def putter(slot):
        def put(j, total, part):
            xs_ref[slot, j] = total
            subs_ref[slot, j] = part

        return put

    def put_other(j, total, part):
        send_ref[j] = total.astype(BF16)
        subo_ref[j] = part

    run_task(
        True, ws, reader(x_ref, mine), 1, head_dim, b, task_w_ref.at[0], rows_ref, putter(kind_slot), span, width
    )
    run_task(
        False, wg, reader(dy_ref, mine), 1, head_dim, c, task_w_ref.at[1], rows_ref,
        putter(1 - kind_slot), span, width,
    )
    upper = jnp.logical_not(lower)
    read_x, read_dy = reader(x_ref, 1 - mine), reader(dy_ref, 1 - mine)

    def read_either(s, g):
        return None if s is None else jnp.where(upper, read_x(s, g), read_dy(s, g))

    run_task(
        upper, jnp.where(upper, wo_ref[0], wo_ref[1]), read_either, 1, head_dim, jnp.where(upper, b, c),
        task_w_ref.at[2], rowso_ref, put_other, span, width,
    )


def table_shapes(heads, span):
    shape = jax.ShapeDtypeStruct
    half, pairs = heads // 2, heads // 4
    return [
        shape((2, half, span), F32),
        shape((2, pairs, LANES), F32),
        shape((half, span), F32),
        shape((span, half), F32),
        shape((pairs, LANES), F32),
    ]


def own_part(length, skip, ld, dt, b, c, other, x, dy):
    heads, span = ld.shape
    columns = x.shape[1]
    states = b.shape[0]
    pairs = heads // 4
    sub = span // 2
    tiles = columns // 2 // LANES
    shape = jax.ShapeDtypeStruct
    outs = [shape((2, tiles, states, LANES), F32)] * 2
    outs += [shape((tiles, states, LANES), BF16), shape((tiles, states, LANES), F32)]
    outs += [shape((pairs, LANES), F32), shape((2, sub, sub), F32)]
    outs += table_shapes(heads, span) + table_shapes(heads, span)[3:]
    return pl.pallas_call(
        functools.partial(own_kernel, columns // heads),
        out_shape=outs,
        in_specs=[smem(), smem()] + [whole() for _ in range(9)],
        out_specs=[whole() for _ in outs],
        scratch_shapes=[
            pltpu.VMEM((3, heads // 2, span), F32),
            pltpu.VMEM((heads // 2, LANES), F32),
        ],
        compiler_params=pltpu.CompilerParams(vmem_limit_bytes=8 << 20),
        name="own",
    )(length, skip, ld, dt, b, c, *other, x, dy)


def pair_flags(second):
    idx, mine, lower = place()
    ahead = jnp.where(lower, mine == 0, mine == 1)
    return jnp.logical_not(ahead) if second else ahead


def inner_unit():
    unit = lax.axis_index("seq") // 2
    return jnp.logical_or(unit == 1, unit == 2)


def wide_rows(ref, tiles):
    both = ref[tiles:]
    both = both.reshape(both.shape[0] * both.shape[1], LANES).astype(F32)
    count = both.shape[0] // 2
    return both[:count] + both[count:]


def narrow_rows(rows):
    high = rows.astype(BF16).astype(F32)
    return jnp.concatenate([high, rows - high], axis=0).astype(BF16)


def pair_total(ahead, d, dp, x, y):
    return jnp.where(ahead, dp, d) * jnp.where(ahead, x, y) + jnp.where(ahead, y, x)


def hand_on(ahead, d, dp, x, y, carry):
    passed = jnp.where(ahead, d, dp) * carry + jnp.where(ahead, x, y)
    return jnp.where(ahead, carry, passed), jnp.where(ahead, passed, carry)


def total_kernel(second, decay_ref, mine_ref, x_ref, y_ref, *refs):
    out_ref, dp_ref = refs[-2:]
    ahead = pair_flags(second)
    tiles = x_ref.shape[1]
    dp_ref[...] = wide_rows(decay_ref, tiles)
    if not second:
        rows = narrow_rows(dp_ref[...] * mine_ref[...])
        out_ref[tiles:] = rows.reshape((out_ref.shape[0] - tiles,) + out_ref.shape[1:])
    for j in range(tiles):
        dp, d = dp_ref[pl.ds(j, 1), :], mine_ref[pl.ds(j, 1), :]
        total = pair_total(ahead, d, dp, x_ref[int(second), j], y_ref[j].astype(F32))
        out_ref[j] = total.astype(BF16)


def near_kernel(decay_ref, mine_ref, x_ref, y_ref, r_ref, *refs):
    msg_ref, own_ref, send_ref, dp_ref, pd_ref = refs[-5:]
    ahead = pair_flags(False)
    inner = inner_unit()
    tiles = x_ref.shape[1]
    dp_ref[...] = wide_rows(decay_ref, tiles)
    pd_ref[...] = wide_rows(r_ref, tiles)
    for j in range(tiles):
        dp, d, pd = dp_ref[pl.ds(j, 1), :], mine_ref[pl.ds(j, 1), :], pd_ref[pl.ds(j, 1), :]
        x, y, got = x_ref[0, j], y_ref[j].astype(F32), r_ref[j].astype(F32)
        total = pair_total(ahead, d, dp, x, y)
        joined = jnp.where(inner, d * dp, pd) * jnp.where(inner, got, total) + jnp.where(
            inner, total, got
        )
        msg_ref[j] = joined.astype(BF16)
        own, send = hand_on(ahead, d, dp, x, y, jnp.where(inner, got, 0.0))
        own_ref[j] = own.astype(BF16)
        send_ref[j] = send.astype(BF16)


def far_kernel(decay_ref, mine_ref, x_ref, y_ref, r_ref, r2_ref, far_ref, *refs):
    own_ref, send_ref, dp_ref, pd_ref = refs[-4:]
    ahead = pair_flags(True)
    inner = inner_unit()
    tiles = x_ref.shape[1]
    dp_ref[...] = wide_rows(decay_ref, tiles)
    pd_ref[...] = wide_rows(r_ref, tiles)
    for j in range(tiles):
        dp, d, pd = dp_ref[pl.ds(j, 1), :], mine_ref[pl.ds(j, 1), :], pd_ref[pl.ds(j, 1), :]
        x, y = x_ref[1, j], y_ref[j].astype(F32)
        far = far_ref[j].astype(F32)
        carry = jnp.where(inner, far, r2_ref[j].astype(F32) + pd * far)
        own, send = hand_on(ahead, d, dp, x, y, carry)
        own_ref[j] = own.astype(BF16)
        send_ref[j] = send.astype(BF16)


def small_call(kernel, name, outs, rows_shape, scratch, args, after=()):
    return pl.pallas_call(
        kernel,
        out_shape=[jax.ShapeDtypeStruct(o, BF16) for o in outs],
        in_specs=[whole() for _ in args] + [pl.BlockSpec(memory_space=pl.ANY) for _ in after],
        out_specs=[whole() for _ in outs],
        scratch_shapes=[pltpu.VMEM(rows_shape, F32)] * scratch,
        compiler_params=pltpu.CompilerParams(vmem_limit_bytes=4 << 20),
        name=name,
    )(*args, *after)


def intra_kernel(rel, pair0, pairs, head_dim, first, len_ref, row_ref, col_ref, cb_ref, skip_ref, x_ref, dy_ref, *refs):
    mix_in = None if first else refs[0]
    part_ref, mix_ref = refs[-2:]
    sub = cb_ref.shape[1]
    idx, mine, lower = place()
    base = (mine if rel == OWN else 1 - mine) * (x_ref.shape[1] // 2)
    valid = len_ref[0] - idx * x_ref.shape[0]
    lane = iota((1, LANES), 1)
    keep = [
        (lane < head_dim).astype(F32).astype(BF16),
        (lane >= head_dim).astype(F32).astype(BF16),
    ]
    for s in range(2):
        here = pl.ds(s * sub, sub)
        acc = None if first else mix_in[s]
        inside = iota((sub, LANES), 0) + s * sub < valid
        for p in range(pairs):
            cols = pl.ds(pl.multiple_of(base + (pair0 + p) * LANES, LANES), LANES)
            xs = x_ref[here, cols]
            ys = dy_ref[here, cols]
            split = jnp.concatenate([ys * keep[0], ys * keep[1]], axis=0)
            scores = mm(xs, split, NT)
            kernels = []
            for j in range(2):
                h = 2 * (pair0 + p) + j
                row = row_ref[pl.ds(h, 1), here]
                col = col_ref[here, pl.ds(h, 1)]
                decay = jnp.exp2(jnp.minimum(row - col, 100.0))
                kernels.append((decay * cb_ref[s]).astype(BF16))
                term = decay * scores[:, j * sub : (j + 1) * sub]
                acc = term if acc is None else acc + term
            within = mm(jnp.concatenate(kernels, axis=1), split)
            skip = skip_ref[pl.ds(pair0 + p, 1), :]
            part_ref[here, pl.ds(p * LANES, LANES)] = (
                within + jnp.where(inside, skip * ys.astype(F32), 0.0)
            ).astype(part_ref.dtype)
        mix_ref[s] = acc


def intra(rel, pair0, pairs, head_dim, length, row, col, cb, skip, x, dy, mix, after=()):
    span = x.shape[0]
    args = [row, col, cb, skip, x, dy] + ([] if mix is None else [mix])
    heads = 2 * pairs
    return pl.pallas_call(
        functools.partial(intra_kernel, rel, pair0, pairs, head_dim, mix is None),
        out_shape=[
            jax.ShapeDtypeStruct((span, pairs * LANES), BF16),
            jax.ShapeDtypeStruct(cb.shape, F32),
        ],
        in_specs=[smem()] + [whole() for _ in args] + [pl.BlockSpec(memory_space=pl.ANY) for _ in after],
        out_specs=[whole(), whole()],
        compiler_params=pltpu.CompilerParams(vmem_limit_bytes=8 << 20),
        cost_estimate=pl.CostEstimate(
            flops=heads * 2 * span * span * 128,
            transcendentals=heads * span * span // 2,
            bytes_accessed=heads * head_dim * span * 2 * 3,
        ),
        name="intra",
    )(length, *args, *after)


def pair_tiles(ref, g):
    return jnp.concatenate([ref[2 * g], ref[2 * g + 1]], axis=1)


def pair_rows(rows_ref, k, g):
    return jnp.concatenate(
        [rows_ref[k, pl.ds(2 * g, 1), :], rows_ref[k, pl.ds(2 * g + 1, 1), :]], axis=1
    )


def carry_pass(is_grad, carry_ref, sub_ref, data_ref, b_ref, w_ref, rows_ref, parts, buf_ref, base, head_dim, done):
    span, width = data_ref.shape[0], data_ref.shape[1] // 2
    sub = span // 2
    states = b_ref.shape[0]
    per = SLAB // head_dim
    rowhead = iota((per * states, SLAB), 0) // states
    lanehead = iota((per * states, SLAB), 1) // head_dim
    diag = (rowhead == lanehead).astype(F32).astype(BF16)
    b = b_ref[...].astype(F32) if is_grad else None
    slab_width = parts[0].shape[1] if is_grad else width
    total = [None, None]
    for g in range(width // SLAB):
        carry = pair_tiles(carry_ref, g)
        moved = pair_tiles(sub_ref, g) + pair_rows(rows_ref, int(is_grad), g) * carry.astype(F32)
        carries = [moved.astype(BF16), carry] if is_grad else [carry, moved.astype(BF16)]
        data_cols = pl.ds(pl.multiple_of(base + g * SLAB, LANES), SLAB)
        for s in range(2):
            here = pl.ds(s * sub, sub)
            rows = [w_ref[1 - int(is_grad), pl.ds(per * g + i, 1), here] for i in range(per)]
            spread_out = jnp.concatenate([carries[s]] * per, axis=0) * diag
            if is_grad:
                bs = b[:, s * sub : (s + 1) * sub]
                left = jnp.concatenate([(bs * r).astype(BF16) for r in rows], axis=0)
                across = mm(left, spread_out, TN)
                part = parts[g * SLAB // slab_width][here, pl.ds(g * SLAB % slab_width, SLAB)]
                buf_ref[here, pl.ds(g * SLAB, SLAB)] = (part.astype(F32) + across).astype(BF16)
            terms = mm(spread_out, data_ref[here, data_cols], NT)
            for i in range(per):
                term = rows[i] * terms[i * states : (i + 1) * states]
                total[s] = term if total[s] is None else total[s] + term
        done(g)
    return jnp.concatenate(total, axis=1)


class Sender:
    def __init__(self, buf_ref, out_ref, sems, base, every):
        self.buf_ref, self.out_ref, self.sems = buf_ref, out_ref, sems
        self.base, self.every, self.copies = base, every, []

    def __call__(self, g):
        if (g + 1) % self.every == 0:
            wide = self.every * SLAB
            k = len(self.copies)
            copy = pltpu.make_async_copy(
                self.buf_ref.at[:, pl.ds(k * wide, wide)],
                self.out_ref.at[:, pl.ds(pl.multiple_of(self.base + k * wide, LANES), wide)],
                self.sems.at[k],
            )
            copy.start()
            self.copies.append(copy)

    def wait(self):
        for copy in self.copies:
            copy.wait()


def inter_own_kernel(
    head_dim, slabs, len_ref, b_ref, c_ref, w_ref, rows_ref, x_ref, dy_ref, one_ref, two_ref,
    subs_ref, mix_ref, *refs
):
    idx, mine, lower = place()
    parts = refs[:slabs]
    buf_ref, gb_ref, gc_ref, pick_ref = refs[slabs:]
    span, width = x_ref.shape[0], x_ref.shape[1] // 2
    sub = span // 2
    base = mine * width
    valid = len_ref[0] - idx * span
    for j in range(one_ref.shape[0]):
        pick_ref[0, j] = jnp.where(lower, two_ref[j], one_ref[j])
        pick_ref[1, j] = jnp.where(lower, one_ref[j], two_ref[j])
    slot = jnp.where(lower, 0, 1)
    gb = carry_pass(
        True, pick_ref.at[0], subs_ref.at[1 - slot], x_ref, b_ref, w_ref, rows_ref, parts, buf_ref, base,
        head_dim, lambda g: None,
    )
    gc = carry_pass(
        False, pick_ref.at[1], subs_ref.at[slot], dy_ref, b_ref, w_ref, rows_ref, None, None, base,
        head_dim, lambda g: None,
    )
    mixed_b, mixed_c = [], []
    for s in range(2):
        here = slice(s * sub, (s + 1) * sub)
        t, u = iota((sub, sub), 0), iota((sub, sub), 1)
        mix = jnp.where(jnp.logical_and(u >= t, u + s * sub < valid), mix_ref[s], 0.0)
        high = mix.astype(BF16)
        rest = (mix - high.astype(F32)).astype(BF16)
        bs, cs = b_ref[:, here], c_ref[:, here]
        mixed_b.append(mm(cs, high, NT) + mm(cs, rest, NT))
        mixed_c.append(mm(bs, high) + mm(bs, rest))
    gb_ref[...] = gb + jnp.concatenate(mixed_b, axis=1)
    gc_ref[...] = gc + jnp.concatenate(mixed_c, axis=1)


def near_other_kernel(
    head_dim, slabs, b_ref, w_ref, rows_ref, x_ref, dy_ref, carry_ref, sub_ref, gb_in, gc_in, slab_ref, *refs
):
    idx, mine, lower = place()
    parts = refs[:slabs]
    out_ref, buf_ref, gb_ref, gc_ref, sem = refs[slabs:]
    width = x_ref.shape[1] // 2
    base = (1 - mine) * width
    start = pl.multiple_of(mine * width, LANES)
    own_copy = pltpu.make_async_copy(slab_ref, out_ref.at[:, pl.ds(start, width)], sem)
    own_copy.start()
    gb_ref[...] = gb_in[...]
    gc_ref[...] = gc_in[...]

    @pl.when(jnp.logical_not(lower))
    def _():
        gb_ref[...] += carry_pass(
            True, carry_ref, sub_ref, x_ref, b_ref, w_ref, rows_ref, parts, buf_ref, base, head_dim,
            lambda g: None,
        )

    @pl.when(lower)
    def _():
        gc_ref[...] += carry_pass(
            False, carry_ref, sub_ref, dy_ref, b_ref, w_ref, rows_ref, None, None, base, head_dim,
            lambda g: None,
        )

    own_copy.wait()


def far_other_kernel(
    head_dim, slabs, every, scale_b, scale_c, b_ref, w_ref, rows_ref, x_ref, dy_ref, carry_ref, sub_ref,
    gb_in, gc_in, slab_ref, out_in, *refs
):
    idx, mine, lower = place()
    parts = refs[:slabs]
    out_ref, gb_out, gc_out, buf_ref, gb_ref, gc_ref, sems, small_sems = refs[slabs:]
    width = x_ref.shape[1] // 2
    base = (1 - mine) * width
    gb_ref[...] = gb_in[...] * scale_b
    gc_ref[...] = gc_in[...] * scale_c
    copies = [
        pltpu.make_async_copy(src, dst, small_sems.at[i])
        for i, (src, dst) in enumerate(((gb_ref, gb_out), (gc_ref, gc_out)))
    ]

    @pl.when(lower)
    def _():
        send = Sender(buf_ref, out_ref, sems, base, every)
        gb_ref[...] += scale_b * carry_pass(
            True, carry_ref, sub_ref, x_ref, b_ref, w_ref, rows_ref, parts, buf_ref, base, head_dim, send
        )
        for copy in copies:
            copy.start()
        send.wait()

    @pl.when(jnp.logical_not(lower))
    def _():
        start = pl.multiple_of(base, LANES)
        slab_copy = pltpu.make_async_copy(slab_ref, out_ref.at[:, pl.ds(start, width)], small_sems.at[2])
        slab_copy.start()
        gc_ref[...] += scale_c * carry_pass(
            False, carry_ref, sub_ref, dy_ref, b_ref, w_ref, rows_ref, None, None, base, head_dim,
            lambda g: None,
        )
        for copy in copies:
            copy.start()
        slab_copy.wait()

    for copy in copies:
        copy.wait()


def inter_cost(width, span, passes):
    return pl.CostEstimate(
        flops=width * 2 * span * 256 * passes, transcendentals=0, bytes_accessed=width * span * 2 * 4
    )


def inter_own(head_dim, length, b, c, w, rows, x, dy, one, two, subs, mix, parts):
    states = b.shape[0]
    span, width = x.shape[0], x.shape[1] // 2
    small = jax.ShapeDtypeStruct((states, span), F32)
    args = [b, c, w, rows, x, dy, one, two, subs, mix, *parts]
    return pl.pallas_call(
        functools.partial(inter_own_kernel, head_dim, len(parts)),
        out_shape=[jax.ShapeDtypeStruct((span, width), BF16), small, small],
        in_specs=[smem()] + [whole() for _ in args],
        out_specs=[whole(), whole(), whole()],
        scratch_shapes=[pltpu.VMEM((2,) + one.shape, BF16)],
        compiler_params=pltpu.CompilerParams(vmem_limit_bytes=12 << 20),
        cost_estimate=inter_cost(width, span, 3),
        name="inter_own",
    )(length, *args)


def near_other(head_dim, b, w, rows, x, dy, carry, sub, gb, gc, slab, parts):
    span, width = slab.shape
    args = [b, w, rows, x, dy, carry, sub, gb, gc, slab, *parts]
    return pl.pallas_call(
        functools.partial(near_other_kernel, head_dim, len(parts)),
        out_shape=[
            jax.ShapeDtypeStruct(v, t)
            for v, t in (((span, 2 * width), BF16), (slab.shape, BF16), (gb.shape, F32), (gc.shape, F32))
        ],
        in_specs=[whole() for _ in args],
        out_specs=[hbm(), whole(), whole(), whole()],
        scratch_shapes=[pltpu.SemaphoreType.DMA],
        compiler_params=pltpu.CompilerParams(vmem_limit_bytes=12 << 20),
        cost_estimate=inter_cost(width, span, 2),
        name="near_other",
    )(*args)


def far_other(head_dim, scale_b, scale_c, b, w, rows, x, dy, carry, sub, gb, gc, slab, out, parts):
    span, width = slab.shape
    every = 2
    sends = width // SLAB // every
    args = [b, w, rows, x, dy, carry, sub, gb, gc, slab]
    return pl.pallas_call(
        functools.partial(far_other_kernel, head_dim, len(parts), every, scale_b, scale_c),
        out_shape=[jax.ShapeDtypeStruct(v.shape, v.dtype) for v in (out, gb, gc)],
        in_specs=[whole() for _ in args] + [hbm()] + [whole() for _ in parts],
        out_specs=[hbm(), hbm(), hbm()],
        scratch_shapes=[
            pltpu.VMEM((span, width), BF16),
            pltpu.VMEM(gb.shape, F32),
            pltpu.VMEM(gc.shape, F32),
            pltpu.SemaphoreType.DMA((sends,)),
            pltpu.SemaphoreType.DMA((3,)),
        ],
        input_output_aliases={len(args): 0},
        compiler_params=pltpu.CompilerParams(vmem_limit_bytes=12 << 20),
        cost_estimate=inter_cost(width, span, 2),
        name="far_other",
    )(*args, out, *parts)


def local(inputs, out_grad, step_size, log_decay, b_matrix, c_matrix, skip_gain, lengths):
    x, dy = inputs[0], out_grad[0]
    tokens, columns = x.shape
    heads = step_size.shape[1]
    states = b_matrix.shape[1]
    head_dim = columns // heads
    count = lax.axis_size("seq")
    units = count // 2
    if tokens != SPAN or count % 4:
        raise ValueError("unsupported sizes")
    scale_b = 1.0 / math.sqrt(columns)
    scale_c = math.sqrt(states / (columns * count * tokens))
    def swap(v, bit):
        return lax.ppermute(v, "seq", [(i, i ^ bit) for i in range(count)])

    fixed = lambda v: pltpu.with_memory_space_constraint(v, pltpu.HBM)
    small = [fixed(v) for v in (log_decay[0], step_size[0], b_matrix[0], c_matrix[0])]
    msg, sub1_other, ld, dt, b, c, *other = first_part(lengths, *small, fixed(x), fixed(dy))
    y1 = swap(msg, 1)
    xs, subs, send, sub2_other, d, cb, *tables = own_part(
        lengths, skip_gain, ld, dt, b, c, other, x, dy
    )
    own, other = tables[:5], other + tables[5:]
    calls = 3
    pairs = heads // 4 // calls
    parts = {OTHER: [], OWN: []}

    def block(rel, k, mix, after=()):
        table = own if rel == OWN else other
        part, mix = intra(
            rel, k * pairs, pairs, head_dim, lengths, table[2], table[3], cb, table[4], x, dy, mix, after
        )
        parts[rel].append(part)
        return mix

    tile = xs.shape[1:]
    order = [(OWN, 0), (OWN, 1), (OWN, 2), (OTHER, 0), (OTHER, 1), (OTHER, 2)]
    mix = block(*order[0], None)
    if units == 4:
        (m1,) = small_call(
            functools.partial(total_kernel, False), "total", [msg.shape], d.shape, 1,
            [y1, d, xs, y1], [mix],
        )
        r1 = swap(m1, 2)
        y2 = swap(send, 1)
        mix = block(*order[1], mix, [m1])
        mix = block(*order[2], mix)
        far, own1, send1 = small_call(
            near_kernel, "near", [tile] * 3, d.shape, 2, [y1, d, xs, y1, r1], [mix]
        )
        r3 = swap(far, 4)
        mix = block(*order[3], mix, [far])
        (m2,) = small_call(
            functools.partial(total_kernel, True), "total", [tile], d.shape, 1, [y1, d, xs, y2], [mix]
        )
        r2 = swap(m2, 2)
        got1 = swap(send1, 1)
        mix = block(*order[4], mix, [m2])
        mix = block(*order[5], mix)
        own2, send2 = small_call(
            far_kernel, "far", [tile] * 2, d.shape, 2, [y1, d, xs, y2, r1, r2, r3], [mix]
        )
    else:
        y2 = swap(send, 1)
        for item in order[1:]:
            mix = block(*item, mix)
        (own1, send1), (own2, send2) = gathered(units, d, xs[0], xs[1], y1, y2)
        got1 = swap(send1, 1)
    got2 = swap(send2, 1)
    slab, gb, gc = inter_own(
        head_dim, lengths, b, c, *own[:2], x, dy, own1, own2, subs, mix, parts[OWN]
    )
    table = other[:2]
    out, slab, gb, gc = near_other(
        head_dim, b, *table, x, dy, got1, sub1_other, gb, gc, slab, parts[OTHER]
    )
    out, gb, gc = far_other(
        head_dim, scale_b, scale_c, b, *table, x, dy, got2, sub2_other, gb, gc, slab, out, parts[OTHER]
    )
    return (out[None], gb[None], gc[None])


def gathered(units, d, x1, x2, y1, y2):
    idx = lax.axis_index("seq")
    mine, unit = idx % 2, idx // 2
    lower = unit < units // 2
    tiles = x1.shape[0]
    dp = wide_rows(y1, tiles)[:, None, :]
    d = d[:, None, :]
    ys = (y1[:tiles].astype(F32), y2.astype(F32))
    xs = (x1, x2)
    totals = [pair_total(pair_flags(k == 1), d, dp, xs[k], ys[k]) for k in range(2)]
    own_half = lambda v: jnp.take(lax.all_gather(v, "seq"), 2 * jnp.arange(units) + mine, axis=0)
    forward = own_half(jnp.where(lower, totals[0], totals[1]))
    backward = own_half(jnp.where(lower, totals[1], totals[0]))
    decays = own_half(d * dp)
    state = grad = jnp.zeros_like(x1)
    for u in range(units):
        state = jnp.where(u < unit, decays[u] * state + forward[u], state)
        v = units - 1 - u
        grad = jnp.where(v > unit, decays[v] * grad + backward[v], grad)
    carries = (jnp.where(lower, state, grad), jnp.where(lower, grad, state))
    outs = [hand_on(pair_flags(k == 1), d, dp, xs[k], ys[k], carries[k]) for k in range(2)]
    return [[v.astype(BF16) for v in pair] for pair in outs]


def solution(mesh):
    placed = (
        P("batch", "seq", None),
        P("batch", "seq", None),
        P("batch", None, "seq"),
        P("batch", None, "seq"),
        P("batch", None, "seq"),
        P("batch", None, "seq"),
        P(),
        P("batch"),
    )
    return jax.shard_map(
        local,
        mesh=mesh,
        in_specs=placed,
        out_specs=(P("batch", "seq", None), P("batch", None, "seq"), P("batch", None, "seq")),
        check_vma=False,
    )
```

time: 34.5 us -> 31.4 us (0.910)
  waiting for transfers between devices: 3.69 us -> 0.99 us
  Pallas kernels: 18.8 us -> 16.7 us
  starting transfers between devices: 10.6 us -> 12.2 us
    ppermute x6 -> x7, waiting for transfers between devices: 3.69 us -> 0.99 us  [swap(): return lax.ppermute(v, 'seq', [(i, i ^ bit) for i in range(count)])]
    pallas_call x1, Pallas kernels: 3.76 us -> 1.91 us  [own_part(): pl.pallas_call(functools.partial(own_kernel, columns // heads), out_shape...]
    ppermute x6 -> x7, starting transfers between devices: 10.6 us -> 12.2 us  [swap(): return lax.ppermute(v, 'seq', [(i, i ^ bit) for i in range(count)])]
    pallas_call x1, Pallas kernels: 3.74 us -> 2.62 us  [first_part(): pl.pallas_call(functools.partial(first_kernel, columns // heads), out_sha...]
    pallas_call x2 -> x3, Pallas kernels: 4.3 us -> 4.85 us  [the longest x1 1.93 us: far_other(): pl.pallas_call(functools.partial(far_other_kernel, head_dim, len(parts),...]
  transfers between devices with their start and end apart: 6 -> 7, of which waited for: 2 -> 1; matrix products, arithmetic and copies ran while one was open for 0% -> 0% of each run, Pallas kernels for 35% -> 38%
where the time goes in v4:
time: 31.4 us; the launch traced here: 31.3 us
  Pallas kernels  16.7 us (53%)
  starting transfers between devices  12.2 us (39%)
  between operations  1.44 us (5%)
  waiting for transfers between devices  0.99 us (3%)
    ppermute x7, starting transfers between devices, swap(): return lax.ppermute(v, 'seq', [(i, i ^ bit) for i in range(count)])  12.2 us
    pallas_call x6, Pallas kernels, intra(): pl.pallas_call(functools.partial(intra_kernel, rel, pair0, pairs, head_di...  6.88 us
    pallas_call x1, Pallas kernels, first_part(): pl.pallas_call(functools.partial(first_kernel, columns // heads), out_sha...  2.62 us
    pallas_call x1, Pallas kernels, far_other(): pl.pallas_call(functools.partial(far_other_kernel, head_dim, len(parts),...  1.93 us
    pallas_call x1, Pallas kernels, own_part(): pl.pallas_call(functools.partial(own_kernel, columns // heads), out_shape...  1.91 us
    pallas_call x1, Pallas kernels, inter_own(): pl.pallas_call(functools.partial(inter_own_kernel, head_dim, len(parts)),...  1.74 us
    pallas_call x1, Pallas kernels, near_other(): pl.pallas_call(functools.partial(near_other_kernel, head_dim, len(parts))...  1.18 us
    ppermute x7, waiting for transfers between devices, swap(): return lax.ppermute(v, 'seq', [(i, i ^ bit) for i in range(count)])  0.99 us
  transfers between devices with their start and end apart: 7, of which 1 were waited for; matrix products, arithmetic and copies ran while one was open for 0% of the time, Pallas kernels for 38%

profile of v4, /device:TPU:0, one launch (start us, length us, event | category | flops | bytes accessed | tf_op | source)
XLA Modules:
  0.0 31.3 jit_solution(2736512565131132998)
XLA Ops:
  1.3 0.0 copy-start
  1.3 0.0 copy-start.1
  1.3 0.0 copy-start.2
  1.3 2.6 %first.1 = (bf16[27,16,128]{2,1,0:T(8,128)(2,1)S(1)}, f32[24,16,128]{2,1,0:T(8,128)S(1)}, f32[96,256]{1,0:T(8,128)S(1)}, f32[96,256]{1,0:T(8,128)S(1)}, bf16[16,...) custom-call(s32[1]{0:T(128)S(6)} %copy.13.len_ref, ...), custom_call_target="tpu_custom_call" | custom-call | tf_op jit(solution)/shard_map/first/pallas_call | solution.py:200
  3.9 3.0 %collective-permute-start = (bf16[27,16,128]{2,1,0:T(8,128)(2,1)S(1)}, bf16[27,16,128]{2,1,0:T(8,128)(2,1)S(1)}, u32[]{:S(2)}, u32[]{:S(2)}) collective-permute-start(bf16[27,16,128]{2,1,0:T(8,128)(2,1)S(1)} %get-tuple-element.55), channel_id=1, source_target_pairs={{0,4},{4,0},{8,12},{12,8},{16,20},{20,16},{24,28},{28,24},{1,5},{5... | collective-permute-start | bytes 331784 | tf_op jit(solution)/shard_map/ppermute | solution.py:746
  7.0 0.0 copy-done
  7.0 0.0 copy-done.1
  7.0 0.0 copy-done.2
  7.0 1.9 %own.1 = (f32[2,24,16,128]{3,2,1,0:T(8,128)S(1)}, f32[2,24,16,128]{3,2,1,0:T(8,128)S(1)}, bf16[24,16,128]{2,1,0:T(8,128)(2,1)S(1)}, f32[24,16,128]{2,1,0:T(8,128...) custom-call(s32[1]{0:T(128)S(6)} %copy.13.len_ref, ...), custom_call_target="tpu_custom_call" | custom-call | tf_op jit(solution)/shard_map/own/pallas_call | solution.py:321
  8.9 1.1 %intra.6 = (bf16[256,1024]{1,0:T(8,128)(2,1)S(1)}, f32[2,128,128]{2,1,0:T(8,128)S(1)}) custom-call(s32[1]{0:T(128)S(6)} %copy.13.len_ref, f32[48,256]{1,0:T(8,128)S(1)} %get-tuple-element.63.row_ref, f32[256,48]{1,0:T(8,128)S(1)} %get-tuple-element.64.col_ref, f32[2,128,128]{2,1,0:T(8,128)S(1)} %get-tuple-element.65.cb_ref, ...), custom_call_target="tpu_custom_call" | custom-call | flops 268435456 | bytes 1572864 | tf_op jit(solution)/shard_map/intra/pallas_call | solution.py:473
  10.0 0.0 collective-permute-done.decay_ref.y_ref
  10.0 0.1 total.2.refs_1_
  10.1 1.9 %collective-permute-start.2 = (bf16[27,16,128]{2,1,0:T(8,128)(2,1)S(1)}, bf16[27,16,128]{2,1,0:T(8,128)(2,1)S(1)}, u32[]{:S(2)}, u32[]{:S(2)}) collective-permute-start(bf16[27,16,128]{2,1,0:T(8,128)(2,1)S(1)} %total.2.refs_1_), channel_id=1, source_target_pairs={{0,8},{4,12},{8,0},{12,4},{16,24},{20,28},{24,16},{28,20},{1,9},{5... | collective-permute-start | bytes 331784 | tf_op jit(solution)/shard_map/ppermute | solution.py:746
  12.0 1.5 %collective-permute-start.1 = (bf16[24,16,128]{2,1,0:T(8,128)(2,1)S(1)}, bf16[24,16,128]{2,1,0:T(8,128)(2,1)S(1)}, u32[]{:S(2)}, u32[]{:S(2)}) collective-permute-start(bf16[24,16,128]{2,1,0:T(8,128)(2,1)S(1)} %get-tuple-element.62), channel_id=1, source_target_pairs={{0,4},{4,0},{8,12},{12,8},{16,20},{20,16},{24,28},{28,24},{1,5},{5... | collective-permute-start | bytes 294920 | tf_op jit(solution)/shard_map/ppermute | solution.py:746
  13.5 1.1 %intra.7 = (bf16[256,1024]{1,0:T(8,128)(2,1)S(1)}, f32[2,128,128]{2,1,0:T(8,128)S(1)}) custom-call(s32[1]{0:T(128)S(6)} %copy.13.len_ref, f32[48,256]{1,0:T(8,128)S(1)} %get-tuple-element.63.row_ref, f32[256,48]{1,0:T(8,128)S(1)} %get-tuple-element.64.col_ref, f32[2,128,128]{2,1,0:T(8,128)S(1)} %get-tuple-element.65.cb_ref, ...), custom_call_target="tpu_custom_call" | custom-call | flops 268435456 | bytes 1572864 | tf_op jit(solution)/shard_map/intra/pallas_call | solution.py:473
  14.6 1.1 %intra.8 = (bf16[256,1024]{1,0:T(8,128)(2,1)S(1)}, f32[2,128,128]{2,1,0:T(8,128)S(1)}) custom-call(s32[1]{0:T(128)S(6)} %copy.13.len_ref, f32[48,256]{1,0:T(8,128)S(1)} %get-tuple-element.63.row_ref, f32[256,48]{1,0:T(8,128)S(1)} %get-tuple-element.64.col_ref, f32[2,128,128]{2,1,0:T(8,128)S(1)} %get-tuple-element.65.cb_ref, ...), custom_call_target="tpu_custom_call" | custom-call | flops 268435456 | bytes 1572864 | tf_op jit(solution)/shard_map/intra/pallas_call | solution.py:473
  15.8 0.0 collective-permute-done.2.r_ref
  15.8 0.2 near.1
  15.9 2.5 %collective-permute-start.4 = (bf16[24,16,128]{2,1,0:T(8,128)(2,1)S(1)}, bf16[24,16,128]{2,1,0:T(8,128)(2,1)S(1)}, u32[]{:S(2)}, u32[]{:S(2)}) collective-permute-start(bf16[24,16,128]{2,1,0:T(8,128)(2,1)S(1)} %get-tuple-element.72.refs_1_), channel_id=1, source_target_pairs={{0,16},{4,20},{8,24},{12,28},{16,0},{20,4},{24,8},{28,12},{1,17},{... | collective-permute-start | bytes 294920 | tf_op jit(solution)/shard_map/ppermute | solution.py:746
  18.5 1.2 %intra.9 = (bf16[256,1024]{1,0:T(8,128)(2,1)S(1)}, f32[2,128,128]{2,1,0:T(8,128)S(1)}) custom-call(s32[1]{0:T(128)S(6)} %copy.13.len_ref, f32[48,256]{1,0:T(8,128)S(1)} %get-tuple-element.59.rowo_ref.row_ref, f32[256,48]{1,0:T(8,128)S(1)} %get-tuple-element.68.col_ref, f32[2,128,128]{2,1,0:T(8,128)S(1)} %get-tuple-element.65.cb_ref, ...), custom_call_target="tpu_custom_call" | custom-call | flops 268435456 | bytes 1572864 | tf_op jit(solution)/shard_map/intra/pallas_call | solution.py:473
  19.6 0.0 collective-permute-done.1.y_ref
  19.6 0.1 total.3.refs_1_
  19.7 1.0 %collective-permute-start.3 = (bf16[24,16,128]{2,1,0:T(8,128)(2,1)S(1)}, bf16[24,16,128]{2,1,0:T(8,128)(2,1)S(1)}, u32[]{:S(2)}, u32[]{:S(2)}) collective-permute-start(bf16[24,16,128]{2,1,0:T(8,128)(2,1)S(1)} %total.3.refs_1_), channel_id=1, source_target_pairs={{0,8},{4,12},{8,0},{12,4},{16,24},{20,28},{24,16},{28,20},{1,9},{5... | collective-permute-start | bytes 294920 | tf_op jit(solution)/shard_map/ppermute | solution.py:746
  20.7 1.5 %collective-permute-start.6 = (bf16[24,16,128]{2,1,0:T(8,128)(2,1)S(1)}, bf16[24,16,128]{2,1,0:T(8,128)(2,1)S(1)}, u32[]{:S(2)}, u32[]{:S(2)}) collective-permute-start(bf16[24,16,128]{2,1,0:T(8,128)(2,1)S(1)} %get-tuple-element.78), channel_id=1, source_target_pairs={{0,4},{4,0},{8,12},{12,8},{16,20},{20,16},{24,28},{28,24},{1,5},{5... | collective-permute-start | bytes 294920 | tf_op jit(solution)/shard_map/ppermute | solution.py:746
  22.2 1.2 %intra.10 = (bf16[256,1024]{1,0:T(8,128)(2,1)S(1)}, f32[2,128,128]{2,1,0:T(8,128)S(1)}) custom-call(s32[1]{0:T(128)S(6)} %copy.13.len_ref, f32[48,256]{1,0:T(8,128)S(1)} %get-tuple-element.59.rowo_ref.row_ref, f32[256,48]{1,0:T(8,128)S(1)} %get-tuple-element.68.col_ref, f32[2,128,128]{2,1,0:T(8,128)S(1)} %get-tuple-element.65.cb_ref, ...), custom_call_target="tpu_custom_call" | custom-call | flops 268435456 | bytes 1572864 | tf_op jit(solution)/shard_map/intra/pallas_call | solution.py:473
  23.4 1.2 %intra.11 = (bf16[256,1024]{1,0:T(8,128)(2,1)S(1)}, f32[2,128,128]{2,1,0:T(8,128)S(1)}) custom-call(s32[1]{0:T(128)S(6)} %copy.13.len_ref, f32[48,256]{1,0:T(8,128)S(1)} %get-tuple-element.59.rowo_ref.row_ref, f32[256,48]{1,0:T(8,128)S(1)} %get-tuple-element.68.col_ref, f32[2,128,128]{2,1,0:T(8,128)S(1)} %get-tuple-element.65.cb_ref, ...), custom_call_target="tpu_custom_call" | custom-call | flops 268435456 | bytes 1572864 | tf_op jit(solution)/shard_map/intra/pallas_call | solution.py:473
  24.5 0.0 collective-permute-done.4.far_ref
  24.6 0.0 collective-permute-done.3.r2_ref
  24.6 0.1 far.1
  24.7 0.8 %collective-permute-start.5 = (bf16[24,16,128]{2,1,0:T(8,128)(2,1)S(1)}, bf16[24,16,128]{2,1,0:T(8,128)(2,1)S(1)}, u32[]{:S(2)}, u32[]{:S(2)}) collective-permute-start(bf16[24,16,128]{2,1,0:T(8,128)(2,1)S(1)} %get-tuple-element.76), channel_id=1, source_target_pairs={{0,4},{4,0},{8,12},{12,8},{16,20},{20,16},{24,28},{28,24},{1,5},{5... | collective-permute-start | bytes 294920 | tf_op jit(solution)/shard_map/ppermute | solution.py:746
  25.4 1.7 %inter_own.1 = (bf16[256,3072]{1,0:T(8,128)(2,1)S(1)}, f32[16,256]{1,0:T(8,128)S(1)}, f32[16,256]{1,0:T(8,128)S(1)}) custom-call(s32[1]{0:T(128)S(6)} %copy.13.len_ref, bf16[16,256]{1,0:T(8,128)(2,1)S(1)} %get-tuple-element.52.b_ref, bf16[16,256]{1,0:T(8,128)(2,1)S(1)} %get-tuple-element.58.c_ref, f32[2,48,256]{2,1,0:T(8,128)S(1)} %get-tuple-element.80.w_ref, ...), custom_call_target="tpu_custom_call" | custom-call | flops 1207959552 | bytes 6291456 | tf_op jit(solution)/shard_map/inter_own/pallas_call | solution.py:679
  27.2 0.0 collective-permute-done.6.carry_ref
  27.2 1.2 %near_other.1 = (bf16[256,6144]{1,0:T(8,128)(2,1)}, bf16[256,3072]{1,0:T(8,128)(2,1)S(1)}, f32[16,256]{1,0:T(8,128)S(1)}, f32[16,256]{1,0:T(8,128)S(1)}) custom-call(bf16[16,256]{1,0:T(8,128)(2,1)S(1)} %get-tuple-element.52.b_ref, f32[2,48,256]{2,1,0:T(8,128)S(1)} %get-tuple-element.53.wo_ref.w_ref, f32[2,24,128]{2,1,0:T(8,128)S(1)} %get-tuple-element.54.rowso_ref.rows_ref, ...), custom_call_target="tpu_custom_call" | custom-call | flops 805306368 | bytes 6291456 | tf_op jit(solution)/shard_map/near_other/pallas_call | solution.py:694
  28.4 1.0 %collective-permute-done.5.carry_ref = bf16[24,16,128]{2,1,0:T(8,128)(2,1)S(1)} collective-permute-done((bf16[24,16,128]{2,1,0:T(8,128)(2,1)S(1)}, bf16[24,16,128]{2,1,0:T(8,128)(2,1)S(1)}, u32[]{:S(2)}, u32[]{:S(2)}) %collective-permute-start.5) | collective-permute-done | bytes 98336 | tf_op jit(solution)/shard_map/ppermute | solution.py:746
  29.4 1.9 %far_other.1 = (bf16[256,6144]{1,0:T(8,128)(2,1)}, f32[16,256]{1,0:T(8,128)}, f32[16,256]{1,0:T(8,128)}) custom-call(bf16[16,256]{1,0:T(8,128)(2,1)S(1)} %get-tuple-element.52.b_ref, f32[2,48,256]{2,1,0:T(8,128)S(1)} %get-tuple-element.53.wo_ref.w_ref, f32[2,24,128]{2,1,0:T(8,128)S(1)} %get-tuple-element.54.rowso_ref.rows_ref, ...), custom_call_target="tpu_custom_call", output_to_operand_aliasing={{0}: (10, {})} | custom-call | flops 805306368 | bytes 6291456 | tf_op jit(solution)/shard_map/far_other/pallas_call | solution.py:714
Async XLA Ops:
  1.3 5.7 %copy-start = (bf16[1,256,6144]{2,1,0:T(8,128)(2,1)S(1)}, bf16[1,256,6144]{2,1,0:T(8,128)(2,1)}, u32[]{:S(2)}) copy-start(bf16[1,256,6144]{2,1,0:T(8,128)(2,1)} %param.8) | copy-start | bytes 9437188
  1.3 5.7 %copy-start.1 = (bf16[1,256,6144]{2,1,0:T(8,128)(2,1)S(1)}, bf16[1,256,6144]{2,1,0:T(8,128)(2,1)}, u32[]{:S(2)}) copy-start(bf16[1,256,6144]{2,1,0:T(8,128)(2,1)} %param.9) | copy-start | bytes 9437188
  1.3 5.7 %copy-start.2 = (f32[96]{0:T(128)S(1)}, f32[96]{0:T(128)}, u32[]{:S(2)}) copy-start(f32[96]{0:T(128)} %skip_ref.1) | copy-start | bytes 1156
  3.9 6.1 %collective-permute-start = (bf16[27,16,128]{2,1,0:T(8,128)(2,1)S(1)}, bf16[27,16,128]{2,1,0:T(8,128)(2,1)S(1)}, u32[]{:S(2)}, u32[]{:S(2)}) collective-permute-start(bf16[27,16,128]{2,1,0:T(8,128)(2,1)S(1)} %get-tuple-element.55), channel_id=1, source_target_pairs={{0,4},{4,0},{8,12},{12,8},{16,20},{20,16},{24,28},{28,24},{1,5},{5... | collective-permute-start | bytes 331784 | tf_op jit(solution)/shard_map/ppermute | solution.py:746
  10.1 5.6 %collective-permute-start.2 = (bf16[27,16,128]{2,1,0:T(8,128)(2,1)S(1)}, bf16[27,16,128]{2,1,0:T(8,128)(2,1)S(1)}, u32[]{:S(2)}, u32[]{:S(2)}) collective-permute-start(bf16[27,16,128]{2,1,0:T(8,128)(2,1)S(1)} %total.2.refs_1_), channel_id=1, source_target_pairs={{0,8},{4,12},{8,0},{12,4},{16,24},{20,28},{24,16},{28,20},{1,9},{5... | collective-permute-start | bytes 331784 | tf_op jit(solution)/shard_map/ppermute | solution.py:746
  12.0 7.6 %collective-permute-start.1 = (bf16[24,16,128]{2,1,0:T(8,128)(2,1)S(1)}, bf16[24,16,128]{2,1,0:T(8,128)(2,1)S(1)}, u32[]{:S(2)}, u32[]{:S(2)}) collective-permute-start(bf16[24,16,128]{2,1,0:T(8,128)(2,1)S(1)} %get-tuple-element.62), channel_id=1, source_target_pairs={{0,4},{4,0},{8,12},{12,8},{16,20},{20,16},{24,28},{28,24},{1,5},{5... | collective-permute-start | bytes 294920 | tf_op jit(solution)/shard_map/ppermute | solution.py:746
  15.9 8.6 %collective-permute-start.4 = (bf16[24,16,128]{2,1,0:T(8,128)(2,1)S(1)}, bf16[24,16,128]{2,1,0:T(8,128)(2,1)S(1)}, u32[]{:S(2)}, u32[]{:S(2)}) collective-permute-start(bf16[24,16,128]{2,1,0:T(8,128)(2,1)S(1)} %get-tuple-element.72.refs_1_), channel_id=1, source_target_pairs={{0,16},{4,20},{8,24},{12,28},{16,0},{20,4},{24,8},{28,12},{1,17},{... | collective-permute-start | bytes 294920 | tf_op jit(solution)/shard_map/ppermute | solution.py:746
  19.7 4.9 %collective-permute-start.3 = (bf16[24,16,128]{2,1,0:T(8,128)(2,1)S(1)}, bf16[24,16,128]{2,1,0:T(8,128)(2,1)S(1)}, u32[]{:S(2)}, u32[]{:S(2)}) collective-permute-start(bf16[24,16,128]{2,1,0:T(8,128)(2,1)S(1)} %total.3.refs_1_), channel_id=1, source_target_pairs={{0,8},{4,12},{8,0},{12,4},{16,24},{20,28},{24,16},{28,20},{1,9},{5... | collective-permute-start | bytes 294920 | tf_op jit(solution)/shard_map/ppermute | solution.py:746
  20.7 6.5 %collective-permute-start.6 = (bf16[24,16,128]{2,1,0:T(8,128)(2,1)S(1)}, bf16[24,16,128]{2,1,0:T(8,128)(2,1)S(1)}, u32[]{:S(2)}, u32[]{:S(2)}) collective-permute-start(bf16[24,16,128]{2,1,0:T(8,128)(2,1)S(1)} %get-tuple-element.78), channel_id=1, source_target_pairs={{0,4},{4,0},{8,12},{12,8},{16,20},{20,16},{24,28},{28,24},{1,5},{5... | collective-permute-start | bytes 294920 | tf_op jit(solution)/shard_map/ppermute | solution.py:746
  24.7 4.7 %collective-permute-start.5 = (bf16[24,16,128]{2,1,0:T(8,128)(2,1)S(1)}, bf16[24,16,128]{2,1,0:T(8,128)(2,1)S(1)}, u32[]{:S(2)}, u32[]{:S(2)}) collective-permute-start(bf16[24,16,128]{2,1,0:T(8,128)(2,1)S(1)} %get-tuple-element.76), channel_id=1, source_target_pairs={{0,4},{4,0},{8,12},{12,8},{16,20},{20,16},{24,28},{28,24},{1,5},{5... | collective-permute-start | bytes 294920 | tf_op jit(solution)/shard_map/ppermute | solution.py:746

commit v5 on v4

--- a/solution.py
+++ b/solution.py
@@ -7,6 +7,7 @@
 from jax.experimental import pallas as pl
 from jax.experimental.pallas import tpu as pltpu
 from jax.sharding import PartitionSpec as P
+
 
 SPAN = 256
 LANES = 128
@@ -71,7 +72,7 @@
 
 def weights(ld, dt, valid):
     cum = running_sum(ld)
-    rows, span = cum.shape
+    _, span = cum.shape
     sub = span // 2
     end_a, end_b = cum[:, sub - 1 : sub], cum[:, span - 1 : span]
     ends = jnp.where(iota(cum.shape, 1) < sub, end_a, end_b)
@@ -333,7 +334,7 @@
 
 
 def pair_flags(second):
-    idx, mine, lower = place()
+    _, mine, lower = place()
     ahead = jnp.where(lower, mine == 0, mine == 1)
     return jnp.logical_not(ahead) if second else ahead
 
@@ -415,7 +416,7 @@
         send_ref[j] = send.astype(BF16)
 
 
-def small_call(kernel, name, outs, rows_shape, scratch, args, after=()):
+def small_call(kernel, outs, rows_shape, scratch, args, after=()):
     return pl.pallas_call(
         kernel,
         out_shape=[jax.ShapeDtypeStruct(o, BF16) for o in outs],
@@ -423,15 +424,14 @@
         out_specs=[whole() for _ in outs],
         scratch_shapes=[pltpu.VMEM(rows_shape, F32)] * scratch,
         compiler_params=pltpu.CompilerParams(vmem_limit_bytes=4 << 20),
-        name=name,
     )(*args, *after)
 
 
 def intra_kernel(rel, pair0, pairs, head_dim, first, len_ref, row_ref, col_ref, cb_ref, skip_ref, x_ref, dy_ref, *refs):
     mix_in = None if first else refs[0]
-    part_ref, mix_ref = refs[-2:]
+    part_ref, mix_ref, split_ref = refs[-3:]
     sub = cb_ref.shape[1]
-    idx, mine, lower = place()
+    idx, mine, _ = place()
     base = (mine if rel == OWN else 1 - mine) * (x_ref.shape[1] // 2)
     valid = len_ref[0] - idx * x_ref.shape[0]
     lane = iota((1, LANES), 1)
@@ -447,8 +447,9 @@
             cols = pl.ds(pl.multiple_of(base + (pair0 + p) * LANES, LANES), LANES)
             xs = x_ref[here, cols]
             ys = dy_ref[here, cols]
-            split = jnp.concatenate([ys * keep[0], ys * keep[1]], axis=0)
-            scores = mm(xs, split, NT)
+            split_ref[p % 2, :sub, :] = ys * keep[0]
+            split_ref[p % 2, sub:, :] = ys * keep[1]
+            scores = mm(xs, split_ref[p % 2], NT)
             kernels = []
             for j in range(2):
                 h = 2 * (pair0 + p) + j
@@ -458,7 +459,7 @@
                 kernels.append((decay * cb_ref[s]).astype(BF16))
                 term = decay * scores[:, j * sub : (j + 1) * sub]
                 acc = term if acc is None else acc + term
-            within = mm(jnp.concatenate(kernels, axis=1), split)
+            within = mm(jnp.concatenate(kernels, axis=1), split_ref[p % 2])
             skip = skip_ref[pl.ds(pair0 + p, 1), :]
             part_ref[here, pl.ds(p * LANES, LANES)] = (
                 within + jnp.where(inside, skip * ys.astype(F32), 0.0)
@@ -478,6 +479,7 @@
         ],
         in_specs=[smem()] + [whole() for _ in args] + [pl.BlockSpec(memory_space=pl.ANY) for _ in after],
         out_specs=[whole(), whole()],
+        scratch_shapes=[pltpu.VMEM((2, span, LANES), BF16)],
         compiler_params=pltpu.CompilerParams(vmem_limit_bytes=8 << 20),
         cost_estimate=pl.CostEstimate(
             flops=heads * 2 * span * span * 128,
@@ -594,7 +596,7 @@
 def near_other_kernel(
     head_dim, slabs, b_ref, w_ref, rows_ref, x_ref, dy_ref, carry_ref, sub_ref, gb_in, gc_in, slab_ref, *refs
 ):
-    idx, mine, lower = place()
+    _, mine, lower = place()
     parts = refs[:slabs]
     out_ref, buf_ref, gb_ref, gc_ref, sem = refs[slabs:]
     width = x_ref.shape[1] // 2
@@ -626,7 +628,7 @@
     head_dim, slabs, every, scale_b, scale_c, b_ref, w_ref, rows_ref, x_ref, dy_ref, carry_ref, sub_ref,
     gb_in, gc_in, slab_ref, out_in, *refs
 ):
-    idx, mine, lower = place()
+    _, mine, lower = place()
     parts = refs[:slabs]
     out_ref, gb_out, gc_out, buf_ref, gb_ref, gc_ref, sems, small_sems = refs[slabs:]
     width = x_ref.shape[1] // 2
@@ -708,7 +710,7 @@
 
 def far_other(head_dim, scale_b, scale_c, b, w, rows, x, dy, carry, sub, gb, gc, slab, out, parts):
     span, width = slab.shape
-    every = 2
+    every = 1
     sends = width // SLAB // every
     args = [b, w, rows, x, dy, carry, sub, gb, gc, slab]
     return pl.pallas_call(
@@ -730,7 +732,7 @@
     )(*args, out, *parts)
 
 
-def local(inputs, out_grad, step_size, log_decay, b_matrix, c_matrix, skip_gain, lengths):
+def device_work(inputs, out_grad, step_size, log_decay, b_matrix, c_matrix, skip_gain, lengths):
     x, dy = inputs[0], out_grad[0]
     tokens, columns = x.shape
     heads = step_size.shape[1]
@@ -742,6 +744,7 @@
         raise ValueError("unsupported sizes")
     scale_b = 1.0 / math.sqrt(columns)
     scale_c = math.sqrt(states / (columns * count * tokens))
+
     def swap(v, bit):
         return lax.ppermute(v, "seq", [(i, i ^ bit) for i in range(count)])
 
@@ -753,7 +756,7 @@
         lengths, skip_gain, ld, dt, b, c, other, x, dy
     )
     own, other = tables[:5], other + tables[5:]
-    calls = 3
+    calls = 6
     pairs = heads // 4 // calls
     parts = {OTHER: [], OWN: []}
 
@@ -766,36 +769,33 @@
         return mix
 
     tile = xs.shape[1:]
-    order = [(OWN, 0), (OWN, 1), (OWN, 2), (OTHER, 0), (OTHER, 1), (OTHER, 2)]
-    mix = block(*order[0], None)
+    order = [(rel, k) for rel in (OWN, OTHER) for k in range(calls)]
+
+    def run(count, mix, after=()):
+        for _ in range(count):
+            mix = block(*order.pop(0), mix, after)
+            after = ()
+        return mix
+
+    mix = run(3, None)
     if units == 4:
         (m1,) = small_call(
-            functools.partial(total_kernel, False), "total", [msg.shape], d.shape, 1,
+            functools.partial(total_kernel, False), [msg.shape], d.shape, 1,
             [y1, d, xs, y1], [mix],
         )
         r1 = swap(m1, 2)
         y2 = swap(send, 1)
-        mix = block(*order[1], mix, [m1])
-        mix = block(*order[2], mix)
-        far, own1, send1 = small_call(
-            near_kernel, "near", [tile] * 3, d.shape, 2, [y1, d, xs, y1, r1], [mix]
-        )
+        mix = run(4, mix, [m1])
+        far, own1, send1 = small_call(near_kernel, [tile] * 3, d.shape, 2, [y1, d, xs, y1, r1], [mix])
         r3 = swap(far, 4)
-        mix = block(*order[3], mix, [far])
-        (m2,) = small_call(
-            functools.partial(total_kernel, True), "total", [tile], d.shape, 1, [y1, d, xs, y2], [mix]
-        )
+        (m2,) = small_call(functools.partial(total_kernel, True), [tile], d.shape, 1, [y1, d, xs, y2], [far])
         r2 = swap(m2, 2)
         got1 = swap(send1, 1)
-        mix = block(*order[4], mix, [m2])
-        mix = block(*order[5], mix)
-        own2, send2 = small_call(
-            far_kernel, "far", [tile] * 2, d.shape, 2, [y1, d, xs, y2, r1, r2, r3], [mix]
-        )
+        mix = run(5, mix, [m2])
+        own2, send2 = small_call(far_kernel, [tile] * 2, d.shape, 2, [y1, d, xs, y2, r1, r2, r3], [mix])
     else:
         y2 = swap(send, 1)
-        for item in order[1:]:
-            mix = block(*item, mix)
+        mix = run(len(order), mix)
         (own1, send1), (own2, send2) = gathered(units, d, xs[0], xs[1], y1, y2)
         got1 = swap(send1, 1)
     got2 = swap(send2, 1)
@@ -848,7 +848,7 @@
         P("batch"),
     )
     return jax.shard_map(
-        local,
+        device_work,
         mesh=mesh,
         in_specs=placed,
         out_specs=(P("batch", "seq", None), P("batch", None, "seq"), P("batch", None, "seq")),

time: 31.4 us -> 31.4 us (level)
  starting transfers between devices: 12.2 us -> 10.7 us
  Pallas kernels: 16.7 us -> 17.5 us
  waiting for transfers between devices: 0.99 us -> 1.41 us
    ppermute x7, starting transfers between devices: 12.2 us -> 10.7 us  [swap(): return lax.ppermute(v, 'seq', [(i, i ^ bit) for i in range(count)])]
    pallas_call x6 -> x12, Pallas kernels: 6.88 us -> 7.53 us  [intra(): pl.pallas_call(functools.partial(intra_kernel, rel, pair0, pairs, head_di...]
    ppermute x7, waiting for transfers between devices: 0.99 us -> 1.41 us  [swap(): return lax.ppermute(v, 'seq', [(i, i ^ bit) for i in range(count)])]
  transfers between devices with their start and end apart: 7 -> 7, of which waited for: 1 -> 2; matrix products, arithmetic and copies ran while one was open for 0% -> 0% of each run, Pallas kernels for 38% -> 41%
where the time goes in v5:
time: 31.4 us; the launch traced here: 31.2 us
  Pallas kernels  17.5 us (56%)
  starting transfers between devices  10.7 us (34%)
  between operations  1.6 us (5%)
  waiting for transfers between devices  1.41 us (4%)
    ppermute x7, starting transfers between devices, swap(): return lax.ppermute(v, 'seq', [(i, i ^ bit) for i in range(count)])  10.7 us
    pallas_call x12, Pallas kernels, intra(): pl.pallas_call(functools.partial(intra_kernel, rel, pair0, pairs, head_di...  7.53 us
    pallas_call x1, Pallas kernels, first_part(): pl.pallas_call(functools.partial(first_kernel, columns // heads), out_sha...  2.62 us
    pallas_call x1, Pallas kernels, far_other(): pl.pallas_call(functools.partial(far_other_kernel, head_dim, len(parts),...  1.93 us
    pallas_call x1, Pallas kernels, own_part(): pl.pallas_call(functools.partial(own_kernel, columns // heads), out_shape...  1.9 us
    pallas_call x1, Pallas kernels, inter_own(): pl.pallas_call(functools.partial(inter_own_kernel, head_dim, len(parts)),...  1.74 us
    ppermute x7, waiting for transfers between devices, swap(): return lax.ppermute(v, 'seq', [(i, i ^ bit) for i in range(count)])  1.41 us
    pallas_call x1, Pallas kernels, near_other(): pl.pallas_call(functools.partial(near_other_kernel, head_dim, len(parts))...  1.36 us
  transfers between devices with their start and end apart: 7, of which 2 were waited for; matrix products, arithmetic and copies ran while one was open for 0% of the time, Pallas kernels for 41%

profile of v5, /device:TPU:0, one launch (start us, length us, event | category | flops | bytes accessed | tf_op | source)
XLA Modules:
  0.0 31.2 jit_solution(9628340438689292270)
XLA Ops:
  1.3 0.0 copy-start
  1.3 0.0 copy-start.1
  1.3 0.0 copy-start.2
  1.3 2.6 %first.1 = (bf16[27,16,128]{2,1,0:T(8,128)(2,1)S(1)}, f32[24,16,128]{2,1,0:T(8,128)S(1)}, f32[96,256]{1,0:T(8,128)S(1)}, f32[96,256]{1,0:T(8,128)S(1)}, bf16[16,...) custom-call(s32[1]{0:T(128)S(6)} %copy.13.len_ref, ...), custom_call_target="tpu_custom_call" | custom-call | tf_op jit(solution)/shard_map/first/pallas_call | solution.py:201
  3.9 3.0 %collective-permute-start = (bf16[27,16,128]{2,1,0:T(8,128)(2,1)S(1)}, bf16[27,16,128]{2,1,0:T(8,128)(2,1)S(1)}, u32[]{:S(2)}, u32[]{:S(2)}) collective-permute-start(bf16[27,16,128]{2,1,0:T(8,128)(2,1)S(1)} %get-tuple-element.67), channel_id=1, source_target_pairs={{0,4},{4,0},{8,12},{12,8},{16,20},{20,16},{24,28},{28,24},{1,5},{5... | collective-permute-start | bytes 331784 | tf_op jit(solution)/shard_map/ppermute | solution.py:749
  7.0 0.0 copy-done
  7.0 0.0 copy-done.1
  7.0 0.0 copy-done.2
  7.0 1.9 %own.1 = (f32[2,24,16,128]{3,2,1,0:T(8,128)S(1)}, f32[2,24,16,128]{3,2,1,0:T(8,128)S(1)}, bf16[24,16,128]{2,1,0:T(8,128)(2,1)S(1)}, f32[24,16,128]{2,1,0:T(8,128...) custom-call(s32[1]{0:T(128)S(6)} %copy.13.len_ref, ...), custom_call_target="tpu_custom_call" | custom-call | tf_op jit(solution)/shard_map/own/pallas_call | solution.py:322
  8.9 0.6 %intra.12 = (bf16[256,512]{1,0:T(8,128)(2,1)S(1)}, f32[2,128,128]{2,1,0:T(8,128)S(1)}) custom-call(s32[1]{0:T(128)S(6)} %copy.13.len_ref, f32[48,256]{1,0:T(8,128)S(1)} %get-tuple-element.75.row_ref, f32[256,48]{1,0:T(8,128)S(1)} %get-tuple-element.76.col_ref, f32[2,128,128]{2,1,0:T(8,128)S(1)} %get-tuple-element.77.cb_ref, ...), custom_call_target="tpu_custom_call" | custom-call | flops 134217728 | bytes 786432 | tf_op jit(solution)/shard_map/intra/pallas_call | solution.py:474
  9.5 0.6 %intra.13 = (bf16[256,512]{1,0:T(8,128)(2,1)S(1)}, f32[2,128,128]{2,1,0:T(8,128)S(1)}) custom-call(s32[1]{0:T(128)S(6)} %copy.13.len_ref, f32[48,256]{1,0:T(8,128)S(1)} %get-tuple-element.75.row_ref, f32[256,48]{1,0:T(8,128)S(1)} %get-tuple-element.76.col_ref, f32[2,128,128]{2,1,0:T(8,128)S(1)} %get-tuple-element.77.cb_ref, ...), custom_call_target="tpu_custom_call" | custom-call | flops 134217728 | bytes 786432 | tf_op jit(solution)/shard_map/intra/pallas_call | solution.py:474
  10.1 0.6 %intra.14 = (bf16[256,512]{1,0:T(8,128)(2,1)S(1)}, f32[2,128,128]{2,1,0:T(8,128)S(1)}) custom-call(s32[1]{0:T(128)S(6)} %copy.13.len_ref, f32[48,256]{1,0:T(8,128)S(1)} %get-tuple-element.75.row_ref, f32[256,48]{1,0:T(8,128)S(1)} %get-tuple-element.76.col_ref, f32[2,128,128]{2,1,0:T(8,128)S(1)} %get-tuple-element.77.cb_ref, ...), custom_call_target="tpu_custom_call" | custom-call | flops 134217728 | bytes 786432 | tf_op jit(solution)/shard_map/intra/pallas_call | solution.py:474
  10.8 0.0 collective-permute-done.decay_ref.y_ref
  10.8 0.1 shard_map.103.refs_1_
  10.8 1.6 %collective-permute-start.2 = (bf16[27,16,128]{2,1,0:T(8,128)(2,1)S(1)}, bf16[27,16,128]{2,1,0:T(8,128)(2,1)S(1)}, u32[]{:S(2)}, u32[]{:S(2)}) collective-permute-start(bf16[27,16,128]{2,1,0:T(8,128)(2,1)S(1)} %shard_map.103.refs_1_), channel_id=1, source_target_pairs={{0,8},{4,12},{8,0},{12,4},{16,24},{20,28},{24,16},{28,20},{1,9},{5... | collective-permute-start | bytes 331784 | tf_op jit(solution)/shard_map/ppermute | solution.py:749
  12.5 1.0 %collective-permute-start.1 = (bf16[24,16,128]{2,1,0:T(8,128)(2,1)S(1)}, bf16[24,16,128]{2,1,0:T(8,128)(2,1)S(1)}, u32[]{:S(2)}, u32[]{:S(2)}) collective-permute-start(bf16[24,16,128]{2,1,0:T(8,128)(2,1)S(1)} %get-tuple-element.74), channel_id=1, source_target_pairs={{0,4},{4,0},{8,12},{12,8},{16,20},{20,16},{24,28},{28,24},{1,5},{5... | collective-permute-start | bytes 294920 | tf_op jit(solution)/shard_map/ppermute | solution.py:749
  13.5 0.6 %intra.15 = (bf16[256,512]{1,0:T(8,128)(2,1)S(1)}, f32[2,128,128]{2,1,0:T(8,128)S(1)}) custom-call(s32[1]{0:T(128)S(6)} %copy.13.len_ref, f32[48,256]{1,0:T(8,128)S(1)} %get-tuple-element.75.row_ref, f32[256,48]{1,0:T(8,128)S(1)} %get-tuple-element.76.col_ref, f32[2,128,128]{2,1,0:T(8,128)S(1)} %get-tuple-element.77.cb_ref, ...), custom_call_target="tpu_custom_call" | custom-call | flops 134217728 | bytes 786432 | tf_op jit(solution)/shard_map/intra/pallas_call | solution.py:474
  14.1 0.6 %intra.16 = (bf16[256,512]{1,0:T(8,128)(2,1)S(1)}, f32[2,128,128]{2,1,0:T(8,128)S(1)}) custom-call(s32[1]{0:T(128)S(6)} %copy.13.len_ref, f32[48,256]{1,0:T(8,128)S(1)} %get-tuple-element.75.row_ref, f32[256,48]{1,0:T(8,128)S(1)} %get-tuple-element.76.col_ref, f32[2,128,128]{2,1,0:T(8,128)S(1)} %get-tuple-element.77.cb_ref, ...), custom_call_target="tpu_custom_call" | custom-call | flops 134217728 | bytes 786432 | tf_op jit(solution)/shard_map/intra/pallas_call | solution.py:474
  14.7 0.6 %intra.17 = (bf16[256,512]{1,0:T(8,128)(2,1)S(1)}, f32[2,128,128]{2,1,0:T(8,128)S(1)}) custom-call(s32[1]{0:T(128)S(6)} %copy.13.len_ref, f32[48,256]{1,0:T(8,128)S(1)} %get-tuple-element.75.row_ref, f32[256,48]{1,0:T(8,128)S(1)} %get-tuple-element.76.col_ref, f32[2,128,128]{2,1,0:T(8,128)S(1)} %get-tuple-element.77.cb_ref, ...), custom_call_target="tpu_custom_call" | custom-call | flops 134217728 | bytes 786432 | tf_op jit(solution)/shard_map/intra/pallas_call | solution.py:474
  15.3 0.6 %intra.18 = (bf16[256,512]{1,0:T(8,128)(2,1)S(1)}, f32[2,128,128]{2,1,0:T(8,128)S(1)}) custom-call(s32[1]{0:T(128)S(6)} %copy.13.len_ref, f32[48,256]{1,0:T(8,128)S(1)} %get-tuple-element.71.rowo_ref.row_ref, f32[256,48]{1,0:T(8,128)S(1)} %get-tuple-element.82.col_ref, f32[2,128,128]{2,1,0:T(8,128)S(1)} %get-tuple-element.77.cb_ref, ...), custom_call_target="tpu_custom_call" | custom-call | flops 134217728 | bytes 786432 | tf_op jit(solution)/shard_map/intra/pallas_call | solution.py:474
  16.0 0.0 collective-permute-done.2.r_ref
  16.0 0.2 shard_map.104
  16.1 1.0 %collective-permute-done.1.y_ref = bf16[24,16,128]{2,1,0:T(8,128)(2,1)S(1)} collective-permute-done((bf16[24,16,128]{2,1,0:T(8,128)(2,1)S(1)}, bf16[24,16,128]{2,1,0:T(8,128)(2,1)S(1)}, u32[]{:S(2)}, u32[]{:S(2)}) %collective-permute-start.1) | collective-permute-done | bytes 98336 | tf_op jit(solution)/shard_map/ppermute | solution.py:749
  17.1 0.1 shard_map.105.refs_1_
  17.2 0.5 %collective-permute-start.3 = (bf16[24,16,128]{2,1,0:T(8,128)(2,1)S(1)}, bf16[24,16,128]{2,1,0:T(8,128)(2,1)S(1)}, u32[]{:S(2)}, u32[]{:S(2)}) collective-permute-start(bf16[24,16,128]{2,1,0:T(8,128)(2,1)S(1)} %shard_map.105.refs_1_), channel_id=1, source_target_pairs={{0,8},{4,12},{8,0},{12,4},{16,24},{20,28},{24,16},{28,20},{1,9},{5... | collective-permute-start | bytes 294920 | tf_op jit(solution)/shard_map/ppermute | solution.py:749
  17.7 2.5 %collective-permute-start.4 = (bf16[24,16,128]{2,1,0:T(8,128)(2,1)S(1)}, bf16[24,16,128]{2,1,0:T(8,128)(2,1)S(1)}, u32[]{:S(2)}, u32[]{:S(2)}) collective-permute-start(bf16[24,16,128]{2,1,0:T(8,128)(2,1)S(1)} %get-tuple-element.88.refs_0_), channel_id=1, source_target_pairs={{0,16},{4,20},{8,24},{12,28},{16,0},{20,4},{24,8},{28,12},{1,17},{... | collective-permute-start | bytes 294920 | tf_op jit(solution)/shard_map/ppermute | solution.py:749
  20.2 1.0 %collective-permute-start.6 = (bf16[24,16,128]{2,1,0:T(8,128)(2,1)S(1)}, bf16[24,16,128]{2,1,0:T(8,128)(2,1)S(1)}, u32[]{:S(2)}, u32[]{:S(2)}) collective-permute-start(bf16[24,16,128]{2,1,0:T(8,128)(2,1)S(1)} %get-tuple-element.96), channel_id=1, source_target_pairs={{0,4},{4,0},{8,12},{12,8},{16,20},{20,16},{24,28},{28,24},{1,5},{5... | collective-permute-start | bytes 294920 | tf_op jit(solution)/shard_map/ppermute | solution.py:749
  21.1 0.6 %intra.19 = (bf16[256,512]{1,0:T(8,128)(2,1)S(1)}, f32[2,128,128]{2,1,0:T(8,128)S(1)}) custom-call(s32[1]{0:T(128)S(6)} %copy.13.len_ref, f32[48,256]{1,0:T(8,128)S(1)} %get-tuple-element.71.rowo_ref.row_ref, f32[256,48]{1,0:T(8,128)S(1)} %get-tuple-element.82.col_ref, f32[2,128,128]{2,1,0:T(8,128)S(1)} %get-tuple-element.77.cb_ref, ...), custom_call_target="tpu_custom_call" | custom-call | flops 134217728 | bytes 786432 | tf_op jit(solution)/shard_map/intra/pallas_call | solution.py:474
  21.8 0.6 %intra.20 = (bf16[256,512]{1,0:T(8,128)(2,1)S(1)}, f32[2,128,128]{2,1,0:T(8,128)S(1)}) custom-call(s32[1]{0:T(128)S(6)} %copy.13.len_ref, f32[48,256]{1,0:T(8,128)S(1)} %get-tuple-element.71.rowo_ref.row_ref, f32[256,48]{1,0:T(8,128)S(1)} %get-tuple-element.82.col_ref, f32[2,128,128]{2,1,0:T(8,128)S(1)} %get-tuple-element.77.cb_ref, ...), custom_call_target="tpu_custom_call" | custom-call | flops 134217728 | bytes 786432 | tf_op jit(solution)/shard_map/intra/pallas_call | solution.py:474
  22.4 0.6 %intra.21 = (bf16[256,512]{1,0:T(8,128)(2,1)S(1)}, f32[2,128,128]{2,1,0:T(8,128)S(1)}) custom-call(s32[1]{0:T(128)S(6)} %copy.13.len_ref, f32[48,256]{1,0:T(8,128)S(1)} %get-tuple-element.71.rowo_ref.row_ref, f32[256,48]{1,0:T(8,128)S(1)} %get-tuple-element.82.col_ref, f32[2,128,128]{2,1,0:T(8,128)S(1)} %get-tuple-element.77.cb_ref, ...), custom_call_target="tpu_custom_call" | custom-call | flops 134217728 | bytes 786432 | tf_op jit(solution)/shard_map/intra/pallas_call | solution.py:474
  23.0 0.6 %intra.22 = (bf16[256,512]{1,0:T(8,128)(2,1)S(1)}, f32[2,128,128]{2,1,0:T(8,128)S(1)}) custom-call(s32[1]{0:T(128)S(6)} %copy.13.len_ref, f32[48,256]{1,0:T(8,128)S(1)} %get-tuple-element.71.rowo_ref.row_ref, f32[256,48]{1,0:T(8,128)S(1)} %get-tuple-element.82.col_ref, f32[2,128,128]{2,1,0:T(8,128)S(1)} %get-tuple-element.77.cb_ref, ...), custom_call_target="tpu_custom_call" | custom-call | flops 134217728 | bytes 786432 | tf_op jit(solution)/shard_map/intra/pallas_call | solution.py:474
  23.7 0.6 %intra.23 = (bf16[256,512]{1,0:T(8,128)(2,1)S(1)}, f32[2,128,128]{2,1,0:T(8,128)S(1)}) custom-call(s32[1]{0:T(128)S(6)} %copy.13.len_ref, f32[48,256]{1,0:T(8,128)S(1)} %get-tuple-element.71.rowo_ref.row_ref, f32[256,48]{1,0:T(8,128)S(1)} %get-tuple-element.82.col_ref, f32[2,128,128]{2,1,0:T(8,128)S(1)} %get-tuple-element.77.cb_ref, ...), custom_call_target="tpu_custom_call" | custom-call | flops 134217728 | bytes 786432 | tf_op jit(solution)/shard_map/intra/pallas_call | solution.py:474
  24.3 0.0 collective-permute-done.3.r2_ref
  24.3 0.0 collective-permute-done.4.far_ref
  24.3 0.1 shard_map.106
  24.5 1.1 %collective-permute-start.5 = (bf16[24,16,128]{2,1,0:T(8,128)(2,1)S(1)}, bf16[24,16,128]{2,1,0:T(8,128)(2,1)S(1)}, u32[]{:S(2)}, u32[]{:S(2)}) collective-permute-start(bf16[24,16,128]{2,1,0:T(8,128)(2,1)S(1)} %get-tuple-element.94), channel_id=1, source_target_pairs={{0,4},{4,0},{8,12},{12,8},{16,20},{20,16},{24,28},{28,24},{1,5},{5... | collective-permute-start | bytes 294920 | tf_op jit(solution)/shard_map/ppermute | solution.py:749
  25.6 1.7 %inter_own.1 = (bf16[256,3072]{1,0:T(8,128)(2,1)S(1)}, f32[16,256]{1,0:T(8,128)S(1)}, f32[16,256]{1,0:T(8,128)S(1)}) custom-call(s32[1]{0:T(128)S(6)} %copy.13.len_ref, bf16[16,256]{1,0:T(8,128)(2,1)S(1)} %get-tuple-element.64.b_ref, bf16[16,256]{1,0:T(8,128)(2,1)S(1)} %get-tuple-element.70.c_ref, f32[2,48,256]{2,1,0:T(8,128)S(1)} %get-tuple-element.98.w_ref, ...), custom_call_target="tpu_custom_call" | custom-call | flops 1207959552 | bytes 6291456 | tf_op jit(solution)/shard_map/inter_own/pallas_call | solution.py:681
  27.3 0.0 collective-permute-done.6.carry_ref
  27.3 1.4 %near_other.1 = (bf16[256,6144]{1,0:T(8,128)(2,1)}, bf16[256,3072]{1,0:T(8,128)(2,1)S(1)}, f32[16,256]{1,0:T(8,128)S(1)}, f32[16,256]{1,0:T(8,128)S(1)}) custom-call(bf16[16,256]{1,0:T(8,128)(2,1)S(1)} %get-tuple-element.64.b_ref, f32[2,48,256]{2,1,0:T(8,128)S(1)} %get-tuple-element.65.wo_ref.w_ref, f32[2,24,128]{2,1,0:T(8,128)S(1)} %get-tuple-element.66.rowso_ref.rows_ref, ...), custom_call_target="tpu_custom_call" | custom-call | flops 805306368 | bytes 6291456 | tf_op jit(solution)/shard_map/near_other/pallas_call | solution.py:696
  28.7 0.4 %collective-permute-done.5.carry_ref = bf16[24,16,128]{2,1,0:T(8,128)(2,1)S(1)} collective-permute-done((bf16[24,16,128]{2,1,0:T(8,128)(2,1)S(1)}, bf16[24,16,128]{2,1,0:T(8,128)(2,1)S(1)}, u32[]{:S(2)}, u32[]{:S(2)}) %collective-permute-start.5) | collective-permute-done | bytes 98336 | tf_op jit(solution)/shard_map/ppermute | solution.py:749
  29.1 1.9 %far_other.1 = (bf16[256,6144]{1,0:T(8,128)(2,1)}, f32[16,256]{1,0:T(8,128)}, f32[16,256]{1,0:T(8,128)}) custom-call(bf16[16,256]{1,0:T(8,128)(2,1)S(1)} %get-tuple-element.64.b_ref, f32[2,48,256]{2,1,0:T(8,128)S(1)} %get-tuple-element.65.wo_ref.w_ref, f32[2,24,128]{2,1,0:T(8,128)S(1)} %get-tuple-element.66.rowso_ref.rows_ref, ...), custom_call_target="tpu_custom_call", output_to_operand_aliasing={{0}: (10, {})} | custom-call | flops 805306368 | bytes 6291456 | tf_op jit(solution)/shard_map/far_other/pallas_call | solution.py:716
Async XLA Ops:
  1.3 5.7 %copy-start = (bf16[1,256,6144]{2,1,0:T(8,128)(2,1)S(1)}, bf16[1,256,6144]{2,1,0:T(8,128)(2,1)}, u32[]{:S(2)}) copy-start(bf16[1,256,6144]{2,1,0:T(8,128)(2,1)} %param.8) | copy-start | bytes 9437188
  1.3 5.7 %copy-start.1 = (bf16[1,256,6144]{2,1,0:T(8,128)(2,1)S(1)}, bf16[1,256,6144]{2,1,0:T(8,128)(2,1)}, u32[]{:S(2)}) copy-start(bf16[1,256,6144]{2,1,0:T(8,128)(2,1)} %param.9) | copy-start | bytes 9437188
  1.3 5.7 %copy-start.2 = (f32[96]{0:T(128)S(1)}, f32[96]{0:T(128)}, u32[]{:S(2)}) copy-start(f32[96]{0:T(128)} %skip_ref.1) | copy-start | bytes 1156
  3.9 6.8 %collective-permute-start = (bf16[27,16,128]{2,1,0:T(8,128)(2,1)S(1)}, bf16[27,16,128]{2,1,0:T(8,128)(2,1)S(1)}, u32[]{:S(2)}, u32[]{:S(2)}) collective-permute-start(bf16[27,16,128]{2,1,0:T(8,128)(2,1)S(1)} %get-tuple-element.67), channel_id=1, source_target_pairs={{0,4},{4,0},{8,12},{12,8},{16,20},{20,16},{24,28},{28,24},{1,5},{5... | collective-permute-start | bytes 331784 | tf_op jit(solution)/shard_map/ppermute | solution.py:749
  10.8 5.1 %collective-permute-start.2 = (bf16[27,16,128]{2,1,0:T(8,128)(2,1)S(1)}, bf16[27,16,128]{2,1,0:T(8,128)(2,1)S(1)}, u32[]{:S(2)}, u32[]{:S(2)}) collective-permute-start(bf16[27,16,128]{2,1,0:T(8,128)(2,1)S(1)} %shard_map.103.refs_1_), channel_id=1, source_target_pairs={{0,8},{4,12},{8,0},{12,4},{16,24},{20,28},{24,16},{28,20},{1,9},{5... | collective-permute-start | bytes 331784 | tf_op jit(solution)/shard_map/ppermute | solution.py:749
  12.5 4.6 %collective-permute-start.1 = (bf16[24,16,128]{2,1,0:T(8,128)(2,1)S(1)}, bf16[24,16,128]{2,1,0:T(8,128)(2,1)S(1)}, u32[]{:S(2)}, u32[]{:S(2)}) collective-permute-start(bf16[24,16,128]{2,1,0:T(8,128)(2,1)S(1)} %get-tuple-element.74), channel_id=1, source_target_pairs={{0,4},{4,0},{8,12},{12,8},{16,20},{20,16},{24,28},{28,24},{1,5},{5... | collective-permute-start | bytes 294920 | tf_op jit(solution)/shard_map/ppermute | solution.py:749
  17.2 7.2 %collective-permute-start.3 = (bf16[24,16,128]{2,1,0:T(8,128)(2,1)S(1)}, bf16[24,16,128]{2,1,0:T(8,128)(2,1)S(1)}, u32[]{:S(2)}, u32[]{:S(2)}) collective-permute-start(bf16[24,16,128]{2,1,0:T(8,128)(2,1)S(1)} %shard_map.105.refs_1_), channel_id=1, source_target_pairs={{0,8},{4,12},{8,0},{12,4},{16,24},{20,28},{24,16},{28,20},{1,9},{5... | collective-permute-start | bytes 294920 | tf_op jit(solution)/shard_map/ppermute | solution.py:749
  17.7 6.7 %collective-permute-start.4 = (bf16[24,16,128]{2,1,0:T(8,128)(2,1)S(1)}, bf16[24,16,128]{2,1,0:T(8,128)(2,1)S(1)}, u32[]{:S(2)}, u32[]{:S(2)}) collective-permute-start(bf16[24,16,128]{2,1,0:T(8,128)(2,1)S(1)} %get-tuple-element.88.refs_0_), channel_id=1, source_target_pairs={{0,16},{4,20},{8,24},{12,28},{16,0},{20,4},{24,8},{28,12},{1,17},{... | collective-permute-start | bytes 294920 | tf_op jit(solution)/shard_map/ppermute | solution.py:749
  20.2 7.1 %collective-permute-start.6 = (bf16[24,16,128]{2,1,0:T(8,128)(2,1)S(1)}, bf16[24,16,128]{2,1,0:T(8,128)(2,1)S(1)}, u32[]{:S(2)}, u32[]{:S(2)}) collective-permute-start(bf16[24,16,128]{2,1,0:T(8,128)(2,1)S(1)} %get-tuple-element.96), channel_id=1, source_target_pairs={{0,4},{4,0},{8,12},{12,8},{16,20},{20,16},{24,28},{28,24},{1,5},{5... | collective-permute-start | bytes 294920 | tf_op jit(solution)/shard_map/ppermute | solution.py:749
  24.5 4.7 %collective-permute-start.5 = (bf16[24,16,128]{2,1,0:T(8,128)(2,1)S(1)}, bf16[24,16,128]{2,1,0:T(8,128)(2,1)S(1)}, u32[]{:S(2)}, u32[]{:S(2)}) collective-permute-start(bf16[24,16,128]{2,1,0:T(8,128)(2,1)S(1)} %get-tuple-element.94), channel_id=1, source_target_pairs={{0,4},{4,0},{8,12},{12,8},{16,20},{20,16},{24,28},{28,24},{1,5},{5... | collective-permute-start | bytes 294920 | tf_op jit(solution)/shard_map/ppermute | solution.py:749
